TPU v7x, 256 devices: a whole 4x4x8 slice. The times are simulated.
256 devices in a mesh: gx: 16 (over x, z_lo), gy: 4 (over z_hi, core), gz: 4 (over y).
Axes of the slice: x: 4, y: 4, z: 8 (z_hi: 2, z_lo: 4; z = z_hi * 4 + z_lo), core: 2. Of those that a mesh axis runs over, the one named last changes fastest.
Arguments:
- state_old: float32 [5, 256, 128, 512], P(None, 'gx', 'gy', 'gz'), as said below
- state_section: float32 [5, 256, 128, 512], P(None, 'gx', 'gy', 'gz'), as said below
- panel_record: bfloat16 [1048576, 512], P(('gx', 'gy', 'gz')), may hold values from -6 to 6
- panel_cell: int32 [8192, 128], P(('gx', 'gy', 'gz')), may hold values from 0 to 65535
- panel_angles: float32 [2, 1048576], P(None, ('gx', 'gy', 'gz')), may hold values from -3.140625 to 3.140625
- owned_blocks: int32 [256], P(('gx', 'gy', 'gz')), may hold values from 1 to 32, 2048 in all
- listener_angles: float32 [2, 1024], replicated, may hold values from -3.140625 to 3.140625
- listener_range: float32 [1024], replicated, may hold values from 1.2 to 2.5
Outputs:
- state_next: float32 [5, 256, 128, 512], P(None, 'gx', 'gy', 'gz')
- observer_spectra: float32 [2, 1024, 128], P(None, 'gz')
Inputs may be any that keep to these rules, and one draw needn't show every extreme that they name: `state_old`: density between 0.5 and 2, velocity components of magnitude 0.3 at most, stiffened-gas pressure between 0.3 and 2. `state_section`: density between 0.5 and 2, velocity components of magnitude 0.3 at most, stiffened-gas pressure between 0.3 and 2. A device's live blocks fill its first owned_blocks slots; some device owns 32 blocks, and they total 8 times the number of devices.
All inputs are finite; a program needn't handle non-finite values.
Results may differ from a plain program's by a relative error of at most 0.0003.
The roundings to bfloat16 on the way count: a program that leaves them out, or rounds other values in their place, can miss the bound.
Values may be sent and summed in bfloat16 or wider, within the bound.
A program may use at most 64 MiB of HBM per device.

v0:
```python
import math

import jax
import jax.numpy as jnp
from jax import lax
from jax.sharding import PartitionSpec as P

FREQS = 128
GROUP = 4


GAMMA_GAS = 4.4
PRESSURE_INF = 1.0
WENO_EPS = 1e-06
WAVE_STEP = 0.25
COURANT = 0.08


def with_halo(shard, sides, width):
    edges = {}
    for axis, dim in sides:
        size, length = (lax.axis_size(axis), shard.shape[dim])
        up = [(i, (i + 1) % size) for i in range(size)]
        last = lax.slice_in_dim(shard, length - width, length, axis=dim)
        initial = lax.slice_in_dim(shard, 0, width, axis=dim)
        edges[dim] = (
            lax.ppermute(last, axis, up),
            lax.ppermute(initial, axis, [(b, a) for a, b in up]),
        )
    done = []
    for _, dim in sides:
        low, high = edges[dim]
        around = [(width, width) if d in done else (0, 0) for d in range(shard.ndim)]
        shard = jnp.concatenate([jnp.pad(low, around), shard, jnp.pad(high, around)], axis=dim)
        done.append(dim)
    return shard


def in_blocks(shard, dim, size):
    dims = shard.shape
    blocks = shard.reshape(*dims[:dim], size, dims[dim] // size, *dims[dim + 1 :])
    return jnp.moveaxis(blocks, dim, 0)


def summed_on_arrival(shard, axis, dim):
    size = lax.axis_size(axis)
    blocks = lax.all_to_all(in_blocks(shard, dim, size), axis, 0, 0, tiled=True)
    return jnp.sum(blocks, axis=0)


def filled_up(lines, size):
    spare = -len(lines) % size
    return jnp.pad(lines, [(0, spare)] + [(0, 0)] * (lines.ndim - 1))


def laid_out(blocks, dim):
    dims = list(blocks.shape[1:])
    dims[dim] *= blocks.shape[0]
    return jnp.moveaxis(blocks, 0, dim).reshape(dims)


def copy_for_each(shard, axis):
    copies = jnp.broadcast_to(shard, (lax.axis_size(axis), *shard.shape))
    return lax.all_to_all(copies, axis, split_axis=0, concat_axis=0, tiled=True)


def collect(shard, axis, dim):
    return laid_out(copy_for_each(shard, axis), dim)


def sum_by_parts(shard, axes):
    lines = shard.reshape(-1, shard.shape[-1])
    own = summed_on_arrival(filled_up(lines, lax.axis_size(axes)), axes, 0)
    whole = collect(own, axes, 0)
    return whole[: len(lines)].reshape(shard.shape)


def weno_face(far_left, near_left, middle, near_right, far_right):
    cand_a = (2.0 * far_left - 7.0 * near_left + 11.0 * middle) / 6.0
    cand_b = (-near_left + 5.0 * middle + 2.0 * near_right) / 6.0
    cand_c = (2.0 * middle + 5.0 * near_right - far_right) / 6.0
    rough_a = (
        13.0 / 12.0 * (far_left - 2.0 * near_left + middle) ** 2
        + 0.25 * (far_left - 4.0 * near_left + 3.0 * middle) ** 2
    )
    rough_b = (
        13.0 / 12.0 * (near_left - 2.0 * middle + near_right) ** 2
        + 0.25 * (near_left - near_right) ** 2
    )
    rough_c = (
        13.0 / 12.0 * (middle - 2.0 * near_right + far_right) ** 2
        + 0.25 * (3.0 * middle - 4.0 * near_right + far_right) ** 2
    )
    weight_a = 0.1 / (WENO_EPS + rough_a) ** 2
    weight_b = 0.6 / (WENO_EPS + rough_b) ** 2
    weight_c = 0.3 / (WENO_EPS + rough_c) ** 2
    return (weight_a * cand_a + weight_b * cand_b + weight_c * cand_c) / (
        weight_a + weight_b + weight_c
    )


def euler_flux(state_slab, axis_d):
    density = state_slab[0]
    momenta = state_slab[1:4]
    energy = state_slab[4]
    velocity = momenta / density[None]
    kinetic = 0.5 * jnp.sum(momenta * velocity, axis=0)
    pressure = (GAMMA_GAS - 1.0) * (energy - kinetic) - GAMMA_GAS * PRESSURE_INF
    normal_speed = velocity[axis_d]
    sound_speed = jnp.sqrt(GAMMA_GAS * (pressure + PRESSURE_INF) / density)
    rows_out = [momenta[axis_d]]
    for component in range(3):
        carried = momenta[component] * normal_speed
        if component == axis_d:
            carried = carried + pressure
        rows_out.append(carried)
    rows_out.append((energy + pressure) * normal_speed)
    return (jnp.stack(rows_out), jnp.abs(normal_speed) + sound_speed)


def face_difference(padded, axis_d, count_d):
    array_axis = axis_d + 1
    picker = [slice(None), slice(3, -3), slice(3, -3), slice(3, -3)]
    picker[array_axis] = slice(None)
    state_slab = padded[tuple(picker)]
    fluxes, speeds = euler_flux(state_slab, axis_d)
    cell_count = state_slab.shape[array_axis] - 6

    def shifted(values, offset, along):
        return lax.slice_in_dim(values, offset, offset + cell_count + 1, axis=along)

    wave_speed = shifted(speeds, 0, axis_d)
    for offset in range(1, 6):
        wave_speed = jnp.maximum(wave_speed, shifted(speeds, offset, axis_d))
    split_up = [
        0.5
        * (
            shifted(fluxes, offset, array_axis)
            + wave_speed[None] * shifted(state_slab, offset, array_axis)
        )
        for offset in range(6)
    ]
    split_down = [
        0.5
        * (
            shifted(fluxes, offset, array_axis)
            - wave_speed[None] * shifted(state_slab, offset, array_axis)
        )
        for offset in range(6)
    ]
    face_flux = weno_face(
        split_up[0], split_up[1], split_up[2], split_up[3], split_up[4]
    ) + weno_face(split_down[5], split_down[4], split_down[3], split_down[2], split_down[1])
    after = lax.slice_in_dim(face_flux, 1, cell_count + 1, axis=array_axis)
    before = lax.slice_in_dim(face_flux, 0, cell_count, axis=array_axis)
    return (after - before) * float(count_d)


def section_update(padded, old_block, counts, step_size):
    change = (
        face_difference(padded, 0, counts[0])
        + face_difference(padded, 1, counts[1])
        + face_difference(padded, 2, counts[2])
    )
    return 0.75 * old_block + 0.25 * (padded[:, 3:-3, 3:-3, 3:-3] - step_size * change)


def directions(angles):
    polar_angle = 0.5 * angles[0]
    azimuth = angles[1]
    return jnp.stack(
        [
            jnp.cos(polar_angle) * jnp.cos(azimuth),
            jnp.cos(polar_angle) * jnp.sin(azimuth),
            jnp.sin(polar_angle),
        ]
    )


def panel_places(cell_rows, block_x, block_y, block_z, cells_x, cells_y, cells_z, counts):
    along_x = cell_rows // (cells_y * cells_z)
    along_y = cell_rows // cells_z % cells_y
    along_z = cell_rows % cells_z
    place_x = ((block_x * cells_x + along_x).astype(jnp.float32) + 0.5) / counts[0]
    place_y = ((block_y * cells_y + along_y).astype(jnp.float32) + 0.5) / counts[1]
    place_z = ((block_z * cells_z + along_z).astype(jnp.float32) + 0.5) / counts[2]
    return jnp.stack([place_x, place_y, place_z], axis=1)


def dft_table(sample_count, freq_count):
    times = jnp.arange(sample_count, dtype=jnp.int32)[:, None]
    orders = jnp.arange(1, freq_count + 1, dtype=jnp.int32)[None, :]
    phases = 2.0 * math.pi / sample_count * (times * orders % sample_count).astype(jnp.float32)
    scaling = 1.0 / math.sqrt(sample_count)
    return (jnp.concatenate([jnp.cos(phases), -jnp.sin(phases)], axis=1) * scaling).astype(
        jnp.bfloat16
    )


def observer_group(sources, geometry, live_flags, dft_rows, listeners, wave_numbers):
    places = geometry[:, 0:3]
    normals = geometry[:, 3:6]
    spectra = jnp.einsum(
        "gpt,tk->gpk", sources, dft_rows, preferred_element_type=jnp.float32
    ).astype(jnp.bfloat16)
    offsets = listeners[None, :, :, None] - places[:, :, None, :]
    dist_sq = jnp.sum(offsets * offsets, axis=1)
    facing = jnp.sum(normals[:, :, None, :] * offsets, axis=1)
    weights = (facing / (4.0 * math.pi * dist_sq)).astype(jnp.bfloat16)
    product = jnp.einsum("gop,gpk->gok", weights, spectra, preferred_element_type=jnp.float32)
    centres = jnp.mean(places, axis=2)
    separation = listeners[None, :, :] - centres[:, :, None]
    centre_reach = jnp.sqrt(jnp.sum(separation * separation, axis=1))
    phase_now = centre_reach[:, :, None] * wave_numbers[None, None, :]
    cosine = jnp.cos(phase_now)
    sine_part = jnp.sin(phase_now)
    freq_count = wave_numbers.shape[0]
    real_part = product[:, :, :freq_count] * cosine + product[:, :, freq_count:] * sine_part
    imag_part = product[:, :, freq_count:] * cosine - product[:, :, :freq_count] * sine_part
    masks = live_flags[:, None, None]
    return jnp.stack([jnp.sum(masks * real_part, axis=0), jnp.sum(masks * imag_part, axis=0)])


def local(
    state_old,
    state_section,
    panel_record,
    panel_cell,
    panel_angles,
    owned_blocks,
    listener_angles,
    listener_range,
):
    cells_x = state_section.shape[1]
    cells_y = state_section.shape[2]
    cells_z = state_section.shape[3]
    counts = (
        cells_x * lax.axis_size("gx"),
        cells_y * lax.axis_size("gy"),
        cells_z * lax.axis_size("gz"),
    )
    step_size = COURANT / max(counts)
    padded = with_halo(state_section, (("gx", 1), ("gy", 2), ("gz", 3)), 3)
    updated = section_update(padded, state_old, counts, step_size)
    slot_count = panel_cell.shape[0]
    block_rows = panel_cell.shape[1]
    samples = panel_record.shape[1]
    density = updated[0].reshape(cells_x * cells_y * cells_z)
    sampled = density[panel_cell]
    sources = (
        panel_record.reshape(slot_count, block_rows, samples).astype(jnp.float32)
        * sampled[:, :, None]
    ).astype(jnp.bfloat16)
    places = panel_places(
        panel_cell,
        lax.axis_index("gx"),
        lax.axis_index("gy"),
        lax.axis_index("gz"),
        cells_x,
        cells_y,
        cells_z,
        counts,
    )
    normals = jnp.transpose(directions(panel_angles.reshape(2, slot_count, block_rows)), (1, 0, 2))
    geometry = jnp.concatenate([places, normals], axis=1)
    live_count = owned_blocks[0]
    live_flags = (jnp.arange(slot_count, dtype=jnp.int32) < live_count).astype(jnp.float32)
    dft_rows = dft_table(samples, FREQS)
    listeners = 0.5 + listener_range[None, :] * directions(listener_angles)
    wave_numbers = WAVE_STEP * jnp.arange(1, FREQS + 1, dtype=jnp.int32).astype(jnp.float32)

    def add_group(group_turn, running):
        first_row = group_turn * GROUP
        group_sources = lax.dynamic_slice_in_dim(sources, first_row, GROUP, 0)
        group_geometry = lax.dynamic_slice_in_dim(geometry, first_row, GROUP, 0)
        group_flags = lax.dynamic_slice_in_dim(live_flags, first_row, GROUP, 0)
        return running + observer_group(
            group_sources, group_geometry, group_flags, dft_rows, listeners, wave_numbers
        )

    group_total = (live_count + GROUP - 1) // GROUP
    running = lax.fori_loop(
        0, group_total, add_group, jnp.zeros((2, listeners.shape[1], FREQS), jnp.float32)
    )
    gz_share = summed_on_arrival(running, "gz", 1)
    spectra_out = sum_by_parts(gz_share, ("gx", "gy"))
    return (updated, spectra_out)


def solution(mesh):
    return jax.shard_map(
        local,
        mesh=mesh,
        in_specs=(
            P(None, "gx", "gy", "gz"),
            P(None, "gx", "gy", "gz"),
            P(("gx", "gy", "gz"), None),
            P(("gx", "gy", "gz"), None),
            P(None, ("gx", "gy", "gz")),
            P(("gx", "gy", "gz")),
            P(),
            P(),
        ),
        out_specs=(P(None, "gx", "gy", "gz"), P(None, "gz", None)),
        check_vma=False,
    )
```

profile of v0, /device:TPU:1, one launch (start us, length us, event | category | flops | bytes accessed | tf_op | source)
XLA Modules:
  0.0 334.0 jit_solution(14377910725820207831)
XLA Ops:
  0.6 2.0 fusion.121
  2.6 2.5 collective-permute-start
  5.1 1.9 fusion.120
  6.9 6.9 %collective-permute-start.2 = (f32[5,16,3,128]{3,2,1,0:T(4,128)}, f32[5,16,3,128]{3,2,1,0:T(4,128)}, u32[]{:S(2)}, u32[]{:S(2)}) collective-permute-start(f32[5,16,3,128]{3,2,1,0:T(4,128)} %get-tuple-element.118), channel_id=1, source_target_pairs={{0,4},{4,8},{8,12},{12,0},{1,5},{5,9},{9,13},{13,1},{2,6},{6,10},{... | collective-permute-start | bytes 368648 | tf_op jit(solution)/shard_map/ppermute | solution.py:27
  13.8 0.4 fusion.119
  14.3 0.6 copy.50
  14.9 1.4 collective-permute-start.4
  16.2 0.6 copy.51
  16.8 1.5 collective-permute-start.5
  18.4 1.0 multiply_bitcast_fusion.1
  19.4 0.2 cosine_multiply_fusion
  19.6 1.1 fusion.95
  21.6 0.5 compare_convert_fusion
  22.1 4.6 %collective-permute-start.1 = (f32[5,3,32,128]{3,2,1,0:T(8,128)S(1)}, f32[5,3,32,128]{3,2,1,0:T(8,128)S(1)}, u32[]{:S(2)}, u32[]{:S(2)}) collective-permute-start(f32[5,3,32,128]{3,2,1,0:T(8,128)S(1)} %copy-done.4), channel_id=1, source_target_pairs={{16,0},{32,16},{48,32},{64,48},{80,64},{96,80},{112,96},{128,112},... | collective-permute-start | bytes 737288 | tf_op jit(solution)/shard_map/ppermute | solution.py:28
  26.8 1.6 copy.52
  28.4 1.5 pad.16.clone
  29.9 2.5 copy.53
  32.4 1.5 pad.17.clone
  34.0 1.1 pad.14
  35.0 1.0 pad.15
  36.1 0.4 constant_dynamic-update-slice_fusion.3
  36.7 0.4 pad_maximum_fusion.2
  37.1 0.6 constant_dynamic-update-slice_fusion.8
  37.6 3.4 %pad_maximum_fusion = f32[5,22,38,134]{3,2,1,0:T(8,128)S(1)} fusion(f32[5,22,38,3]{3,2,1,0:T(8,128)S(1)} %pad.17.clone, f32[5,22,3,128]{3,2,1,0:T(4,128)S(1)} %pad.15, f32[5,22,32,128]{3,2,1,0:T(8,128)S(1)} %get-tuple-element.125, f32[5,22,3,128]{3,2,1,0:T(4,128)S(1)} %pad.14, f32[5,22,38,3]{3,2,1,0:T(8,128)S(1)} %pad.16.clone), kind=kLoop, calls=%fused_computation.34 | loop fusion | flops 2240480 | bytes 4480960 | tf_op jit(solution)/shard_map/concatenate | solution.py:34
  41.0 2.8 maximum_maximum_fusion
  45.6 0.4 multiply_reduce_fusion.1
  46.0 0.5 fusion.66
  46.4 0.3 fusion.59
  46.8 0.3 fusion.58
  47.4 0.7 slice_maximum_fusion
  48.2 9.9 %divide_add_fusion.1 = f32[5,16,33,128]{3,2,1,0:T(8,128)S(1)} fusion(f32[5,22,3,128]{3,2,1,0:T(4,128)S(1)} %pad.15, f32[5,22,32,128]{3,2,1,0:T(8,128)S(1)} %get-tuple-element.125, f32[5,16,38,128]{3,2,1,0:T(8,128)S(1)} %multiply_dynamic-update-slice_fusion.2, f32[5,22,3,128]{3,2,1,0:T(4,128)S(1)} %pad.14, f32[16,33,128]{2,1,0:T(8,128)S(1)} %slice_maximum_fusion.5), kind=kLoop, calls=%fused_computation.75 | loop fusion | flops 51701760 | bytes 11872256 | tf_op jit(solution)/shard_map/add | solution.py:151
  58.1 7.1 %divide_add_fusion.2 = f32[5,17,32,128]{3,2,1,0:T(8,128)S(1)} fusion(f32[5,19,32,128]{3,2,1,0:T(8,128)S(1)} %get-tuple-element.124, f32[5,22,32,128]{3,2,1,0:T(8,128)S(1)} %multiply_dynamic-update-slice_fusion.1, f32[5,19,32,128]{3,2,1,0:T(8,128)S(1)} %get-tuple-element.113, f32[17,32,128]{2,1,0:T(8,128)S(1)} %slice_maximum_fusion.10), kind=kLoop, calls=%fused_computation.92 | loop fusion | flops 51179520 | bytes 18382848 | tf_op jit(solution)/shard_map/add | solution.py:151
  65.2 15.6 %divide_add_fusion = f32[5,16,32,129]{3,2,1,0:T(8,128)S(1)} fusion(f32[5,22,38,131]{3,2,1,0:T(8,128)S(1)} %get-tuple-element.110, f32[5,16,32,134]{3,2,1,0:T(8,128)S(1)} %multiply_dynamic-update-slice_fusion, f32[5,22,38,131]{3,2,1,0:T(8,128)S(1)} %get-tuple-element.109, f32[16,32,129]{2,1,0:T(8,128)S(1)} %slice_maximum_fusion), kind=kLoop, calls=%fused_computation.49 | loop fusion | flops 48545280 | bytes 17436672 | tf_op jit(solution)/shard_map/add | solution.py:151
  80.8 0.9 fusion.54
  81.7 23.0 %gather_fusion = f32[4096]{0:T(1024)S(1)} fusion(f32[65536]{0:T(1024)S(1)} %bitcast.129, s32[4096]{0:T(1024)S(1)} %fusion.111), kind=kCustom, calls=%fused_computation | custom fusion | bytes 49152 | tf_op jit(solution)/shard_map/gather | solution.py:249
  104.7 4.0 %fusion.23 = bf16[32,128,512]{2,1,0:T(8,128)(2,1)} fusion(bf16[32,128,512]{2,1,0:T(8,128)(2,1)} %bitcast.133, f32[32,128]{1,0:T(8,128)S(1)} %bitcast.139), kind=kLoop, calls=%fused_computation.33 | loop fusion | flops 6291456 | bytes 8404992 | tf_op jit(solution)/shard_map/convert_element_type | solution.py:253
  108.8 21.2 %while.11 = (s32[]{:T(128)}, f32[2,1024,128]{2,1,0:T(8,128)S(1)}, s32[]{:T(128)}, f32[32]{0:T(128)}, f32[32,6,128]{2,1,0:T(8,128)S(1)}, /*index=5*/f32[3,1024]{1...) while((s32[]{:T(128)}, f32[2,1024,128]{2,1,0:T(8,128)S(1)}, ...), condition=%wide.region_10.11_spmd.clone, body=%wide.region_3.10_spmd.clone.sunk | while | flops 417236864 | bytes 21886488 | solution.py:282
  108.8 0.7 fusion.130
  109.5 2.9 fusion.131
  112.4 4.8 %fusion.132 = f32[4,1024,256]{2,1,0:T(8,128)} fusion(f32[4,1024,128]{2,1,0:T(8,128)} %get-tuple-element.196, f32[4,1024,128]{2,1,0:T(8,128)S(1)} %get-tuple-element.197, bf16[32,128,512]{2,1,0:T(8,128)(2,1)} %get-tuple-element.233, s32[]{:T(128)S(6)} %select_n.94, bf16[512,256]{1,0:T(8,128)(2,1)S(1)} %get-tuple-element.234), kind=kOutput, calls=%fused_computation.20.clone.1 | convolution fusion | flops 404357120 | bytes 9175044 | tf_op jit(solution)/shard_map/while/body/gop,gpk->gok/dot_general | solution.py:210
  117.2 0.7 broadcast_multiply_fusion.2
  118.1 0.7 dynamic_slice.18
  118.8 11.0 %fusion.133 = (f32[1024,128]{1,0:T(8,128)S(1)}, f32[1024,128]{1,0:T(8,128)S(1)}) fusion(f32[4,1024,256]{2,1,0:T(8,128)} %fusion.132, f32[128]{0:T(128)S(1)} %convert_multiply_fusion.3, f32[4,1024]{1,0:T(4,128)S(1)} %sqrt.30, f32[4]{0:T(128)S(1)} %dynamic_slice.18), kind=kLoop, calls=%fused_computation.14.clone.1 | loop fusion | flops 5505024 | bytes 5259792 | tf_op jit(solution)/shard_map/while/body/reduce_sum | solution.py:221
  129.8 0.2 maximum_add_fusion.2
  130.1 162.3 %all_to_all.15 = f32[4,2,256,128]{3,2,1,0:T(8,128)S(1)} all-to-all(f32[4,2,256,128]{3,2,1,0:T(8,128)S(1)} %copy.49), channel_id=1, replica_groups=mesh['gx'=16,'gy'=4,'gz'=4] {'gz'}, dimensions={0} | all-to-all | bytes 2097152 | tf_op jit(solution)/shard_map/all_to_all | solution.py:47
  292.5 22.9 %all_to_all.16 = f32[64,8,128]{2,1,0:T(8,128)S(1)} all-to-all(f32[64,8,128]{2,1,0:T(8,128)S(1)} %bitcast.134), channel_id=1, replica_groups=mesh['gx'=16,'gy'=4,'gz'=4] {'gx','gy'}, dimensions={0} | all-to-all | bytes 524288 | tf_op jit(solution)/shard_map/all_to_all | solution.py:47
  315.5 17.8 %all_to_all.17 = f32[64,8,128]{2,1,0:T(8,128)S(1)} all-to-all(f32[64,8,128]{2,1,0:T(8,128)S(1)} %broadcast_in_dim.8), channel_id=1, replica_groups=mesh['gx'=16,'gy'=4,'gz'=4] {'gx','gy'}, dimensions={0} | all-to-all | bytes 524288 | tf_op jit(solution)/shard_map/all_to_all | solution.py:64
  333.3 0.7 copy.80
  (62 shorter events, 3.1 us)
Async XLA Ops:
  0.6 13.2 %copy-start = (f32[5,16,32,128]{3,2,1,0:T(8,128)S(1)}, f32[5,16,32,128]{3,2,1,0:T(8,128)}, u32[]{:S(2)}) copy-start(f32[5,16,32,128]{3,2,1,0:T(8,128)} %param.11) | copy-start | bytes 3932164
  2.6 33.4 %collective-permute-start = (f32[5,3,32,128]{3,2,1,0:T(8,128)}, f32[5,3,32,128]{3,2,1,0:T(8,128)S(1)}, u32[]{:S(2)}, u32[]{:S(2)}) collective-permute-start(f32[5,3,32,128]{3,2,1,0:T(8,128)} %get-tuple-element.121), channel_id=1, source_target_pairs={{0,16},{16,32},{32,48},{48,64},{64,80},{80,96},{96,112},{112,128},... | collective-permute-start | bytes 737288 | tf_op jit(solution)/shard_map/ppermute | solution.py:27
  6.9 27.0 %collective-permute-start.2 = (f32[5,16,3,128]{3,2,1,0:T(4,128)}, f32[5,16,3,128]{3,2,1,0:T(4,128)}, u32[]{:S(2)}, u32[]{:S(2)}) collective-permute-start(f32[5,16,3,128]{3,2,1,0:T(4,128)} %get-tuple-element.118), channel_id=1, source_target_pairs={{0,4},{4,8},{8,12},{12,0},{1,5},{5,9},{9,13},{13,1},{2,6},{6,10},{... | collective-permute-start | bytes 368648 | tf_op jit(solution)/shard_map/ppermute | solution.py:27
  13.8 21.2 %collective-permute-start.3 = (f32[5,16,3,128]{3,2,1,0:T(4,128)}, f32[5,16,3,128]{3,2,1,0:T(4,128)}, u32[]{:S(2)}, u32[]{:S(2)}) collective-permute-start(f32[5,16,3,128]{3,2,1,0:T(4,128)} %get-tuple-element.119), channel_id=1, source_target_pairs={{4,0},{8,4},{12,8},{0,12},{5,1},{9,5},{13,9},{1,13},{6,2},{10,6},{... | collective-permute-start | bytes 368648 | tf_op jit(solution)/shard_map/ppermute | solution.py:28
  14.2 4.1 %copy-start.5 = (s32[32,128]{1,0:T(8,128)S(1)}, s32[32,128]{1,0:T(8,128)}, u32[]{:S(2)}) copy-start(s32[32,128]{1,0:T(8,128)} %param.13) | copy-start | bytes 49156
  14.3 4.1 %copy-start.6 = (f32[2,4096]{1,0:T(2,128)S(1)}, f32[2,4096]{1,0:T(2,128)}, u32[]{:S(2)}) copy-start(f32[2,4096]{1,0:T(2,128)} %param.14) | copy-start | bytes 98308
  14.3 5.1 %copy-start.7 = (f32[2,1024]{1,0:T(2,128)S(1)}, f32[2,1024]{1,0:T(2,128)}, u32[]{:S(2)}) copy-start(f32[2,1024]{1,0:T(2,128)} %param.16) | copy-start | bytes 24580
  14.9 5.9 %copy-start.8 = (f32[1024]{0:T(1024)S(1)}, f32[1024]{0:T(1024)}, u32[]{:S(2)}) copy-start(f32[1024]{0:T(1024)} %param.17) | copy-start | bytes 12292
  14.9 7.3 %collective-permute-start.4 = (f32[5,16,32,3]{2,1,3,0:T(8,128)S(1)}, f32[5,16,32,3]{2,1,3,0:T(8,128)S(1)}, u32[]{:S(2)}, u32[]{:S(2)}) collective-permute-start(f32[5,16,32,3]{2,1,3,0:T(8,128)S(1)} %copy.50), channel_id=1, source_target_pairs={{0,1},{1,2},{2,3},{3,0},{4,5},{5,6},{6,7},{7,4},{8,9},{9,10},{10,1... | collective-permute-start | bytes 92168 | tf_op jit(solution)/shard_map/ppermute | solution.py:27
  16.2 5.9 %copy-start.4 = (f32[5,3,32,128]{3,2,1,0:T(8,128)S(1)}, f32[5,3,32,128]{3,2,1,0:T(8,128)}, u32[]{:S(2)}) copy-start(f32[5,3,32,128]{3,2,1,0:T(8,128)} %get-tuple-element.120) | copy-start | bytes 737284
  16.8 13.1 %collective-permute-start.5 = (f32[5,16,32,3]{2,1,3,0:T(8,128)S(1)}, f32[5,16,32,3]{2,1,3,0:T(8,128)}, u32[]{:S(2)}, u32[]{:S(2)}) collective-permute-start(f32[5,16,32,3]{2,1,3,0:T(8,128)S(1)} %copy.51), channel_id=1, source_target_pairs={{1,0},{2,1},{3,2},{0,3},{5,4},{6,5},{7,6},{4,7},{9,8},{10,9},{11,1... | collective-permute-start | bytes 92168 | tf_op jit(solution)/shard_map/ppermute | solution.py:28
  22.1 14.3 %collective-permute-start.1 = (f32[5,3,32,128]{3,2,1,0:T(8,128)S(1)}, f32[5,3,32,128]{3,2,1,0:T(8,128)S(1)}, u32[]{:S(2)}, u32[]{:S(2)}) collective-permute-start(f32[5,3,32,128]{3,2,1,0:T(8,128)S(1)} %copy-done.4), channel_id=1, source_target_pairs={{16,0},{32,16},{48,32},{64,48},{80,64},{96,80},{112,96},{128,112},... | collective-permute-start | bytes 737288 | tf_op jit(solution)/shard_map/ppermute | solution.py:28
  33.9 2.1 copy-start.1
  65.2 15.6 %copy-start.3 = (f32[5,16,32,128]{3,2,1,0:T(8,128)S(1)}, f32[5,16,32,128]{3,2,1,0:T(8,128)}, u32[]{:S(2)}) copy-start(f32[5,16,32,128]{3,2,1,0:T(8,128)} %param.10) | copy-start | bytes 3932164
  81.6 23.1 %copy-start.2 = (f32[5,16,32,128]{3,2,1,0:T(8,128)}, f32[5,16,32,128]{3,2,1,0:T(8,128)S(1)}, u32[]{:S(2)}) copy-start(f32[5,16,32,128]{3,2,1,0:T(8,128)S(1)} %fusion.54) | copy-start | bytes 3932164
where the time goes:
time: 334 us
  blocking collectives  203 us (61%)
  other arithmetic  67.7 us (20%)
  local copies, waits for them, and re-layouts  39.9 us (12%)
  starting transfers between devices  16.8 us (5%)
  matrix products  4.77 us (1%)
    all_to_all x2, blocking collectives, summed_on_arrival(): blocks = lax.all_to_all(in_blocks(shard, dim, size), axis, 0, 0, tiled=True)  185 us
    add x3, other arithmetic, face_difference(): weno_face(split_up[0], split_up[1], split_up[2], split_up[3], split_up[4])  32.5 us
    gather x1, local copies, waits for them, and re-layouts, local(): sampled = density[panel_cell]  23 us
    all_to_all x1, blocking collectives, copy_for_each(): return lax.all_to_all(copies, axis, split_axis=0, concat_axis=0, tiled=True)  17.8 us
    reduce_sum x1, other arithmetic, observer_group(): jnp.sum(masks * real_part, axis=0)  11 us
    ppermute x3, starting transfers between devices, with_halo(): lax.ppermute(last, axis, up)  10.7 us
  transfers between devices with their start and end apart: 6, of which 0 were waited for; matrix products, arithmetic and copies ran while one was open for 5% of the time, Pallas kernels for 0%

commit v1 on v0

v1 whole, which is shorter than its diff:
```python
import functools
import math

import jax
import jax.numpy as jnp
from jax import lax
from jax.experimental import pallas as pl
from jax.experimental.pallas import tpu as pltpu
from jax.sharding import PartitionSpec as P

FREQS = 128
GAMMA_GAS = 4.4
PRESSURE_INF = 1.0
WENO_EPS = 1e-06
WAVE_STEP = 0.25
COURANT = 0.08

SCALE = 4.0
EPS = 4.0 * SCALE * SCALE * WENO_EPS


def summed_on_arrival(blocks, axis):
    return jnp.sum(lax.all_to_all(blocks, axis, 0, 0, tiled=True), axis=0)


def collect(shard, axis):
    copies = jnp.broadcast_to(shard, (lax.axis_size(axis), *shard.shape))
    return lax.all_to_all(copies, axis, split_axis=0, concat_axis=0, tiled=True)


def sum_by_parts(shard, axes):
    size = lax.axis_size(axes)
    lines = shard.reshape(size, -1, shard.shape[-1])
    own = summed_on_arrival(lines, axes)
    return collect(own, axes).reshape(shard.shape)


def edge_swap(low_edge, high_edge, axis):
    size = lax.axis_size(axis)
    up = [(i, (i + 1) % size) for i in range(size)]
    down = [(b, a) for a, b in up]
    return lax.ppermute(high_edge, axis, up), lax.ppermute(low_edge, axis, down)


def flux_of(state, axis_d):
    density, energy = state[0], state[4]
    momenta = state[1:4]
    inverse = 1.0 / density
    velocity = [m * inverse for m in momenta]
    kinetic = 0.5 * (momenta[0] * velocity[0] + momenta[1] * velocity[1] + momenta[2] * velocity[2])
    pressure = (GAMMA_GAS - 1.0) * (energy - kinetic) - GAMMA_GAS * PRESSURE_INF * SCALE
    normal = velocity[axis_d]
    sound = jnp.sqrt(GAMMA_GAS * (pressure + PRESSURE_INF * SCALE) * inverse)
    rows = [momenta[axis_d]]
    for component in range(3):
        carried = momenta[component] * normal
        rows.append(carried + pressure if component == axis_d else carried)
    rows.append((energy + pressure) * normal)
    return rows, jnp.abs(normal) + sound


def weno_terms(e0, e1, e2, d1, d2):
    base1 = d1 * d1 + EPS
    base2 = d2 * d2 + EPS
    t0 = e0 * ((4.0 / 3.0) * e0 + d1) + base1
    t1 = e1 * ((4.0 / 3.0) * e1 + d1) + base1
    t2 = e2 * ((4.0 / 3.0) * e2 - d2) + base2
    p01, p02, p12 = t0 * t1, t0 * t2, t1 * t2
    wa = p12 * p12
    wb = 6.0 * (p02 * p02)
    wc = 1.5 * (p01 * p01)
    return wa * (e0 - e1) + wc * (e1 - e2), (wa + wb) + (wc + wc)


def face_value(alpha, df, dq, fsum):
    aq = [alpha * v for v in dq]
    up = [df[j] + aq[j] for j in range(4)]
    dn = [None] + [df[j] - aq[j] for j in range(1, 5)]
    num_p, den_p = weno_terms(up[1] - up[0], up[2] - up[1], up[3] - up[2], up[1], up[2])
    num_m, den_m = weno_terms(dn[4] - dn[3], dn[3] - dn[2], dn[2] - dn[1], -dn[3], -dn[2])
    ratio = (num_p * den_m + num_m * den_p) / (den_p * den_m)
    return fsum + ((0.5 * (up[1] - dn[3]) - aq[2]) + ratio) * (1.0 / 3.0)


def sweep(planes, dq, df, fs, m2, faces, axis_d, cells, chunks):
    for r in range(chunks):
        rows = pl.ds(8 * r, 8)

        def load(j):
            return [planes[c, j, rows, :] for c in range(5)]

        def step(j, carry):
            state, flux, speed = carry
            next_state = load(j + 1)
            next_flux, next_speed = flux_of(next_state, axis_d)
            for c in range(5):
                dq[c, j, rows, :] = next_state[c] - state[c]
                df[c, j, rows, :] = next_flux[c] - flux[c]
                fs[c, j, rows, :] = next_flux[c] + flux[c]
            m2[j, rows, :] = jnp.maximum(next_speed, speed)
            return next_state, next_flux, next_speed

        first = load(0)
        first_flux, first_speed = flux_of(first, axis_d)
        lax.fori_loop(0, cells + 5, step, (first, first_flux, first_speed))

    def face(i, carry):
        for r in range(chunks):
            rows = pl.ds(8 * r, 8)
            alpha = jnp.maximum(jnp.maximum(m2[i, rows, :], m2[i + 2, rows, :]), m2[i + 4, rows, :])
            for c in range(5):
                faces[c, i, rows, :] = face_value(
                    alpha,
                    [df[c, i + j, rows, :] for j in range(5)],
                    [dq[c, i + j, rows, :] for j in range(5)],
                    fs[c, i + 2, rows, :],
                )
        return carry

    lax.fori_loop(0, cells + 1, face, 0)


def z_kernel(coef, q, lo, hi, out, turned, planes, dq, df, fs, m2, faces, diff):
    for c in range(5):
        for blk in range(4):
            tile = jnp.transpose(q[c, pl.ds(128 * blk, 128), :]) * SCALE
            base = 160 * blk
            turned[c, pl.ds(base, 8), :] = lo[c, blk] * SCALE
            turned[c, pl.ds(base + 8, 72), :] = tile[:72]
            turned[c, pl.ds(base + 80, 72), :] = tile[56:]
            turned[c, pl.ds(base + 152, 8), :] = hi[c, blk] * SCALE

    def gather(j, carry):
        for c in range(5):
            planes[c, j] = turned[c, pl.ds(j + 5, 8, stride=80), :]
        return carry

    lax.fori_loop(0, 70, gather, 0)
    sweep(planes, dq, df, fs, m2, faces, 2, 64, 1)

    def difference(i, carry):
        for c in range(5):
            diff[c, pl.ds(pl.multiple_of(8 * i, 8), 8), :] = coef * (faces[c, i + 1] - faces[c, i])
        return carry

    lax.fori_loop(0, 64, difference, 0)
    for c in range(5):
        for blk in range(4):
            tile = jnp.concatenate(
                [diff[c, pl.ds(2 * blk + half, 64, stride=8), :] for half in range(2)], axis=0
            )
            out[c, pl.ds(128 * blk, 128), :] = jnp.transpose(tile)


def y_kernel(coef, q, lo, hi, add, out, planes, dq, df, fs, m2, faces, diff):
    for c in range(5):
        for h in range(2):
            rows = pl.ds(8 * h, 8)
            for k in range(3):
                planes[c, k, rows, :] = lo[c, pl.ds(24 * h + k, 8, stride=3), :] * SCALE
                planes[c, 35 + k, rows, :] = hi[c, pl.ds(24 * h + k, 8, stride=3), :] * SCALE

    def gather(j, carry):
        for c in range(5):
            for h in range(2):
                planes[c, j + 3, pl.ds(8 * h, 8), :] = (
                    q[c, pl.ds(j + 256 * h, 8, stride=32), :] * SCALE
                )
        return carry

    lax.fori_loop(0, 32, gather, 0)
    sweep(planes, dq, df, fs, m2, faces, 1, 32, 2)

    def difference(i, carry):
        for c in range(5):
            diff[c, pl.ds(pl.multiple_of(16 * i, 16), 16), :] = coef * (
                faces[c, i + 1] - faces[c, i]
            )
        return carry

    lax.fori_loop(0, 32, difference, 0)

    def back(x, carry):
        for c in range(5):
            for y8 in range(4):
                rows = pl.ds(pl.multiple_of(32 * x + 8 * y8, 8), 8)
                out[c, rows, :] = add[c, rows, :] + diff[c, pl.ds(128 * y8 + x, 8, stride=16), :]
        return carry

    lax.fori_loop(0, 16, back, 0)


def x_kernel(coef, q, lo, hi, add, old, out, planes, dq, df, fs, m2, faces):
    for c in range(5):
        for k in range(3):
            planes[c, k] = lo[c, k] * SCALE
            planes[c, 19 + k] = hi[c, k] * SCALE

    def gather(j, carry):
        for c in range(5):
            planes[c, j + 3] = q[c, j] * SCALE
        return carry

    lax.fori_loop(0, 16, gather, 0)
    sweep(planes, dq, df, fs, m2, faces, 0, 16, 4)

    def finish(i, carry):
        for c in range(5):
            change = add[c, i] + coef * (faces[c, i + 1] - faces[c, i])
            out[c, i] = 0.75 * old[c, i] + 0.25 * q[c, i] - change
        return carry

    lax.fori_loop(0, 16, finish, 0)


def sweep_scratch(cells, rows):
    f32 = jnp.float32
    return [
        pltpu.VMEM((5, cells + 6, rows, 128), f32),
        pltpu.VMEM((5, cells + 5, rows, 128), f32),
        pltpu.VMEM((5, cells + 5, rows, 128), f32),
        pltpu.VMEM((5, cells + 5, rows, 128), f32),
        pltpu.VMEM((cells + 5, rows, 128), f32),
        pltpu.VMEM((5, cells + 1, rows, 128), f32),
    ]


FLOW_PARAMS = dict(
    compiler_params=pltpu.CompilerParams(vmem_limit_bytes=56 * 2**20),
    cost_estimate=pl.CostEstimate(flops=30_000_000, bytes_accessed=4_000_000, transcendentals=0),
)


def flow_update(state_old, state_section, counts, step_size):
    f32 = jnp.float32
    rows = state_section.reshape(5, 512, 128)
    strips = jnp.concatenate([state_section[..., :8], state_section[..., 120:]], axis=-1)
    strips = jnp.transpose(strips.reshape(5, 4, 128, 16), (0, 1, 3, 2))
    z_lo, z_hi = edge_swap(strips[:, :, :8], strips[:, :, 8:], "gz")
    y_lo, y_hi = edge_swap(
        state_section[:, :, :3].reshape(5, 48, 128), state_section[:, :, 29:].reshape(5, 48, 128), "gy"
    )
    x_lo, x_hi = edge_swap(state_section[:, :3], state_section[:, 13:], "gx")
    coefs = [0.25 * step_size * n / (2.0 * SCALE) for n in counts]
    part = pl.pallas_call(
        functools.partial(z_kernel, coefs[2]),
        out_shape=jax.ShapeDtypeStruct((5, 512, 128), f32),
        scratch_shapes=[pltpu.VMEM((5, 640, 128), f32)]
        + sweep_scratch(64, 8)
        + [pltpu.VMEM((5, 512, 128), f32)],
        name="flow_z",
        **FLOW_PARAMS,
    )(rows, z_lo, z_hi)
    part = pl.pallas_call(
        functools.partial(y_kernel, coefs[1]),
        out_shape=jax.ShapeDtypeStruct((5, 512, 128), f32),
        scratch_shapes=sweep_scratch(32, 16) + [pltpu.VMEM((5, 512, 128), f32)],
        name="flow_y",
        **FLOW_PARAMS,
    )(rows, y_lo, y_hi, part)
    return pl.pallas_call(
        functools.partial(x_kernel, coefs[0]),
        out_shape=jax.ShapeDtypeStruct((5, 16, 32, 128), f32),
        scratch_shapes=sweep_scratch(16, 32),
        name="flow_x",
        **FLOW_PARAMS,
    )(state_section, x_lo, x_hi, part.reshape(5, 16, 32, 128), state_old)


def directions(angles):
    polar_angle = 0.5 * angles[0]
    azimuth = angles[1]
    return jnp.stack(
        [
            jnp.cos(polar_angle) * jnp.cos(azimuth),
            jnp.cos(polar_angle) * jnp.sin(azimuth),
            jnp.sin(polar_angle),
        ]
    )


def panel_places(cell_rows, blocks, cells, counts):
    along = (
        cell_rows // (cells[1] * cells[2]),
        cell_rows // cells[2] % cells[1],
        cell_rows % cells[2],
    )
    return [
        ((blocks[d] * cells[d] + along[d]).astype(jnp.float32) + 0.5) / counts[d] for d in range(3)
    ]


def dft_table(sample_count, freq_count):
    times = jnp.arange(sample_count, dtype=jnp.int32)[None, :]
    orders = jnp.arange(1, freq_count + 1, dtype=jnp.int32)[:, None]
    phases = 2.0 * math.pi / sample_count * (times * orders % sample_count).astype(jnp.float32)
    scaling = 1.0 / math.sqrt(sample_count)
    return (jnp.concatenate([jnp.cos(phases), -jnp.sin(phases)], axis=0) * scaling).astype(
        jnp.bfloat16
    )


def sin_cos(turns):
    rest = turns - jnp.round(turns)
    half = rest * rest
    s = (3.1996934769709044, -14.868610848632139, 42.01616577638672, -76.70155116950977,
         81.60502462208919, -41.341697068940945, 6.283185307179586)
    c = (6.529609897637814, -25.96831291454545, 60.167831622681774, -85.45016553628534,
         64.93911898307624, -19.73920453207708, 1.0)
    sine = jnp.full_like(half, s[0])
    for k in s[1:]:
        sine = sine * half + k
    cosine = jnp.full_like(half, c[0])
    for k in c[1:]:
        cosine = cosine * half + k
    return sine * rest, cosine


OBS_CHUNK = 256


def panel_kernel(live, density, record, cells, geo, turns, listeners, table, out, pieces):
    b = pl.program_id(0)

    @pl.when(b == 0)
    def _():
        out[...] = jnp.zeros_like(out)
        turned = jnp.concatenate(
            [jnp.transpose(density[pl.ds(128 * k, 128), :]) for k in range(4)], axis=1
        )
        high = turned.astype(jnp.bfloat16)
        rest = turned - high.astype(jnp.float32)
        middle = rest.astype(jnp.bfloat16)
        pieces[pl.ds(0, 128), :] = high
        pieces[pl.ds(128, 128), :] = middle
        pieces[pl.ds(256, 128), :] = (rest - middle.astype(jnp.float32)).astype(jnp.bfloat16)

    @pl.when(b < live[0])
    def _():
        cell = cells[0]
        grid_row = lax.broadcasted_iota(jnp.int32, (512, 128), 0)
        chosen = jnp.where(grid_row == cell // 128, 1.0, 0.0).astype(jnp.bfloat16)
        found = jnp.dot(pieces[...], chosen, preferred_element_type=jnp.float32)
        found = (found[:128] + found[128:256]) + found[256:]
        lane = lax.broadcasted_iota(jnp.int32, (128, 128), 0)
        sampled = jnp.sum(jnp.where(lane == cell % 128, found, 0.0), axis=0, keepdims=True)
        place = lax.broadcasted_iota(jnp.int32, (8, 128), 0)
        columns = jnp.transpose(jnp.where(place == 6, sampled, geo[0]))
        sources = (record[...].astype(jnp.float32) * columns[:, 6:7]).astype(jnp.bfloat16)
        spectra = lax.dot_general(
            table[...], sources, (((1,), (1,)), ((), ())), preferred_element_type=jnp.float32
        ).astype(jnp.bfloat16)
        order = (lax.broadcasted_iota(jnp.int32, (8, 128), 0) + 1).astype(jnp.float32)
        for o in range(1024 // OBS_CHUNK):
            span = pl.ds(OBS_CHUNK * o, OBS_CHUNK)
            offs = [listeners[pl.ds(d, 1), span] - columns[:, d : d + 1] for d in range(3)]
            reach = (offs[0] * offs[0] + offs[1] * offs[1]) + offs[2] * offs[2]
            facing = (offs[0] * columns[:, 3:4] + offs[1] * columns[:, 4:5]) + offs[2] * columns[:, 5:6]
            weights = (facing / reach).astype(jnp.bfloat16)
            product = jnp.dot(spectra, weights, preferred_element_type=jnp.float32)
            for h in range(OBS_CHUNK // 128):
                lanes = slice(128 * h, 128 * h + 128)
                base = turns[0, :, pl.ds(OBS_CHUNK * o + 128 * h, 128)]
                sine, cosine = sin_cos(base * order)
                step_s = jnp.broadcast_to(sine[7:8], (8, 128))
                step_c = jnp.broadcast_to(cosine[7:8], (8, 128))
                for a in range(FREQS // 8):
                    re = product[8 * a : 8 * a + 8, lanes]
                    im = product[FREQS + 8 * a : FREQS + 8 * a + 8, lanes]
                    out[o, 0, pl.ds(8 * a, 8), lanes] += re * cosine + im * sine
                    out[o, 1, pl.ds(8 * a, 8), lanes] += im * cosine - re * sine
                    if a + 1 < FREQS // 8:
                        sine, cosine = (
                            sine * step_c + cosine * step_s,
                            cosine * step_c - sine * step_s,
                        )


def panel_sums(live_count, density, record, cells, geo, turns, listeners, table):
    def at(b, live):
        return jnp.minimum(b, live[0] - 1)

    return pl.pallas_call(
        panel_kernel,
        out_shape=jax.ShapeDtypeStruct((1024 // OBS_CHUNK, 2, FREQS, OBS_CHUNK), jnp.float32),
        grid_spec=pltpu.PrefetchScalarGridSpec(
            num_scalar_prefetch=1,
            grid=(32,),
            in_specs=[
                pl.BlockSpec((512, 128), lambda b, live: (0, 0)),
                pl.BlockSpec((128, 512), lambda b, live: (at(b, live), 0)),
                pl.BlockSpec((1, 1, 128), lambda b, live: (at(b, live), 0, 0)),
                pl.BlockSpec((1, 8, 128), lambda b, live: (at(b, live), 0, 0)),
                pl.BlockSpec((1, 1, 1024), lambda b, live: (at(b, live), 0, 0)),
                pl.BlockSpec((8, 1024), lambda b, live: (0, 0)),
                pl.BlockSpec((256, 512), lambda b, live: (0, 0)),
            ],
            out_specs=pl.BlockSpec(
                (1024 // OBS_CHUNK, 2, FREQS, OBS_CHUNK), lambda b, live: (0, 0, 0, 0)
            ),
            scratch_shapes=[pltpu.VMEM((384, 512), jnp.bfloat16)],
        ),
        compiler_params=pltpu.CompilerParams(
            dimension_semantics=("arbitrary",), vmem_limit_bytes=48 * 2**20
        ),
        cost_estimate=pl.CostEstimate(
            flops=4_000_000_000, bytes_accessed=8_000_000, transcendentals=0
        ),
        name="panels",
    )(live_count, density, record, cells, geo, turns, listeners, table)


def panel_geometry(panel_cell, panel_angles, listener_angles, listener_range, blocks, cells, counts):
    slot_count, block_rows = panel_cell.shape
    places = panel_places(panel_cell, blocks, cells, counts)
    normals = directions(panel_angles.reshape(2, slot_count, block_rows)) * (0.25 / math.pi)
    blank = jnp.zeros_like(places[0])
    geo = jnp.stack([*places, normals[0], normals[1], normals[2], blank, blank], axis=1)
    listeners = 0.5 + listener_range[None, :] * directions(listener_angles)
    centres = [jnp.mean(p, axis=1, keepdims=True) for p in places]
    apart = sum((listeners[d][None, :] - centres[d]) ** 2 for d in range(3))
    turns = jnp.sqrt(apart) * (WAVE_STEP / (2.0 * math.pi))
    listeners = jnp.concatenate([listeners, jnp.zeros((5, listeners.shape[1]), jnp.float32)], axis=0)
    return geo, turns.reshape(slot_count, 1, -1), listeners


def local(
    state_old,
    state_section,
    panel_record,
    panel_cell,
    panel_angles,
    owned_blocks,
    listener_angles,
    listener_range,
):
    cells = state_section.shape[1:]
    axes = ("gx", "gy", "gz")
    counts = tuple(n * lax.axis_size(a) for n, a in zip(cells, axes))
    step_size = COURANT / max(counts)
    geo, turns, listeners = panel_geometry(
        panel_cell,
        panel_angles,
        listener_angles,
        listener_range,
        [lax.axis_index(a) for a in axes],
        cells,
        counts,
    )
    updated = flow_update(state_old, state_section, counts, step_size)
    partial = panel_sums(
        owned_blocks,
        updated[0].reshape(512, 128),
        panel_record,
        panel_cell.reshape(32, 1, 128),
        geo,
        turns,
        listeners,
        dft_table(panel_record.shape[1], FREQS),
    )
    gz_share = summed_on_arrival(partial, "gz")
    spectra_out = sum_by_parts(gz_share.reshape(2 * FREQS, OBS_CHUNK), ("gx", "gy"))
    return updated, jnp.transpose(spectra_out.reshape(2, FREQS, OBS_CHUNK), (0, 2, 1))


def solution(mesh):
    return jax.shard_map(
        local,
        mesh=mesh,
        in_specs=(
            P(None, "gx", "gy", "gz"),
            P(None, "gx", "gy", "gz"),
            P(("gx", "gy", "gz"), None),
            P(("gx", "gy", "gz"), None),
            P(None, ("gx", "gy", "gz")),
            P(("gx", "gy", "gz")),
            P(),
            P(),
        ),
        out_specs=(P(None, "gx", "gy", "gz"), P(None, "gz", None)),
        check_vma=False,
    )
```

time: 334 us -> 163 us (0.49)
  blocking collectives: 203 us -> 85.7 us
  other arithmetic: 67.7 us -> 3.78 us
  Pallas kernels: 0 us -> 45.6 us
  local copies, waits for them, and re-layouts: 39.9 us -> 7.71 us
  matrix products: 4.77 us -> 0 us
    all_to_all x3, blocking collectives: 203 us -> 85.7 us  [the longest x2 67.9 us: summed_on_arrival(): return jnp.sum(lax.all_to_all(blocks, axis, 0, 0, tiled=True), axis=0)]
    pallas_call x0 -> x4, Pallas kernels: none -> 45.6 us  [the longest x1 12.7 us: flow_update(): pl.pallas_call(functools.partial(y_kernel, coefs[1]), out_shape=jax.Shape...]
    add x10 -> x2, other arithmetic: 34.6 us -> 0.02 us  [the longest x1 0.02 us: panel_geometry(): listeners = 0.5 + listener_range[None, :] * directions(listener_angles)]
    gather x1 -> x0, local copies, waits for them, and re-layouts: 23 us -> none  [local(): sampled = density[panel_cell]]
    reduce_sum x9 -> x3, other arithmetic: 15.6 us -> 0.33 us  [the longest x2 0.17 us: summed_on_arrival(): return jnp.sum(lax.all_to_all(blocks, axis, 0, 0, tiled=True), axis=0)]
    concatenate x4 -> x1, other arithmetic: 6.6 us -> 0.41 us  [flow_update(): jnp.concatenate([state_section[..., :8], state_section[..., 120:]], axis=-1)]
    pad x4 -> x0, local copies, waits for them, and re-layouts: 5.06 us -> none  [the longest x2 2.58 us: with_halo(): jnp.pad(low, around)]
    dot_general x1 -> x0, matrix products: 4.77 us -> none  [observer_group(): jnp.einsum('gop,gpk->gok', weights, spectra, preferred_element_type=jnp.f...]
  transfers between devices with their start and end apart: 6 -> 6, of which waited for: 0 -> 1; matrix products, arithmetic and copies ran while one was open for 5% -> 2% of each run, Pallas kernels for 0% -> 15%
where the time goes in v1:
time: 163 us; the launch traced here: 164 us
  blocking collectives  85.7 us (53%)
  Pallas kernels  45.6 us (28%)
  starting transfers between devices  17.6 us (11%)
  local copies, waits for them, and re-layouts  7.71 us (5%)
  other arithmetic  3.78 us (2%)
    all_to_all x2, blocking collectives, summed_on_arrival(): return jnp.sum(lax.all_to_all(blocks, axis, 0, 0, tiled=True), axis=0)  67.9 us
    all_to_all x1, blocking collectives, collect(): return lax.all_to_all(copies, axis, split_axis=0, concat_axis=0, tiled=True)  17.8 us
    pallas_call x1, Pallas kernels, flow_update(): pl.pallas_call(functools.partial(y_kernel, coefs[1]), out_shape=jax.Shape...  12.7 us
    pallas_call x1, Pallas kernels, flow_update(): pl.pallas_call(functools.partial(z_kernel, coefs[2]), out_shape=jax.Shape...  12.2 us
    pallas_call x1, Pallas kernels, flow_update(): pl.pallas_call(functools.partial(x_kernel, coefs[0]), out_shape=jax.Shape...  11.2 us
    ppermute x3, starting transfers between devices, edge_swap(): lax.ppermute(high_edge, axis, up)  10.8 us
    pallas_call x1, Pallas kernels, panel_sums(): pl.pallas_call(panel_kernel, out_shape=jax.ShapeDtypeStruct((1024 // OBS_...  9.51 us
    ppermute x3, starting transfers between devices, edge_swap(): lax.ppermute(low_edge, axis, down)  6.77 us
  transfers between devices with their start and end apart: 6, of which 1 were waited for; matrix products, arithmetic and copies ran while one was open for 2% of the time, Pallas kernels for 15%

profile of v1, /device:TPU:1, one launch (start us, length us, event | category | flops | bytes accessed | tf_op | source)
XLA Modules:
  0.0 163.5 jit_solution(10593757255277412943)
XLA Ops:
  0.6 2.2 %fusion.35 = (f32[5,16,32,8]{3,2,1,0:T(8,128)S(1)}, f32[5,16,32,8]{3,2,1,0:T(8,128)S(1)}) fusion(f32[5,16,32,128]{3,2,1,0:T(8,128)} %q.1), kind=kLoop, calls=%fused_computation.63 | loop fusion | bytes 327680 | tf_op jit(solution)/shard_map/slice | solution.py:237
  2.9 0.4 pad_maximum_fusion
  3.3 0.0 copy-start.2
  3.3 0.4 copy.37
  3.6 0.0 copy-start.11
  3.7 0.0 copy-start.9
  3.7 2.2 %collective-permute-start.4 = (f32[5,4,8,128]{3,2,1,0:T(8,128)S(1)}, f32[5,4,8,128]{3,2,1,0:T(8,128)S(1)}, u32[]{:S(2)}, u32[]{:S(2)}) collective-permute-start(f32[5,4,8,128]{3,2,1,0:T(8,128)S(1)} %get-tuple-element.23), channel_id=1, source_target_pairs={{0,1},{1,2},{2,3},{3,0},{4,5},{5,6},{6,7},{7,4},{8,9},{9,10},{10,1... | collective-permute-start | bytes 245768 | tf_op jit(solution)/shard_map/ppermute | solution.py:42
  5.9 0.0 copy-done.2
  5.9 0.1 fusion.36
  6.0 0.1 reshape.260
  6.0 7.8 %collective-permute-start.2 = (f32[5,48,128]{2,1,0:T(8,128)S(1)}, f32[5,48,128]{2,1,0:T(8,128)S(1)}, u32[]{:S(2)}, u32[]{:S(2)}) collective-permute-start(f32[5,48,128]{2,1,0:T(8,128)S(1)} %reshape.260), channel_id=1, source_target_pairs={{0,4},{4,8},{8,12},{12,0},{1,5},{5,9},{9,13},{13,1},{2,6},{6,10},{... | collective-permute-start | bytes 368648 | tf_op jit(solution)/shard_map/ppermute | solution.py:42
  13.8 0.1 reshape.261
  13.9 0.1 collective-permute-start.3
  14.0 0.8 collective-permute-start
  14.9 4.6 %collective-permute-start.1 = (f32[5,3,32,128]{3,2,1,0:T(8,128)S(1)}, f32[5,3,32,128]{3,2,1,0:T(8,128)S(1)}, u32[]{:S(2)}, u32[]{:S(2)}) collective-permute-start(f32[5,3,32,128]{3,2,1,0:T(8,128)S(1)} %get-tuple-element.20), channel_id=1, source_target_pairs={{16,0},{32,16},{48,32},{64,48},{80,64},{96,80},{112,96},{128,112},... | collective-permute-start | bytes 737288 | tf_op jit(solution)/shard_map/ppermute | solution.py:42
  19.5 0.2 fusion.33
  19.7 0.2 cosine_multiply_fusion.1
  20.0 1.0 cosine_multiply_fusion
  21.0 1.1 fusion.7
  22.1 0.6 sqrt_multiply_fusion.turns
  23.4 0.2 stack.32.geo
  23.6 0.0 collective-permute-done.4.lo
  23.6 0.0 copy-start.7
  23.6 2.0 %collective-permute-start.5 = (f32[5,4,8,128]{3,2,1,0:T(8,128)S(1)}, f32[5,4,8,128]{3,2,1,0:T(8,128)S(1)}, u32[]{:S(2)}, u32[]{:S(2)}) collective-permute-start(f32[5,4,8,128]{3,2,1,0:T(8,128)S(1)} %get-tuple-element.22), channel_id=1, source_target_pairs={{1,0},{2,1},{3,2},{0,3},{5,4},{6,5},{7,6},{4,7},{9,8},{10,9},{11,1... | collective-permute-start | bytes 245768 | tf_op jit(solution)/shard_map/ppermute | solution.py:42
  25.7 1.6 collective-permute-done.5.hi
  27.4 0.0 copy-done.7
  27.4 0.6 copy-done.8
  28.0 12.2 %flow_z.1.add = f32[5,512,128]{2,1,0:T(8,128)} custom-call(f32[5,512,128]{2,1,0:T(8,128)} %bitcast.29, f32[5,4,8,128]{3,2,1,0:T(8,128)} %copy-done.7, f32[5,4,8,128]{3,2,1,0:T(8,128)} %copy-done.8), custom_call_target="tpu_custom_call" | custom-call | flops 30000000 | bytes 4000000 | tf_op jit(solution)/shard_map/flow_z/pallas_call | solution.py:245
  40.2 0.0 collective-permute-done.2.lo
  40.2 0.0 collective-permute-done.3.hi
  40.2 0.6 copy-done.5
  40.9 0.6 copy-done.6
  41.5 12.7 %flow_y.1 = f32[5,512,128]{2,1,0:T(8,128)} custom-call(f32[5,512,128]{2,1,0:T(8,128)} %bitcast.30, f32[5,48,128]{2,1,0:T(8,128)} %copy-done.5, f32[5,48,128]{2,1,0:T(8,128)} %copy-done.6, f32[5,512,128]{2,1,0:T(8,128)} %flow_z.1.add), custom_call_target="tpu_custom_call" | custom-call | flops 30000000 | bytes 4000000 | tf_op jit(solution)/shard_map/flow_y/pallas_call | solution.py:254
  54.2 0.0 collective-permute-done.lo
  54.2 0.0 collective-permute-done.1.hi
  54.2 0.7 copy-done.3
  54.9 0.1 copy-done.4
  54.9 11.2 %flow_x.1 = f32[5,16,32,128]{3,2,1,0:T(8,128)} custom-call(f32[5,16,32,128]{3,2,1,0:T(8,128)} %q.1, f32[5,3,32,128]{3,2,1,0:T(8,128)} %copy-done.3, f32[5,3,32,128]{3,2,1,0:T(8,128)} %copy-done.4, f32[5,16,32,128]{3,2,1,0:T(8,128)} %bitcast.31, f32[5,16,32,128]{3,2,1,0:T(8,128)} %old.1), custom_call_target="tpu_custom_call" | custom-call | flops 30000000 | bytes 4000000 | tf_op jit(solution)/shard_map/flow_x/pallas_call | solution.py:261
  66.1 1.0 slice.89
  67.1 9.5 %panels.1 = f32[4,2,128,256]{3,2,1,0:T(8,128)S(1)} custom-call(s32[1]{0:T(128)S(6)} %copy.48.live, f32[512,128]{1,0:T(8,128)S(1)} %bitcast.27, bf16[4096,512]{1,0:T(8,128)(2,1)S(1)} %copy-done.1, s32[32,1,128]{2,1,0:T(1,128)S(1)} %bitcast.28, f32[32,8,128]{2,1,0:T(8,128)S(1)} %stack.32.geo, f32[32,1,1024]{2,1,0:T(1,128)S(1)} %sqrt_multiply_fusion.turns, ...), custom_call_target="tpu_custom_call" | custom-call | flops 4000000000 | bytes 8000000 | tf_op jit(solution)/shard_map/panels/pallas_call | solution.py:383
  76.6 42.3 %all_to_all.15 = f32[4,2,128,256]{3,2,1,0:T(8,128)S(1)} all-to-all(f32[4,2,128,256]{3,2,1,0:T(8,128)S(1)} %panels.1), channel_id=1, replica_groups=mesh['gx'=16,'gy'=4,'gz'=4] {'gz'}, dimensions={0} | all-to-all | bytes 2097152 | tf_op jit(solution)/shard_map/all_to_all | solution.py:23
  118.9 0.1 reduce_sum.48
  119.0 0.1 reshape_reshape.6
  119.1 25.6 %all_to_all.16 = f32[64,4,256]{2,1,0:T(4,128)S(1)} all-to-all(f32[64,4,256]{2,1,0:T(4,128)S(1)} %reshape_reshape.6), channel_id=1, replica_groups=mesh['gx'=16,'gy'=4,'gz'=4] {'gx','gy'}, dimensions={0} | all-to-all | bytes 524288 | tf_op jit(solution)/shard_map/all_to_all | solution.py:23
  144.7 0.1 reduce_sum.49
  144.8 17.8 %all_to_all.17 = f32[64,4,256]{2,1,0:T(4,128)S(1)} all-to-all(f32[64,4,256]{2,1,0:T(4,128)S(1)} %broadcast_in_dim.2), channel_id=1, replica_groups=mesh['gx'=16,'gy'=4,'gz'=4] {'gx','gy'}, dimensions={0} | all-to-all | bytes 524288 | tf_op jit(solution)/shard_map/all_to_all | solution.py:28
  162.6 0.1 reshape_reshape.7
  162.7 0.8 copy.44
  (26 shorter events, 0.2 us)
Async XLA Ops:
  3.3 2.6 %copy-start.2 = (f32[5,16,32,128]{3,2,1,0:T(8,128)S(1)}, f32[5,16,32,128]{3,2,1,0:T(8,128)}, u32[]{:S(2)}) copy-start(f32[5,16,32,128]{3,2,1,0:T(8,128)} %q.1) | copy-start | bytes 3932164
  3.6 15.9 %copy-start = (s32[32,128]{1,0:T(8,128)S(1)}, s32[32,128]{1,0:T(8,128)}, u32[]{:S(2)}) copy-start(s32[32,128]{1,0:T(8,128)} %param.11) | copy-start | bytes 49156
  3.6 16.0 %copy-start.10 = (f32[2,1024]{1,0:T(2,128)S(1)}, f32[2,1024]{1,0:T(2,128)}, u32[]{:S(2)}) copy-start(f32[2,1024]{1,0:T(2,128)} %param.14) | copy-start | bytes 24580
  3.6 16.3 %copy-start.11 = (f32[1024]{0:T(1024)S(1)}, f32[1024]{0:T(1024)}, u32[]{:S(2)}) copy-start(f32[1024]{0:T(1024)} %param.15) | copy-start | bytes 12292
  3.7 16.3 %copy-start.9 = (f32[2,4096]{1,0:T(2,128)S(1)}, f32[2,4096]{1,0:T(2,128)}, u32[]{:S(2)}) copy-start(f32[2,4096]{1,0:T(2,128)} %param.12) | copy-start | bytes 98308
  3.7 19.9 %collective-permute-start.4 = (f32[5,4,8,128]{3,2,1,0:T(8,128)S(1)}, f32[5,4,8,128]{3,2,1,0:T(8,128)S(1)}, u32[]{:S(2)}, u32[]{:S(2)}) collective-permute-start(f32[5,4,8,128]{3,2,1,0:T(8,128)S(1)} %get-tuple-element.23), channel_id=1, source_target_pairs={{0,1},{1,2},{2,3},{3,0},{4,5},{5,6},{6,7},{7,4},{8,9},{9,10},{10,1... | collective-permute-start | bytes 245768 | tf_op jit(solution)/shard_map/ppermute | solution.py:42
  6.0 34.2 %collective-permute-start.2 = (f32[5,48,128]{2,1,0:T(8,128)S(1)}, f32[5,48,128]{2,1,0:T(8,128)S(1)}, u32[]{:S(2)}, u32[]{:S(2)}) collective-permute-start(f32[5,48,128]{2,1,0:T(8,128)S(1)} %reshape.260), channel_id=1, source_target_pairs={{0,4},{4,8},{8,12},{12,0},{1,5},{5,9},{9,13},{13,1},{2,6},{6,10},{... | collective-permute-start | bytes 368648 | tf_op jit(solution)/shard_map/ppermute | solution.py:42
  13.9 26.3 %collective-permute-start.3 = (f32[5,48,128]{2,1,0:T(8,128)S(1)}, f32[5,48,128]{2,1,0:T(8,128)S(1)}, u32[]{:S(2)}, u32[]{:S(2)}) collective-permute-start(f32[5,48,128]{2,1,0:T(8,128)S(1)} %reshape.261), channel_id=1, source_target_pairs={{4,0},{8,4},{12,8},{0,12},{5,1},{9,5},{13,9},{1,13},{6,2},{10,6},{... | collective-permute-start | bytes 368648 | tf_op jit(solution)/shard_map/ppermute | solution.py:42
  14.0 40.1 %collective-permute-start = (f32[5,3,32,128]{3,2,1,0:T(8,128)S(1)}, f32[5,3,32,128]{3,2,1,0:T(8,128)S(1)}, u32[]{:S(2)}, u32[]{:S(2)}) collective-permute-start(f32[5,3,32,128]{3,2,1,0:T(8,128)S(1)} %get-tuple-element.21), channel_id=1, source_target_pairs={{0,16},{16,32},{32,48},{48,64},{64,80},{80,96},{96,112},{112,128},... | collective-permute-start | bytes 737288 | tf_op jit(solution)/shard_map/ppermute | solution.py:42
  14.9 39.3 %collective-permute-start.1 = (f32[5,3,32,128]{3,2,1,0:T(8,128)S(1)}, f32[5,3,32,128]{3,2,1,0:T(8,128)S(1)}, u32[]{:S(2)}, u32[]{:S(2)}) collective-permute-start(f32[5,3,32,128]{3,2,1,0:T(8,128)S(1)} %get-tuple-element.20), channel_id=1, source_target_pairs={{16,0},{32,16},{48,32},{64,48},{80,64},{96,80},{112,96},{128,112},... | collective-permute-start | bytes 737288 | tf_op jit(solution)/shard_map/ppermute | solution.py:42
  23.6 3.7 %copy-start.7 = (f32[5,4,8,128]{3,2,1,0:T(8,128)}, f32[5,4,8,128]{3,2,1,0:T(8,128)S(1)}, u32[]{:S(2)}) copy-start(f32[5,4,8,128]{3,2,1,0:T(8,128)S(1)} %collective-permute-done.4.lo) | copy-start | bytes 245764
  23.6 3.7 %collective-permute-start.5 = (f32[5,4,8,128]{3,2,1,0:T(8,128)S(1)}, f32[5,4,8,128]{3,2,1,0:T(8,128)S(1)}, u32[]{:S(2)}, u32[]{:S(2)}) collective-permute-start(f32[5,4,8,128]{3,2,1,0:T(8,128)S(1)} %get-tuple-element.22), channel_id=1, source_target_pairs={{1,0},{2,1},{3,2},{0,3},{5,4},{6,5},{7,6},{4,7},{9,8},{10,9},{11,1... | collective-permute-start | bytes 245768 | tf_op jit(solution)/shard_map/ppermute | solution.py:42
  27.4 0.6 copy-start.8
  40.2 0.6 copy-start.5
  40.9 0.6 copy-start.6
  54.2 0.7 copy-start.3
  54.2 0.8 copy-start.4
  54.9 12.2 %copy-start.1 = (bf16[4096,512]{1,0:T(8,128)(2,1)S(1)}, bf16[4096,512]{1,0:T(8,128)(2,1)}, u32[]{:S(2)}) copy-start(bf16[4096,512]{1,0:T(8,128)(2,1)} %record.1) | copy-start | bytes 12582916

commit v2 on v1

--- a/solution.py
+++ b/solution.py
@@ -16,7 +16,7 @@
 COURANT = 0.08
 
 SCALE = 4.0
-EPS = 4.0 * SCALE * SCALE * WENO_EPS
+EPS = 0.75 * 4.0 * SCALE * SCALE * WENO_EPS
 
 
 def summed_on_arrival(blocks, axis):
@@ -50,7 +50,8 @@
     kinetic = 0.5 * (momenta[0] * velocity[0] + momenta[1] * velocity[1] + momenta[2] * velocity[2])
     pressure = (GAMMA_GAS - 1.0) * (energy - kinetic) - GAMMA_GAS * PRESSURE_INF * SCALE
     normal = velocity[axis_d]
-    sound = jnp.sqrt(GAMMA_GAS * (pressure + PRESSURE_INF * SCALE) * inverse)
+    square = GAMMA_GAS * (pressure + PRESSURE_INF * SCALE) * inverse
+    sound = square * lax.rsqrt(square)
     rows = [momenta[axis_d]]
     for component in range(3):
         carried = momenta[component] * normal
@@ -60,11 +61,12 @@
 
 
 def weno_terms(e0, e1, e2, d1, d2):
-    base1 = d1 * d1 + EPS
-    base2 = d2 * d2 + EPS
-    t0 = e0 * ((4.0 / 3.0) * e0 + d1) + base1
-    t1 = e1 * ((4.0 / 3.0) * e1 + d1) + base1
-    t2 = e2 * ((4.0 / 3.0) * e2 - d2) + base2
+    q1, q2 = 0.75 * d1, 0.75 * d2
+    base1 = d1 * q1 + EPS
+    base2 = d2 * q2 + EPS
+    t0 = e0 * (e0 + q1) + base1
+    t1 = e1 * (e1 + q1) + base1
+    t2 = e2 * (e2 - q2) + base2
     p01, p02, p12 = t0 * t1, t0 * t2, t1 * t2
     wa = p12 * p12
     wb = 6.0 * (p02 * p02)
@@ -82,27 +84,31 @@
     return fsum + ((0.5 * (up[1] - dn[3]) - aq[2]) + ratio) * (1.0 / 3.0)
 
 
-def sweep(planes, dq, df, fs, m2, faces, axis_d, cells, chunks):
-    for r in range(chunks):
-        rows = pl.ds(8 * r, 8)
-
-        def load(j):
-            return [planes[c, j, rows, :] for c in range(5)]
-
-        def step(j, carry):
-            state, flux, speed = carry
-            next_state = load(j + 1)
-            next_flux, next_speed = flux_of(next_state, axis_d)
-            for c in range(5):
-                dq[c, j, rows, :] = next_state[c] - state[c]
-                df[c, j, rows, :] = next_flux[c] - flux[c]
-                fs[c, j, rows, :] = next_flux[c] + flux[c]
-            m2[j, rows, :] = jnp.maximum(next_speed, speed)
-            return next_state, next_flux, next_speed
-
-        first = load(0)
-        first_flux, first_speed = flux_of(first, axis_d)
-        lax.fori_loop(0, cells + 5, step, (first, first_flux, first_speed))
+def sweep(planes, dq, df, fs, m2, faces, axis_d, cells, chunks, streams):
+    def load(r, j):
+        return [planes[c, j, pl.ds(8 * r, 8), :] for c in range(5)]
+
+    for group, length in streams:
+
+        def step(k, carry):
+            after = []
+            for (r, start), (state, flux, speed) in zip(group, carry):
+                j, rows = start + k, pl.ds(8 * r, 8)
+                next_state = load(r, j + 1)
+                next_flux, next_speed = flux_of(next_state, axis_d)
+                for c in range(5):
+                    dq[c, j, rows, :] = next_state[c] - state[c]
+                    df[c, j, rows, :] = next_flux[c] - flux[c]
+                    fs[c, j, rows, :] = next_flux[c] + flux[c]
+                m2[j, rows, :] = jnp.maximum(next_speed, speed)
+                after.append((next_state, next_flux, next_speed))
+            return after
+
+        begin = []
+        for r, start in group:
+            state = load(r, start)
+            begin.append((state, *flux_of(state, axis_d)))
+        lax.fori_loop(0, length, step, begin)
 
     def face(i, carry):
         for r in range(chunks):
@@ -120,7 +126,7 @@
     lax.fori_loop(0, cells + 1, face, 0)
 
 
-def z_kernel(coef, q, lo, hi, out, turned, planes, dq, df, fs, m2, faces, diff):
+def z_part(coef, q, lo, hi, out, turned, planes, dq, df, fs, m2, faces, diff):
     for c in range(5):
         for blk in range(4):
             tile = jnp.transpose(q[c, pl.ds(128 * blk, 128), :]) * SCALE
@@ -135,15 +141,15 @@
             planes[c, j] = turned[c, pl.ds(j + 5, 8, stride=80), :]
         return carry
 
-    lax.fori_loop(0, 70, gather, 0)
-    sweep(planes, dq, df, fs, m2, faces, 2, 64, 1)
+    lax.fori_loop(0, 70, gather, 0, unroll=2)
+    sweep(planes, dq, df, fs, m2, faces, 2, 64, 1, [(((0, 0), (0, 23), (0, 46)), 23)])
 
     def difference(i, carry):
         for c in range(5):
             diff[c, pl.ds(pl.multiple_of(8 * i, 8), 8), :] = coef * (faces[c, i + 1] - faces[c, i])
         return carry
 
-    lax.fori_loop(0, 64, difference, 0)
+    lax.fori_loop(0, 64, difference, 0, unroll=2)
     for c in range(5):
         for blk in range(4):
             tile = jnp.concatenate(
@@ -152,7 +158,7 @@
             out[c, pl.ds(128 * blk, 128), :] = jnp.transpose(tile)
 
 
-def y_kernel(coef, q, lo, hi, add, out, planes, dq, df, fs, m2, faces, diff):
+def y_part(coef, q, lo, hi, out, planes, dq, df, fs, m2, faces, diff):
     for c in range(5):
         for h in range(2):
             rows = pl.ds(8 * h, 8)
@@ -169,7 +175,7 @@
         return carry
 
     lax.fori_loop(0, 32, gather, 0)
-    sweep(planes, dq, df, fs, m2, faces, 1, 32, 2)
+    sweep(planes, dq, df, fs, m2, faces, 1, 32, 2, [(((0, 0), (1, 0)), 37)])
 
     def difference(i, carry):
         for c in range(5):
@@ -184,33 +190,41 @@
         for c in range(5):
             for y8 in range(4):
                 rows = pl.ds(pl.multiple_of(32 * x + 8 * y8, 8), 8)
-                out[c, rows, :] = add[c, rows, :] + diff[c, pl.ds(128 * y8 + x, 8, stride=16), :]
+                out[c, rows, :] += diff[c, pl.ds(128 * y8 + x, 8, stride=16), :]
         return carry
 
     lax.fori_loop(0, 16, back, 0)
 
 
-def x_kernel(coef, q, lo, hi, add, old, out, planes, dq, df, fs, m2, faces):
+def x_part(coef, q, lo, hi, add, old, out, planes, dq, df, fs, m2, faces):
     for c in range(5):
         for k in range(3):
-            planes[c, k] = lo[c, k] * SCALE
-            planes[c, 19 + k] = hi[c, k] * SCALE
+            planes[c, k] = lo[c, pl.ds(32 * k, 32), :] * SCALE
+            planes[c, 19 + k] = hi[c, pl.ds(32 * k, 32), :] * SCALE
 
     def gather(j, carry):
         for c in range(5):
-            planes[c, j + 3] = q[c, j] * SCALE
+            planes[c, j + 3] = q[c, pl.ds(pl.multiple_of(32 * j, 32), 32), :] * SCALE
         return carry
 
     lax.fori_loop(0, 16, gather, 0)
-    sweep(planes, dq, df, fs, m2, faces, 0, 16, 4)
+    streams = [(((0, 0), (1, 0)), 21), (((2, 0), (3, 0)), 21)]
+    sweep(planes, dq, df, fs, m2, faces, 0, 16, 4, streams)
 
     def finish(i, carry):
-        for c in range(5):
-            change = add[c, i] + coef * (faces[c, i + 1] - faces[c, i])
-            out[c, i] = 0.75 * old[c, i] + 0.25 * q[c, i] - change
+        rows = pl.ds(pl.multiple_of(32 * i, 32), 32)
+        for c in range(5):
+            change = add[c, rows, :] + coef * (faces[c, i + 1] - faces[c, i])
+            out[c, rows, :] = (0.75 * old[c, rows, :] + 0.25 * q[c, rows, :]) - change
         return carry
 
     lax.fori_loop(0, 16, finish, 0)
+
+
+def flow_kernel(coefs, q, old, z_lo, z_hi, y_lo, y_hi, x_lo, x_hi, out, turned, diff, add, *spaces):
+    z_part(coefs[2], q, z_lo, z_hi, add, turned, *spaces[0:6], diff)
+    y_part(coefs[1], q, y_lo, y_hi, add, *spaces[6:12], diff)
+    x_part(coefs[0], q, x_lo, x_hi, add, old, out, *spaces[12:18])
 
 
 def sweep_scratch(cells, rows):
@@ -225,46 +239,29 @@
     ]
 
 
-FLOW_PARAMS = dict(
-    compiler_params=pltpu.CompilerParams(vmem_limit_bytes=56 * 2**20),
-    cost_estimate=pl.CostEstimate(flops=30_000_000, bytes_accessed=4_000_000, transcendentals=0),
-)
-
-
 def flow_update(state_old, state_section, counts, step_size):
     f32 = jnp.float32
     rows = state_section.reshape(5, 512, 128)
+    x_lo, x_hi = edge_swap(rows[:, :96], rows[:, 416:], "gx")
+    y_lo, y_hi = edge_swap(
+        state_section[:, :, :3].reshape(5, 48, 128), state_section[:, :, 29:].reshape(5, 48, 128), "gy"
+    )
     strips = jnp.concatenate([state_section[..., :8], state_section[..., 120:]], axis=-1)
     strips = jnp.transpose(strips.reshape(5, 4, 128, 16), (0, 1, 3, 2))
     z_lo, z_hi = edge_swap(strips[:, :, :8], strips[:, :, 8:], "gz")
-    y_lo, y_hi = edge_swap(
-        state_section[:, :, :3].reshape(5, 48, 128), state_section[:, :, 29:].reshape(5, 48, 128), "gy"
-    )
-    x_lo, x_hi = edge_swap(state_section[:, :3], state_section[:, 13:], "gx")
     coefs = [0.25 * step_size * n / (2.0 * SCALE) for n in counts]
-    part = pl.pallas_call(
-        functools.partial(z_kernel, coefs[2]),
+    return pl.pallas_call(
+        functools.partial(flow_kernel, coefs),
         out_shape=jax.ShapeDtypeStruct((5, 512, 128), f32),
         scratch_shapes=[pltpu.VMEM((5, 640, 128), f32)]
+        + [pltpu.VMEM((5, 512, 128), f32)] * 2
         + sweep_scratch(64, 8)
-        + [pltpu.VMEM((5, 512, 128), f32)],
-        name="flow_z",
-        **FLOW_PARAMS,
-    )(rows, z_lo, z_hi)
-    part = pl.pallas_call(
-        functools.partial(y_kernel, coefs[1]),
-        out_shape=jax.ShapeDtypeStruct((5, 512, 128), f32),
-        scratch_shapes=sweep_scratch(32, 16) + [pltpu.VMEM((5, 512, 128), f32)],
-        name="flow_y",
-        **FLOW_PARAMS,
-    )(rows, y_lo, y_hi, part)
-    return pl.pallas_call(
-        functools.partial(x_kernel, coefs[0]),
-        out_shape=jax.ShapeDtypeStruct((5, 16, 32, 128), f32),
-        scratch_shapes=sweep_scratch(16, 32),
-        name="flow_x",
-        **FLOW_PARAMS,
-    )(state_section, x_lo, x_hi, part.reshape(5, 16, 32, 128), state_old)
+        + sweep_scratch(32, 16)
+        + sweep_scratch(16, 32),
+        compiler_params=pltpu.CompilerParams(vmem_limit_bytes=56 * 2**20),
+        cost_estimate=pl.CostEstimate(flops=100_000_000, bytes_accessed=6_000_000, transcendentals=0),
+        name="flow",
+    )(rows, state_old.reshape(5, 512, 128), z_lo, z_hi, y_lo, y_hi, x_lo, x_hi)
 
 
 def directions(angles):
@@ -319,24 +316,24 @@
 OBS_CHUNK = 256
 
 
-def panel_kernel(live, density, record, cells, geo, turns, listeners, table, out, pieces):
+def in_pieces(values):
+    pieces = []
+    for _ in range(3):
+        piece = values.astype(jnp.bfloat16).astype(jnp.float32)
+        pieces.append(piece)
+        values = values - piece
+    return pieces
+
+
+PAIRS = ((0, 0), (0, 1), (1, 0), (0, 2), (1, 1), (2, 0))
+
+
+def panel_kernel(
+    live, density, record, cells, geo, turns, listeners, table, out, pieces, heard, spectra
+):
     b = pl.program_id(0)
 
-    @pl.when(b == 0)
-    def _():
-        out[...] = jnp.zeros_like(out)
-        turned = jnp.concatenate(
-            [jnp.transpose(density[pl.ds(128 * k, 128), :]) for k in range(4)], axis=1
-        )
-        high = turned.astype(jnp.bfloat16)
-        rest = turned - high.astype(jnp.float32)
-        middle = rest.astype(jnp.bfloat16)
-        pieces[pl.ds(0, 128), :] = high
-        pieces[pl.ds(128, 128), :] = middle
-        pieces[pl.ds(256, 128), :] = (rest - middle.astype(jnp.float32)).astype(jnp.bfloat16)
-
-    @pl.when(b < live[0])
-    def _():
+    def front():
         cell = cells[0]
         grid_row = lax.broadcasted_iota(jnp.int32, (512, 128), 0)
         chosen = jnp.where(grid_row == cell // 128, 1.0, 0.0).astype(jnp.bfloat16)
@@ -344,61 +341,98 @@
         found = (found[:128] + found[128:256]) + found[256:]
         lane = lax.broadcasted_iota(jnp.int32, (128, 128), 0)
         sampled = jnp.sum(jnp.where(lane == cell % 128, found, 0.0), axis=0, keepdims=True)
-        place = lax.broadcasted_iota(jnp.int32, (8, 128), 0)
-        columns = jnp.transpose(jnp.where(place == 6, sampled, geo[0]))
-        sources = (record[...].astype(jnp.float32) * columns[:, 6:7]).astype(jnp.bfloat16)
-        spectra = lax.dot_general(
+        column = jnp.transpose(jnp.broadcast_to(sampled, (8, 128)))[:, 0:1]
+        sources = (record[...].astype(jnp.float32) * column).astype(jnp.bfloat16)
+        spectra[lax.rem(b, 2)] = lax.dot_general(
             table[...], sources, (((1,), (1,)), ((), ())), preferred_element_type=jnp.float32
+        ).astype(jnp.bfloat16)
+
+    def back():
+        spectrum = spectra[lax.rem(b + 1, 2)]
+        facing_pieces, apart_pieces = in_pieces(geo[0, 0:8]), in_pieces(geo[0, 8:16])
+        seen = jnp.concatenate(
+            [
+                jnp.concatenate([facing_pieces[s], apart_pieces[s]], axis=1)
+                for s, _ in PAIRS
+            ],
+            axis=0,
         ).astype(jnp.bfloat16)
         order = (lax.broadcasted_iota(jnp.int32, (8, 128), 0) + 1).astype(jnp.float32)
         for o in range(1024 // OBS_CHUNK):
-            span = pl.ds(OBS_CHUNK * o, OBS_CHUNK)
-            offs = [listeners[pl.ds(d, 1), span] - columns[:, d : d + 1] for d in range(3)]
-            reach = (offs[0] * offs[0] + offs[1] * offs[1]) + offs[2] * offs[2]
-            facing = (offs[0] * columns[:, 3:4] + offs[1] * columns[:, 4:5]) + offs[2] * columns[:, 5:6]
-            weights = (facing / reach).astype(jnp.bfloat16)
-            product = jnp.dot(spectra, weights, preferred_element_type=jnp.float32)
+            both = lax.dot_general(
+                seen,
+                heard[:, OBS_CHUNK * o : OBS_CHUNK * (o + 1)],
+                (((0,), (0,)), ((), ())),
+                preferred_element_type=jnp.float32,
+            )
+            weights = (both[:128] / both[128:]).astype(jnp.bfloat16)
+            product = jnp.dot(spectrum, weights, preferred_element_type=jnp.float32)
             for h in range(OBS_CHUNK // 128):
                 lanes = slice(128 * h, 128 * h + 128)
                 base = turns[0, :, pl.ds(OBS_CHUNK * o + 128 * h, 128)]
                 sine, cosine = sin_cos(base * order)
                 step_s = jnp.broadcast_to(sine[7:8], (8, 128))
                 step_c = jnp.broadcast_to(cosine[7:8], (8, 128))
+                before_s = sine * step_c - cosine * step_s
+                before_c = cosine * step_c + sine * step_s
+                twice = step_c + step_c
                 for a in range(FREQS // 8):
                     re = product[8 * a : 8 * a + 8, lanes]
                     im = product[FREQS + 8 * a : FREQS + 8 * a + 8, lanes]
                     out[o, 0, pl.ds(8 * a, 8), lanes] += re * cosine + im * sine
                     out[o, 1, pl.ds(8 * a, 8), lanes] += im * cosine - re * sine
                     if a + 1 < FREQS // 8:
-                        sine, cosine = (
-                            sine * step_c + cosine * step_s,
-                            cosine * step_c - sine * step_s,
-                        )
+                        sine, before_s = twice * sine - before_s, sine
+                        cosine, before_c = twice * cosine - before_c, cosine
+
+    @pl.when(b == 0)
+    def _():
+        out[...] = jnp.zeros_like(out)
+        turned = jnp.concatenate(
+            [jnp.transpose(density[pl.ds(128 * k, 128), :]) for k in range(4)], axis=1
+        )
+        for k, piece in enumerate(in_pieces(turned)):
+            pieces[pl.ds(128 * k, 128), :] = piece.astype(jnp.bfloat16)
+        split = in_pieces(listeners[...])
+        heard[...] = jnp.concatenate([split[t] for _, t in PAIRS], axis=0).astype(jnp.bfloat16)
+        front()
+
+    @pl.when((b > 0) & (b <= live[0]))
+    def _():
+        front()
+        back()
 
 
 def panel_sums(live_count, density, record, cells, geo, turns, listeners, table):
-    def at(b, live):
+    def now(b, live):
         return jnp.minimum(b, live[0] - 1)
+
+    def last(b, live):
+        return jnp.maximum(jnp.minimum(b, live[0]) - 1, 0)
 
     return pl.pallas_call(
         panel_kernel,
         out_shape=jax.ShapeDtypeStruct((1024 // OBS_CHUNK, 2, FREQS, OBS_CHUNK), jnp.float32),
         grid_spec=pltpu.PrefetchScalarGridSpec(
             num_scalar_prefetch=1,
-            grid=(32,),
+            grid=(33,),
             in_specs=[
                 pl.BlockSpec((512, 128), lambda b, live: (0, 0)),
-                pl.BlockSpec((128, 512), lambda b, live: (at(b, live), 0)),
-                pl.BlockSpec((1, 1, 128), lambda b, live: (at(b, live), 0, 0)),
-                pl.BlockSpec((1, 8, 128), lambda b, live: (at(b, live), 0, 0)),
-                pl.BlockSpec((1, 1, 1024), lambda b, live: (at(b, live), 0, 0)),
+                pl.BlockSpec((128, 512), lambda b, live: (now(b, live), 0)),
+                pl.BlockSpec((1, 1, 128), lambda b, live: (now(b, live), 0, 0)),
+                pl.BlockSpec((1, 16, 128), lambda b, live: (last(b, live), 0, 0)),
+                pl.BlockSpec((1, 1, 1024), lambda b, live: (last(b, live), 0, 0)),
                 pl.BlockSpec((8, 1024), lambda b, live: (0, 0)),
                 pl.BlockSpec((256, 512), lambda b, live: (0, 0)),
             ],
             out_specs=pl.BlockSpec(
                 (1024 // OBS_CHUNK, 2, FREQS, OBS_CHUNK), lambda b, live: (0, 0, 0, 0)
             ),
-            scratch_shapes=[pltpu.VMEM((384, 512), jnp.bfloat16)],
+            scratch_shapes=[
+                pltpu.VMEM((384, 512), jnp.bfloat16),
+                pltpu.VMEM((8 * len(PAIRS), 1024), jnp.bfloat16),
+                pltpu.VMEM((2, 256, 128), jnp.bfloat16),
+            ],
         ),
         compiler_params=pltpu.CompilerParams(
             dimension_semantics=("arbitrary",), vmem_limit_bytes=48 * 2**20
@@ -412,15 +446,25 @@
 
 def panel_geometry(panel_cell, panel_angles, listener_angles, listener_range, blocks, cells, counts):
     slot_count, block_rows = panel_cell.shape
-    places = panel_places(panel_cell, blocks, cells, counts)
+    places = [p - 0.5 for p in panel_places(panel_cell, blocks, cells, counts)]
     normals = directions(panel_angles.reshape(2, slot_count, block_rows)) * (0.25 / math.pi)
-    blank = jnp.zeros_like(places[0])
-    geo = jnp.stack([*places, normals[0], normals[1], normals[2], blank, blank], axis=1)
-    listeners = 0.5 + listener_range[None, :] * directions(listener_angles)
+    across = -sum(normals[d] * places[d] for d in range(3))
+    square = sum(p * p for p in places)
+    blank = jnp.zeros_like(square)
+    geo = jnp.stack(
+        [normals[0], normals[1], normals[2], across, blank, blank, blank, blank]
+        + [-2.0 * p for p in places]
+        + [square, blank + 1.0, blank, blank, blank],
+        axis=1,
+    )
+    heard = listener_range[None, :] * directions(listener_angles)
     centres = [jnp.mean(p, axis=1, keepdims=True) for p in places]
-    apart = sum((listeners[d][None, :] - centres[d]) ** 2 for d in range(3))
+    apart = sum((heard[d][None, :] - centres[d]) ** 2 for d in range(3))
     turns = jnp.sqrt(apart) * (WAVE_STEP / (2.0 * math.pi))
-    listeners = jnp.concatenate([listeners, jnp.zeros((5, listeners.shape[1]), jnp.float32)], axis=0)
+    listeners = jnp.concatenate(
+        [heard, jnp.ones_like(heard[:1]), jnp.sum(heard * heard, axis=0, keepdims=True), jnp.zeros_like(heard)],
+        axis=0,
+    )
     return geo, turns.reshape(slot_count, 1, -1), listeners
 
 
@@ -450,7 +494,7 @@
     updated = flow_update(state_old, state_section, counts, step_size)
     partial = panel_sums(
         owned_blocks,
-        updated[0].reshape(512, 128),
+        updated[0],
         panel_record,
         panel_cell.reshape(32, 1, 128),
         geo,
@@ -460,7 +504,7 @@
     )
     gz_share = summed_on_arrival(partial, "gz")
     spectra_out = sum_by_parts(gz_share.reshape(2 * FREQS, OBS_CHUNK), ("gx", "gy"))
-    return updated, jnp.transpose(spectra_out.reshape(2, FREQS, OBS_CHUNK), (0, 2, 1))
+    return updated.reshape(state_section.shape), jnp.transpose(spectra_out.reshape(2, FREQS, OBS_CHUNK), (0, 2, 1))
 
 
 def solution(mesh):

time: 163 us -> 158 us (0.969); the launches traced: 164 us -> 156 us
  Pallas kernels: 45.6 us -> 36.5 us
  waiting for transfers between devices: 1.63 us -> 5.09 us
  local copies, waits for them, and re-layouts: 7.71 us -> 6.04 us
    pallas_call x3 -> x1, Pallas kernels: 36.1 us -> 25.9 us  [flow_update(): pl.pallas_call(functools.partial(flow_kernel, coefs), out_shape=jax.Shape...]
    ppermute x3, waiting for transfers between devices: 1.62 us -> 5.08 us  [edge_swap(): lax.ppermute(low_edge, axis, down)]
    unnamed x25, local copies, waits for them, and re-layouts: 3.53 us -> 1.56 us
  transfers between devices with their start and end apart: 6 -> 6, of which waited for: 1 -> 2; matrix products, arithmetic and copies ran while one was open for 2% -> 3% of each run, Pallas kernels for 15% -> 0%
where the time goes in v2:
time: 158 us; the launch traced here: 156 us
  blocking collectives  85.1 us (54%)
  Pallas kernels  36.5 us (23%)
  starting transfers between devices  17.8 us (11%)
  local copies, waits for them, and re-layouts  6.04 us (4%)
  waiting for transfers between devices  5.09 us (3%)
  other arithmetic  3.95 us (2%)
  between operations  1.63 us (1%)
    all_to_all x2, blocking collectives, summed_on_arrival(): return jnp.sum(lax.all_to_all(blocks, axis, 0, 0, tiled=True), axis=0)  67.3 us
    pallas_call x1, Pallas kernels, flow_update(): pl.pallas_call(functools.partial(flow_kernel, coefs), out_shape=jax.Shape...  25.9 us
    all_to_all x1, blocking collectives, collect(): return lax.all_to_all(copies, axis, split_axis=0, concat_axis=0, tiled=True)  17.8 us
    ppermute x3, starting transfers between devices, edge_swap(): lax.ppermute(high_edge, axis, up)  10.8 us
    pallas_call x1, Pallas kernels, panel_sums(): pl.pallas_call(panel_kernel, out_shape=jax.ShapeDtypeStruct((1024 // OBS_...  10.6 us
    ppermute x3, starting transfers between devices, edge_swap(): lax.ppermute(low_edge, axis, down)  6.93 us
    ppermute x3, waiting for transfers between devices, edge_swap(): lax.ppermute(low_edge, axis, down)  5.08 us
  transfers between devices with their start and end apart: 6, of which 2 were waited for; matrix products, arithmetic and copies ran while one was open for 3% of the time, Pallas kernels for 0%

profile of v2, /device:TPU:1, one launch (start us, length us, event | category | flops | bytes accessed | tf_op | source)
XLA Modules:
  0.0 156.1 jit_solution(13764043851207069374)
XLA Ops:
  0.6 2.2 %fusion.40 = (f32[5,16,32,8]{3,2,1,0:T(8,128)S(1)}, f32[5,16,32,8]{3,2,1,0:T(8,128)S(1)}) fusion(f32[5,16,32,128]{3,2,1,0:T(8,128)} %param.9), kind=kLoop, calls=%fused_computation.80 | loop fusion | bytes 327680 | tf_op jit(solution)/shard_map/slice | solution.py:249
  2.9 0.4 pad_maximum_fusion
  3.3 0.0 copy-start.2
  3.3 0.4 copy.49
  3.7 0.0 copy-start.10
  3.7 0.0 copy-start.11
  3.7 0.0 copy-start
  3.7 2.2 %collective-permute-start = (f32[5,4,8,128]{3,2,1,0:T(8,128)S(1)}, f32[5,4,8,128]{3,2,1,0:T(8,128)S(1)}, u32[]{:S(2)}, u32[]{:S(2)}) collective-permute-start(f32[5,4,8,128]{3,2,1,0:T(8,128)S(1)} %get-tuple-element.23), channel_id=1, source_target_pairs={{0,1},{1,2},{2,3},{3,0},{4,5},{5,6},{6,7},{7,4},{8,9},{9,10},{10,1... | collective-permute-start | bytes 245768 | tf_op jit(solution)/shard_map/ppermute | solution.py:42
  5.9 0.1 fusion.39
  6.0 0.1 reshape.265
  6.0 7.8 %collective-permute-start.2 = (f32[5,48,128]{2,1,0:T(8,128)S(1)}, f32[5,48,128]{2,1,0:T(8,128)S(1)}, u32[]{:S(2)}, u32[]{:S(2)}) collective-permute-start(f32[5,48,128]{2,1,0:T(8,128)S(1)} %reshape.265), channel_id=1, source_target_pairs={{0,4},{4,8},{8,12},{12,0},{1,5},{5,9},{9,13},{13,1},{2,6},{6,10},{... | collective-permute-start | bytes 368648 | tf_op jit(solution)/shard_map/ppermute | solution.py:42
  13.9 0.1 reshape.266
  13.9 0.1 collective-permute-start.3
  14.1 0.8 collective-permute-start.4
  14.9 4.6 %collective-permute-start.5 = (f32[5,96,128]{2,1,0:T(8,128)S(1)}, f32[5,96,128]{2,1,0:T(8,128)S(1)}, u32[]{:S(2)}, u32[]{:S(2)}) collective-permute-start(f32[5,96,128]{2,1,0:T(8,128)S(1)} %get-tuple-element.16), channel_id=1, source_target_pairs={{16,0},{32,16},{48,32},{64,48},{80,64},{96,80},{112,96},{128,112},... | collective-permute-start | bytes 737288 | tf_op jit(solution)/shard_map/ppermute | solution.py:42
  19.5 0.0 copy-done.9
  19.5 1.0 cosine_multiply_fusion
  20.5 0.2 cosine_multiply_fusion.1
  20.8 0.0 copy-done.11
  20.9 0.1 fusion.36
  21.0 0.1 pad.5.clone
  21.1 0.1 pad.3.clone
  21.2 1.1 fusion.7
  22.3 0.1 fusion.34
  22.4 0.6 sqrt_multiply_fusion.turns
  23.1 0.1 maximum_maximum_fusion.listeners
  23.9 0.3 stack.48.geo
  24.2 0.0 collective-permute-done.z_lo
  24.2 2.2 %collective-permute-start.1 = (f32[5,4,8,128]{3,2,1,0:T(8,128)S(1)}, f32[5,4,8,128]{3,2,1,0:T(8,128)S(1)}, u32[]{:S(2)}, u32[]{:S(2)}) collective-permute-start(f32[5,4,8,128]{3,2,1,0:T(8,128)S(1)} %get-tuple-element.22), channel_id=1, source_target_pairs={{1,0},{2,1},{3,2},{0,3},{5,4},{6,5},{7,6},{4,7},{9,8},{10,9},{11,1... | collective-permute-start | bytes 245768 | tf_op jit(solution)/shard_map/ppermute | solution.py:42
  26.4 1.6 %collective-permute-done.1.z_hi = f32[5,4,8,128]{3,2,1,0:T(8,128)S(1)} collective-permute-done((f32[5,4,8,128]{3,2,1,0:T(8,128)S(1)}, f32[5,4,8,128]{3,2,1,0:T(8,128)S(1)}, u32[]{:S(2)}, u32[]{:S(2)}) %collective-permute-start.1) | collective-permute-done | bytes 81952 | tf_op jit(solution)/shard_map/ppermute | solution.py:42
  28.1 0.0 collective-permute-done.2.y_lo
  28.1 0.0 collective-permute-done.3.y_hi
  28.1 0.0 collective-permute-done.4.x_lo
  28.1 0.0 copy-start.3
  28.1 3.4 %collective-permute-done.5.x_hi = f32[5,96,128]{2,1,0:T(8,128)S(1)} collective-permute-done((f32[5,96,128]{2,1,0:T(8,128)S(1)}, f32[5,96,128]{2,1,0:T(8,128)S(1)}, u32[]{:S(2)}, u32[]{:S(2)}) %collective-permute-start.5) | collective-permute-done | bytes 245792 | tf_op jit(solution)/shard_map/ppermute | solution.py:42
  31.6 0.0 copy-done.7
  31.6 0.7 copy-done.4
  32.3 25.9 %flow.1 = f32[5,512,128]{2,1,0:T(8,128)} custom-call(f32[5,512,128]{2,1,0:T(8,128)} %bitcast.56, f32[5,512,128]{2,1,0:T(8,128)} %bitcast.60, f32[5,4,8,128]{3,2,1,0:T(8,128)} %copy-done.7, f32[5,4,8,128]{3,2,1,0:T(8,128)} %copy-done.8, f32[5,48,128]{2,1,0:T(8,128)} %copy-done.5, f32[5,48,128]{2,1,0:T(8,128)} %copy-done.6, f32[5,96,128]{2,1,0:T(8,128)} %copy-done.3, ...), custom_call_target="tpu_custom_call" | custom-call | flops 100000000 | bytes 6000000 | tf_op jit(solution)/shard_map/flow/pallas_call | solution.py:253
  58.1 1.0 slice_bitcast_fusion.density
  59.1 10.6 %panels.1 = f32[4,2,128,256]{3,2,1,0:T(8,128)S(1)} custom-call(s32[1]{0:T(128)S(6)} %copy.63.live, f32[512,128]{1,0:T(8,128)S(1)} %slice_bitcast_fusion.density, bf16[4096,512]{1,0:T(8,128)(2,1)S(1)} %copy-done.1, s32[32,1,128]{2,1,0:T(1,128)S(1)} %bitcast.55, f32[32,16,128]{2,1,0:T(8,128)S(1)} %stack.48.geo, f32[32,1,1024]{2,1,0:T(1,128)S(1)} %sqrt_multiply_fusion.turns, ...), custom_call_target="tpu_custom_call" | custom-call | flops 4000000000 | bytes 8000000 | tf_op jit(solution)/shard_map/panels/pallas_call | solution.py:413
  69.7 16.0 %all_to_all.15 = f32[4,2,128,256]{3,2,1,0:T(8,128)S(1)} all-to-all(f32[4,2,128,256]{3,2,1,0:T(8,128)S(1)} %panels.1), channel_id=1, replica_groups=mesh['gx'=16,'gy'=4,'gz'=4] {'gz'}, dimensions={0} | all-to-all | bytes 2097152 | tf_op jit(solution)/shard_map/all_to_all | solution.py:23
  85.7 0.1 reduce_sum.58
  85.8 0.1 reshape_reshape.6
  85.9 51.3 %all_to_all.16 = f32[64,4,256]{2,1,0:T(4,128)S(1)} all-to-all(f32[64,4,256]{2,1,0:T(4,128)S(1)} %reshape_reshape.6), channel_id=1, replica_groups=mesh['gx'=16,'gy'=4,'gz'=4] {'gx','gy'}, dimensions={0} | all-to-all | bytes 524288 | tf_op jit(solution)/shard_map/all_to_all | solution.py:23
  137.2 0.1 reduce_sum.59
  137.4 17.8 %all_to_all.17 = f32[64,4,256]{2,1,0:T(4,128)S(1)} all-to-all(f32[64,4,256]{2,1,0:T(4,128)S(1)} %broadcast_in_dim.21), channel_id=1, replica_groups=mesh['gx'=16,'gy'=4,'gz'=4] {'gx','gy'}, dimensions={0} | all-to-all | bytes 524288 | tf_op jit(solution)/shard_map/all_to_all | solution.py:28
  155.1 0.1 reshape_reshape.7
  155.2 0.8 copy.59
  (31 shorter events, 0.3 us)
Async XLA Ops:
  3.3 2.6 %copy-start.2 = (f32[5,16,32,128]{3,2,1,0:T(8,128)S(1)}, f32[5,16,32,128]{3,2,1,0:T(8,128)}, u32[]{:S(2)}) copy-start(f32[5,16,32,128]{3,2,1,0:T(8,128)} %param.9) | copy-start | bytes 3932164
  3.6 15.9 %copy-start.9 = (f32[2,4096]{1,0:T(2,128)S(1)}, f32[2,4096]{1,0:T(2,128)}, u32[]{:S(2)}) copy-start(f32[2,4096]{1,0:T(2,128)} %param.12) | copy-start | bytes 98308
  3.7 16.9 %copy-start.10 = (f32[2,1024]{1,0:T(2,128)S(1)}, f32[2,1024]{1,0:T(2,128)}, u32[]{:S(2)}) copy-start(f32[2,1024]{1,0:T(2,128)} %param.14) | copy-start | bytes 24580
  3.7 17.1 %copy-start.11 = (f32[1024]{0:T(1024)S(1)}, f32[1024]{0:T(1024)}, u32[]{:S(2)}) copy-start(f32[1024]{0:T(1024)} %param.15) | copy-start | bytes 12292
  3.7 17.2 %copy-start = (s32[32,128]{1,0:T(8,128)S(1)}, s32[32,128]{1,0:T(8,128)}, u32[]{:S(2)}) copy-start(s32[32,128]{1,0:T(8,128)} %param.11) | copy-start | bytes 49156
  3.7 20.5 %collective-permute-start = (f32[5,4,8,128]{3,2,1,0:T(8,128)S(1)}, f32[5,4,8,128]{3,2,1,0:T(8,128)S(1)}, u32[]{:S(2)}, u32[]{:S(2)}) collective-permute-start(f32[5,4,8,128]{3,2,1,0:T(8,128)S(1)} %get-tuple-element.23), channel_id=1, source_target_pairs={{0,1},{1,2},{2,3},{3,0},{4,5},{5,6},{6,7},{7,4},{8,9},{9,10},{10,1... | collective-permute-start | bytes 245768 | tf_op jit(solution)/shard_map/ppermute | solution.py:42
  6.0 22.0 %collective-permute-start.2 = (f32[5,48,128]{2,1,0:T(8,128)S(1)}, f32[5,48,128]{2,1,0:T(8,128)S(1)}, u32[]{:S(2)}, u32[]{:S(2)}) collective-permute-start(f32[5,48,128]{2,1,0:T(8,128)S(1)} %reshape.265), channel_id=1, source_target_pairs={{0,4},{4,8},{8,12},{12,0},{1,5},{5,9},{9,13},{13,1},{2,6},{6,10},{... | collective-permute-start | bytes 368648 | tf_op jit(solution)/shard_map/ppermute | solution.py:42
  13.9 14.2 %collective-permute-start.3 = (f32[5,48,128]{2,1,0:T(8,128)S(1)}, f32[5,48,128]{2,1,0:T(8,128)S(1)}, u32[]{:S(2)}, u32[]{:S(2)}) collective-permute-start(f32[5,48,128]{2,1,0:T(8,128)S(1)} %reshape.266), channel_id=1, source_target_pairs={{4,0},{8,4},{12,8},{0,12},{5,1},{9,5},{13,9},{1,13},{6,2},{10,6},{... | collective-permute-start | bytes 368648 | tf_op jit(solution)/shard_map/ppermute | solution.py:42
  14.1 14.0 %collective-permute-start.4 = (f32[5,96,128]{2,1,0:T(8,128)S(1)}, f32[5,96,128]{2,1,0:T(8,128)S(1)}, u32[]{:S(2)}, u32[]{:S(2)}) collective-permute-start(f32[5,96,128]{2,1,0:T(8,128)S(1)} %get-tuple-element.17), channel_id=1, source_target_pairs={{0,16},{16,32},{32,48},{48,64},{64,80},{80,96},{96,112},{112,128},... | collective-permute-start | bytes 737288 | tf_op jit(solution)/shard_map/ppermute | solution.py:42
  14.9 16.7 %collective-permute-start.5 = (f32[5,96,128]{2,1,0:T(8,128)S(1)}, f32[5,96,128]{2,1,0:T(8,128)S(1)}, u32[]{:S(2)}, u32[]{:S(2)}) collective-permute-start(f32[5,96,128]{2,1,0:T(8,128)S(1)} %get-tuple-element.16), channel_id=1, source_target_pairs={{16,0},{32,16},{48,32},{64,48},{80,64},{96,80},{112,96},{128,112},... | collective-permute-start | bytes 737288 | tf_op jit(solution)/shard_map/ppermute | solution.py:42
  24.2 7.4 %copy-start.7 = (f32[5,4,8,128]{3,2,1,0:T(8,128)}, f32[5,4,8,128]{3,2,1,0:T(8,128)S(1)}, u32[]{:S(2)}) copy-start(f32[5,4,8,128]{3,2,1,0:T(8,128)S(1)} %collective-permute-done.z_lo) | copy-start | bytes 245764
  24.2 3.9 %collective-permute-start.1 = (f32[5,4,8,128]{3,2,1,0:T(8,128)S(1)}, f32[5,4,8,128]{3,2,1,0:T(8,128)S(1)}, u32[]{:S(2)}, u32[]{:S(2)}) collective-permute-start(f32[5,4,8,128]{3,2,1,0:T(8,128)S(1)} %get-tuple-element.22), channel_id=1, source_target_pairs={{1,0},{2,1},{3,2},{0,3},{5,4},{6,5},{7,6},{4,7},{9,8},{10,9},{11,1... | collective-permute-start | bytes 245768 | tf_op jit(solution)/shard_map/ppermute | solution.py:42
  28.1 3.5 %copy-start.8 = (f32[5,4,8,128]{3,2,1,0:T(8,128)}, f32[5,4,8,128]{3,2,1,0:T(8,128)S(1)}, u32[]{:S(2)}) copy-start(f32[5,4,8,128]{3,2,1,0:T(8,128)S(1)} %collective-permute-done.1.z_hi) | copy-start | bytes 245764
  28.1 3.5 %copy-start.5 = (f32[5,48,128]{2,1,0:T(8,128)}, f32[5,48,128]{2,1,0:T(8,128)S(1)}, u32[]{:S(2)}) copy-start(f32[5,48,128]{2,1,0:T(8,128)S(1)} %collective-permute-done.2.y_lo) | copy-start | bytes 368644
  28.1 3.5 %copy-start.6 = (f32[5,48,128]{2,1,0:T(8,128)}, f32[5,48,128]{2,1,0:T(8,128)S(1)}, u32[]{:S(2)}) copy-start(f32[5,48,128]{2,1,0:T(8,128)S(1)} %collective-permute-done.3.y_hi) | copy-start | bytes 368644
  28.1 3.5 %copy-start.3 = (f32[5,96,128]{2,1,0:T(8,128)}, f32[5,96,128]{2,1,0:T(8,128)S(1)}, u32[]{:S(2)}) copy-start(f32[5,96,128]{2,1,0:T(8,128)S(1)} %collective-permute-done.4.x_lo) | copy-start | bytes 737284
  31.6 0.7 copy-start.4
  32.3 26.8 %copy-start.1 = (bf16[4096,512]{1,0:T(8,128)(2,1)S(1)}, bf16[4096,512]{1,0:T(8,128)(2,1)}, u32[]{:S(2)}) copy-start(bf16[4096,512]{1,0:T(8,128)(2,1)} %record.1) | copy-start | bytes 12582916

commit v3 on v2

--- a/solution.py
+++ b/solution.py
@@ -91,18 +91,20 @@
     for group, length in streams:
 
         def step(k, carry):
-            after = []
-            for (r, start), (state, flux, speed) in zip(group, carry):
-                j, rows = start + k, pl.ds(8 * r, 8)
-                next_state = load(r, j + 1)
-                next_flux, next_speed = flux_of(next_state, axis_d)
-                for c in range(5):
-                    dq[c, j, rows, :] = next_state[c] - state[c]
-                    df[c, j, rows, :] = next_flux[c] - flux[c]
-                    fs[c, j, rows, :] = next_flux[c] + flux[c]
-                m2[j, rows, :] = jnp.maximum(next_speed, speed)
-                after.append((next_state, next_flux, next_speed))
-            return after
+            for u in range(3):
+                after = []
+                for (r, start), (state, flux, speed) in zip(group, carry):
+                    j, rows = start + 3 * k + u, pl.ds(8 * r, 8)
+                    next_state = load(r, j + 1)
+                    next_flux, next_speed = flux_of(next_state, axis_d)
+                    for c in range(5):
+                        dq[c, j, rows, :] = next_state[c] - state[c]
+                        df[c, j, rows, :] = next_flux[c] - flux[c]
+                        fs[c, j, rows, :] = next_flux[c] + flux[c]
+                    m2[j, rows, :] = jnp.maximum(next_speed, speed)
+                    after.append((next_state, next_flux, next_speed))
+                carry = after
+            return carry
 
         begin = []
         for r, start in group:
@@ -142,7 +144,7 @@
         return carry
 
     lax.fori_loop(0, 70, gather, 0, unroll=2)
-    sweep(planes, dq, df, fs, m2, faces, 2, 64, 1, [(((0, 0), (0, 23), (0, 46)), 23)])
+    sweep(planes, dq, df, fs, m2, faces, 2, 64, 1, [(((0, 0), (0, 33)), 12)])
 
     def difference(i, carry):
         for c in range(5):
@@ -175,7 +177,7 @@
         return carry
 
     lax.fori_loop(0, 32, gather, 0)
-    sweep(planes, dq, df, fs, m2, faces, 1, 32, 2, [(((0, 0), (1, 0)), 37)])
+    sweep(planes, dq, df, fs, m2, faces, 1, 32, 2, [(((0, 0), (1, 0)), 13)])
 
     def difference(i, carry):
         for c in range(5):
@@ -208,7 +210,7 @@
         return carry
 
     lax.fori_loop(0, 16, gather, 0)
-    streams = [(((0, 0), (1, 0)), 21), (((2, 0), (3, 0)), 21)]
+    streams = [(((0, 0), (1, 0)), 7), (((2, 0), (3, 0)), 7)]
     sweep(planes, dq, df, fs, m2, faces, 0, 16, 4, streams)
 
     def finish(i, carry):
@@ -229,12 +231,13 @@
 
 def sweep_scratch(cells, rows):
     f32 = jnp.float32
+    steps = -(-(cells + 5) // 3) * 3
     return [
-        pltpu.VMEM((5, cells + 6, rows, 128), f32),
-        pltpu.VMEM((5, cells + 5, rows, 128), f32),
-        pltpu.VMEM((5, cells + 5, rows, 128), f32),
-        pltpu.VMEM((5, cells + 5, rows, 128), f32),
-        pltpu.VMEM((cells + 5, rows, 128), f32),
+        pltpu.VMEM((5, steps + 1, rows, 128), f32),
+        pltpu.VMEM((5, steps, rows, 128), f32),
+        pltpu.VMEM((5, steps, rows, 128), f32),
+        pltpu.VMEM((5, steps, rows, 128), f32),
+        pltpu.VMEM((steps, rows, 128), f32),
         pltpu.VMEM((5, cells + 1, rows, 128), f32),
     ]
 
@@ -328,120 +331,136 @@
 PAIRS = ((0, 0), (0, 1), (1, 0), (0, 2), (1, 1), (2, 0))
 
 
+GROUP = 4
+GROUPS = 8
+PAIR = 2
+
+
 def panel_kernel(
-    live, density, record, cells, geo, turns, listeners, table, out, pieces, heard, spectra
+    live, updated, record, cells, geo, turns, listeners, table, out, density, records, pieces, heard, spectra, sems
 ):
-    b = pl.program_id(0)
-
-    def front():
-        cell = cells[0]
-        grid_row = lax.broadcasted_iota(jnp.int32, (512, 128), 0)
+    groups = (live[0] + GROUP - 1) // GROUP
+
+    def fetch(g):
+        return pltpu.make_async_copy(
+            record.at[pl.ds(128 * GROUP * g, 128 * GROUP)], records.at[g], sems.at[g]
+        )
+
+    first = pltpu.make_async_copy(updated.at[0], density, sems.at[GROUPS])
+    first.start()
+    for g in range(GROUPS):
+        pl.when(g < groups)(fetch(g).start)
+
+    out[...] = jnp.zeros_like(out)
+    split = in_pieces(listeners[...])
+    heard[...] = jnp.concatenate([split[t] for _, t in PAIRS], axis=0).astype(jnp.bfloat16)
+    first.wait()
+    turned = jnp.concatenate(
+        [jnp.transpose(density[pl.ds(128 * k, 128), :]) for k in range(4)], axis=1
+    )
+    for k, piece in enumerate(in_pieces(turned)):
+        pieces[pl.ds(128 * k, 128), :] = piece.astype(jnp.bfloat16)
+
+    def front(g, carry):
+        cell = cells[g]
+        grid_row = lax.broadcasted_iota(jnp.int32, (512, 128 * GROUP), 0)
         chosen = jnp.where(grid_row == cell // 128, 1.0, 0.0).astype(jnp.bfloat16)
         found = jnp.dot(pieces[...], chosen, preferred_element_type=jnp.float32)
         found = (found[:128] + found[128:256]) + found[256:]
-        lane = lax.broadcasted_iota(jnp.int32, (128, 128), 0)
+        lane = lax.broadcasted_iota(jnp.int32, (128, 128 * GROUP), 0)
         sampled = jnp.sum(jnp.where(lane == cell % 128, found, 0.0), axis=0, keepdims=True)
-        column = jnp.transpose(jnp.broadcast_to(sampled, (8, 128)))[:, 0:1]
-        sources = (record[...].astype(jnp.float32) * column).astype(jnp.bfloat16)
-        spectra[lax.rem(b, 2)] = lax.dot_general(
+        column = jnp.transpose(jnp.broadcast_to(sampled, (8, 128 * GROUP)))[:, 0:1]
+        fetch(g).wait()
+        sources = (records[g].astype(jnp.float32) * column).astype(jnp.bfloat16)
+        made = lax.dot_general(
             table[...], sources, (((1,), (1,)), ((), ())), preferred_element_type=jnp.float32
         ).astype(jnp.bfloat16)
-
-    def back():
-        spectrum = spectra[lax.rem(b + 1, 2)]
-        facing_pieces, apart_pieces = in_pieces(geo[0, 0:8]), in_pieces(geo[0, 8:16])
-        seen = jnp.concatenate(
-            [
-                jnp.concatenate([facing_pieces[s], apart_pieces[s]], axis=1)
-                for s, _ in PAIRS
-            ],
-            axis=0,
+        for k in range(GROUP):
+            spectra[GROUP * g + k] = made[:, 128 * k : 128 * (k + 1)]
+        return carry
+
+    lax.fori_loop(0, groups, front, 0)
+
+    order = (lax.broadcasted_iota(jnp.int32, (8, 128), 0) + 1).astype(jnp.float32)
+
+    def features(b, alive):
+        facing, apart = in_pieces(geo[b, 0:8] * alive), in_pieces(geo[b, 8:16])
+        return jnp.concatenate(
+            [jnp.concatenate([facing[s], apart[s]], axis=1) for s, _ in PAIRS], axis=0
         ).astype(jnp.bfloat16)
-        order = (lax.broadcasted_iota(jnp.int32, (8, 128), 0) + 1).astype(jnp.float32)
+
+    def weights_of(seen, o):
+        both = lax.dot_general(
+            seen,
+            heard[:, OBS_CHUNK * o : OBS_CHUNK * (o + 1)],
+            (((0,), (0,)), ((), ())),
+            preferred_element_type=jnp.float32,
+        )
+        return (both[:128] / both[128:]).astype(jnp.bfloat16)
+
+    def add_turned(b, o, product):
+        for h in range(OBS_CHUNK // 128):
+            lanes = slice(128 * h, 128 * h + 128)
+            base = turns[b, :, pl.ds(OBS_CHUNK * o + 128 * h, 128)]
+            sine, cosine = sin_cos(base * order)
+            step_s = jnp.broadcast_to(sine[7:8], (8, 128))
+            step_c = jnp.broadcast_to(cosine[7:8], (8, 128))
+            before_s = sine * step_c - cosine * step_s
+            before_c = cosine * step_c + sine * step_s
+            twice = step_c + step_c
+            for a in range(FREQS // 8):
+                re = product[8 * a : 8 * a + 8, lanes]
+                im = product[FREQS + 8 * a : FREQS + 8 * a + 8, lanes]
+                out[o, 0, pl.ds(8 * a, 8), lanes] += re * cosine + im * sine
+                out[o, 1, pl.ds(8 * a, 8), lanes] += im * cosine - re * sine
+                if a + 1 < FREQS // 8:
+                    sine, before_s = twice * sine - before_s, sine
+                    cosine, before_c = twice * cosine - before_c, cosine
+
+    def back(pair, carry):
+        blocks = []
+        for k in range(PAIR):
+            b = PAIR * pair + k
+            alive = jnp.where(b < live[0], 1.0, 0.0)
+            blocks.append((b, features(b, alive), spectra[b]))
         for o in range(1024 // OBS_CHUNK):
-            both = lax.dot_general(
-                seen,
-                heard[:, OBS_CHUNK * o : OBS_CHUNK * (o + 1)],
-                (((0,), (0,)), ((), ())),
-                preferred_element_type=jnp.float32,
-            )
-            weights = (both[:128] / both[128:]).astype(jnp.bfloat16)
-            product = jnp.dot(spectrum, weights, preferred_element_type=jnp.float32)
-            for h in range(OBS_CHUNK // 128):
-                lanes = slice(128 * h, 128 * h + 128)
-                base = turns[0, :, pl.ds(OBS_CHUNK * o + 128 * h, 128)]
-                sine, cosine = sin_cos(base * order)
-                step_s = jnp.broadcast_to(sine[7:8], (8, 128))
-                step_c = jnp.broadcast_to(cosine[7:8], (8, 128))
-                before_s = sine * step_c - cosine * step_s
-                before_c = cosine * step_c + sine * step_s
-                twice = step_c + step_c
-                for a in range(FREQS // 8):
-                    re = product[8 * a : 8 * a + 8, lanes]
-                    im = product[FREQS + 8 * a : FREQS + 8 * a + 8, lanes]
-                    out[o, 0, pl.ds(8 * a, 8), lanes] += re * cosine + im * sine
-                    out[o, 1, pl.ds(8 * a, 8), lanes] += im * cosine - re * sine
-                    if a + 1 < FREQS // 8:
-                        sine, before_s = twice * sine - before_s, sine
-                        cosine, before_c = twice * cosine - before_c, cosine
-
-    @pl.when(b == 0)
-    def _():
-        out[...] = jnp.zeros_like(out)
-        turned = jnp.concatenate(
-            [jnp.transpose(density[pl.ds(128 * k, 128), :]) for k in range(4)], axis=1
-        )
-        for k, piece in enumerate(in_pieces(turned)):
-            pieces[pl.ds(128 * k, 128), :] = piece.astype(jnp.bfloat16)
-        split = in_pieces(listeners[...])
-        heard[...] = jnp.concatenate([split[t] for _, t in PAIRS], axis=0).astype(jnp.bfloat16)
-        front()
-
-    @pl.when((b > 0) & (b <= live[0]))
-    def _():
-        front()
-        back()
-
-
-def panel_sums(live_count, density, record, cells, geo, turns, listeners, table):
-    def now(b, live):
-        return jnp.minimum(b, live[0] - 1)
-
-    def last(b, live):
-        return jnp.maximum(jnp.minimum(b, live[0]) - 1, 0)
-
+            for b, seen, spectrum in blocks:
+                product = jnp.dot(
+                    spectrum, weights_of(seen, o), preferred_element_type=jnp.float32
+                )
+                add_turned(b, o, product)
+        return carry
+
+    lax.fori_loop(0, (live[0] + PAIR - 1) // PAIR, back, 0)
+
+
+def panel_sums(live_count, updated, record, cells, geo, turns, listeners, table):
+    vmem = pl.BlockSpec(memory_space=pltpu.VMEM)
+    bf16 = jnp.bfloat16
     return pl.pallas_call(
         panel_kernel,
         out_shape=jax.ShapeDtypeStruct((1024 // OBS_CHUNK, 2, FREQS, OBS_CHUNK), jnp.float32),
-        grid_spec=pltpu.PrefetchScalarGridSpec(
-            num_scalar_prefetch=1,
-            grid=(33,),
-            in_specs=[
-                pl.BlockSpec((512, 128), lambda b, live: (0, 0)),
-                pl.BlockSpec((128, 512), lambda b, live: (now(b, live), 0)),
-                pl.BlockSpec((1, 1, 128), lambda b, live: (now(b, live), 0, 0)),
-                pl.BlockSpec((1, 16, 128), lambda b, live: (last(b, live), 0, 0)),
-                pl.BlockSpec((1, 1, 1024), lambda b, live: (last(b, live), 0, 0)),
-                pl.BlockSpec((8, 1024), lambda b, live: (0, 0)),
-                pl.BlockSpec((256, 512), lambda b, live: (0, 0)),
-            ],
-            out_specs=pl.BlockSpec(
-                (1024 // OBS_CHUNK, 2, FREQS, OBS_CHUNK), lambda b, live: (0, 0, 0, 0)
-            ),
-            scratch_shapes=[
-                pltpu.VMEM((384, 512), jnp.bfloat16),
-                pltpu.VMEM((8 * len(PAIRS), 1024), jnp.bfloat16),
-                pltpu.VMEM((2, 256, 128), jnp.bfloat16),
-            ],
-        ),
-        compiler_params=pltpu.CompilerParams(
-            dimension_semantics=("arbitrary",), vmem_limit_bytes=48 * 2**20
-        ),
+        in_specs=[
+            pl.BlockSpec(memory_space=pltpu.SMEM),
+            pl.BlockSpec(memory_space=pl.ANY),
+            pl.BlockSpec(memory_space=pl.ANY),
+        ]
+        + [vmem] * 5,
+        out_specs=vmem,
+        scratch_shapes=[
+            pltpu.VMEM((512, 128), jnp.float32),
+            pltpu.VMEM((GROUPS, 128 * GROUP, 512), bf16),
+            pltpu.VMEM((384, 512), bf16),
+            pltpu.VMEM((8 * len(PAIRS), 1024), bf16),
+            pltpu.VMEM((32, 256, 128), bf16),
+            pltpu.SemaphoreType.DMA((GROUPS + 1,)),
+        ],
+        compiler_params=pltpu.CompilerParams(vmem_limit_bytes=48 * 2**20),
         cost_estimate=pl.CostEstimate(
             flops=4_000_000_000, bytes_accessed=8_000_000, transcendentals=0
         ),
         name="panels",
-    )(live_count, density, record, cells, geo, turns, listeners, table)
+    )(live_count, updated, record, cells, geo, turns, listeners, table)
 
 
 def panel_geometry(panel_cell, panel_angles, listener_angles, listener_range, blocks, cells, counts):
@@ -494,9 +513,9 @@
     updated = flow_update(state_old, state_section, counts, step_size)
     partial = panel_sums(
         owned_blocks,
-        updated[0],
+        updated,
         panel_record,
-        panel_cell.reshape(32, 1, 128),
+        panel_cell.reshape(GROUPS, 1, 128 * GROUP),
         geo,
         turns,
         listeners,

time: 158 us -> 139 us (0.88)
  blocking collectives: 85.1 us -> 54.9 us
  Pallas kernels: 36.5 us -> 48.9 us
    all_to_all x2, blocking collectives: 67.3 us -> 37.1 us  [summed_on_arrival(): return jnp.sum(lax.all_to_all(blocks, axis, 0, 0, tiled=True), axis=0)]
    pallas_call x1, Pallas kernels: 10.6 us -> 24 us  [panel_sums(): pl.pallas_call(panel_kernel, out_shape=jax.ShapeDtypeStruct((1024 // OBS_...]
where the time goes in v3:
time: 139 us
  blocking collectives  54.9 us (39%)
  Pallas kernels  48.9 us (35%)
  starting transfers between devices  17.6 us (13%)
  local copies, waits for them, and re-layouts  6.39 us (5%)
  waiting for transfers between devices  5.27 us (4%)
  other arithmetic  3.95 us (3%)
  between operations  1.62 us (1%)
    all_to_all x2, blocking collectives, summed_on_arrival(): return jnp.sum(lax.all_to_all(blocks, axis, 0, 0, tiled=True), axis=0)  37.1 us
    pallas_call x1, Pallas kernels, flow_update(): pl.pallas_call(functools.partial(flow_kernel, coefs), out_shape=jax.Shape...  24.8 us
    pallas_call x1, Pallas kernels, panel_sums(): pl.pallas_call(panel_kernel, out_shape=jax.ShapeDtypeStruct((1024 // OBS_...  24 us
    all_to_all x1, blocking collectives, collect(): return lax.all_to_all(copies, axis, split_axis=0, concat_axis=0, tiled=True)  17.8 us
    ppermute x3, starting transfers between devices, edge_swap(): lax.ppermute(high_edge, axis, up)  10.8 us
    ppermute x3, starting transfers between devices, edge_swap(): lax.ppermute(low_edge, axis, down)  6.75 us
    ppermute x3, waiting for transfers between devices, edge_swap(): lax.ppermute(low_edge, axis, down)  5.26 us
    unnamed x25, local copies, waits for them, and re-layouts  2.87 us
  transfers between devices with their start and end apart: 6, of which 2 were waited for; matrix products, arithmetic and copies ran while one was open for 3% of the time, Pallas kernels for 0%

profile of v3, /device:TPU:1, one launch (start us, length us, event | category | flops | bytes accessed | tf_op | source)
XLA Modules:
  0.0 138.5 jit_solution(15842241430686346798)
XLA Ops:
  0.6 2.2 %fusion.40 = (f32[5,16,32,8]{3,2,1,0:T(8,128)S(1)}, f32[5,16,32,8]{3,2,1,0:T(8,128)S(1)}) fusion(f32[5,16,32,128]{3,2,1,0:T(8,128)} %param.9), kind=kLoop, calls=%fused_computation.79 | loop fusion | bytes 327680 | tf_op jit(solution)/shard_map/slice | solution.py:252
  2.9 0.4 pad_maximum_fusion
  3.3 0.0 copy-start.2
  3.3 0.4 copy.49
  3.7 0.0 copy-start.10
  3.7 0.0 copy-start.11
  3.7 0.0 copy-start.1
  3.7 2.2 %collective-permute-start = (f32[5,4,8,128]{3,2,1,0:T(8,128)S(1)}, f32[5,4,8,128]{3,2,1,0:T(8,128)S(1)}, u32[]{:S(2)}, u32[]{:S(2)}) collective-permute-start(f32[5,4,8,128]{3,2,1,0:T(8,128)S(1)} %get-tuple-element.23), channel_id=1, source_target_pairs={{0,1},{1,2},{2,3},{3,0},{4,5},{5,6},{6,7},{7,4},{8,9},{9,10},{10,1... | collective-permute-start | bytes 245768 | tf_op jit(solution)/shard_map/ppermute | solution.py:42
  5.9 0.1 fusion.39
  6.0 0.1 reshape.265
  6.0 7.8 %collective-permute-start.2 = (f32[5,48,128]{2,1,0:T(8,128)S(1)}, f32[5,48,128]{2,1,0:T(8,128)S(1)}, u32[]{:S(2)}, u32[]{:S(2)}) collective-permute-start(f32[5,48,128]{2,1,0:T(8,128)S(1)} %reshape.265), channel_id=1, source_target_pairs={{0,4},{4,8},{8,12},{12,0},{1,5},{5,9},{9,13},{13,1},{2,6},{6,10},{... | collective-permute-start | bytes 368648 | tf_op jit(solution)/shard_map/ppermute | solution.py:42
  13.9 0.1 reshape.266
  13.9 0.1 collective-permute-start.3
  14.1 0.8 collective-permute-start.4
  14.9 4.6 %collective-permute-start.5 = (f32[5,96,128]{2,1,0:T(8,128)S(1)}, f32[5,96,128]{2,1,0:T(8,128)S(1)}, u32[]{:S(2)}, u32[]{:S(2)}) collective-permute-start(f32[5,96,128]{2,1,0:T(8,128)S(1)} %get-tuple-element.16), channel_id=1, source_target_pairs={{16,0},{32,16},{48,32},{64,48},{80,64},{96,80},{112,96},{128,112},... | collective-permute-start | bytes 737288 | tf_op jit(solution)/shard_map/ppermute | solution.py:42
  19.5 0.0 copy-done.9
  19.5 1.0 cosine_multiply_fusion
  20.5 0.2 cosine_multiply_fusion.1
  20.8 0.0 copy-done.11
  20.9 0.1 fusion.36
  21.0 0.1 pad.5.clone
  21.1 0.1 pad.3.clone
  21.2 1.1 fusion.7
  22.3 0.1 fusion.34
  22.4 0.6 sqrt_multiply_fusion.turns
  23.1 0.1 maximum_maximum_fusion.listeners
  23.9 0.3 stack.48.geo
  24.2 0.0 collective-permute-done.z_lo
  24.2 2.0 %collective-permute-start.1 = (f32[5,4,8,128]{3,2,1,0:T(8,128)S(1)}, f32[5,4,8,128]{3,2,1,0:T(8,128)S(1)}, u32[]{:S(2)}, u32[]{:S(2)}) collective-permute-start(f32[5,4,8,128]{3,2,1,0:T(8,128)S(1)} %get-tuple-element.22), channel_id=1, source_target_pairs={{1,0},{2,1},{3,2},{0,3},{5,4},{6,5},{7,6},{4,7},{9,8},{10,9},{11,1... | collective-permute-start | bytes 245768 | tf_op jit(solution)/shard_map/ppermute | solution.py:42
  26.3 1.6 %collective-permute-done.1.z_hi = f32[5,4,8,128]{3,2,1,0:T(8,128)S(1)} collective-permute-done((f32[5,4,8,128]{3,2,1,0:T(8,128)S(1)}, f32[5,4,8,128]{3,2,1,0:T(8,128)S(1)}, u32[]{:S(2)}, u32[]{:S(2)}) %collective-permute-start.1) | collective-permute-done | bytes 81952 | tf_op jit(solution)/shard_map/ppermute | solution.py:42
  27.9 0.0 collective-permute-done.2.y_lo
  27.9 0.0 collective-permute-done.3.y_hi
  27.9 0.0 copy-start.6
  27.9 0.0 collective-permute-done.4.x_lo
  27.9 0.0 copy-start.3
  27.9 3.6 %collective-permute-done.5.x_hi = f32[5,96,128]{2,1,0:T(8,128)S(1)} collective-permute-done((f32[5,96,128]{2,1,0:T(8,128)S(1)}, f32[5,96,128]{2,1,0:T(8,128)S(1)}, u32[]{:S(2)}, u32[]{:S(2)}) %collective-permute-start.5) | collective-permute-done | bytes 245792 | tf_op jit(solution)/shard_map/ppermute | solution.py:42
  31.6 0.7 copy-done.4
  32.3 24.8 %flow.1.updated = f32[5,512,128]{2,1,0:T(8,128)} custom-call(f32[5,512,128]{2,1,0:T(8,128)} %bitcast.55, f32[5,512,128]{2,1,0:T(8,128)} %bitcast.58, f32[5,4,8,128]{3,2,1,0:T(8,128)} %copy-done.7, f32[5,4,8,128]{3,2,1,0:T(8,128)} %copy-done.8, f32[5,48,128]{2,1,0:T(8,128)} %copy-done.5, f32[5,48,128]{2,1,0:T(8,128)} %copy-done.6, f32[5,96,128]{2,1,0:T(8,128)} %copy-done.3, ...), custom_call_target="tpu_custom_call" | custom-call | flops 100000000 | bytes 6000000 | tf_op jit(solution)/shard_map/flow/pallas_call | solution.py:256
  57.1 1.3 copy-done
  58.4 24.0 %panels.1 = f32[4,2,128,256]{3,2,1,0:T(8,128)S(1)} custom-call(s32[1]{0:T(128)S(6)} %copy.63.live, f32[5,512,128]{2,1,0:T(8,128)S(1)} %copy-done, bf16[4096,512]{1,0:T(8,128)(2,1)} %record.1, s32[8,1,512]{2,1,0:T(1,128)S(1)} %bitcast.54, f32[32,16,128]{2,1,0:T(8,128)S(1)} %stack.48.geo, f32[32,1,1024]{2,1,0:T(1,128)S(1)} %sqrt_multiply_fusion.turns, ...), custom_call_target="tpu_custom_call" | custom-call | flops 4000000000 | bytes 8000000 | tf_op jit(solution)/shard_map/panels/pallas_call | solution.py:440
  82.4 12.2 %all_to_all.15 = f32[4,2,128,256]{3,2,1,0:T(8,128)S(1)} all-to-all(f32[4,2,128,256]{3,2,1,0:T(8,128)S(1)} %panels.1), channel_id=1, replica_groups=mesh['gx'=16,'gy'=4,'gz'=4] {'gz'}, dimensions={0} | all-to-all | bytes 2097152 | tf_op jit(solution)/shard_map/all_to_all | solution.py:23
  94.6 0.1 reduce_sum.58
  94.7 0.1 reshape_reshape.6
  94.8 24.9 %all_to_all.16 = f32[64,4,256]{2,1,0:T(4,128)S(1)} all-to-all(f32[64,4,256]{2,1,0:T(4,128)S(1)} %reshape_reshape.6), channel_id=1, replica_groups=mesh['gx'=16,'gy'=4,'gz'=4] {'gx','gy'}, dimensions={0} | all-to-all | bytes 524288 | tf_op jit(solution)/shard_map/all_to_all | solution.py:23
  119.7 0.1 reduce_sum.59
  119.8 17.8 %all_to_all.17 = f32[64,4,256]{2,1,0:T(4,128)S(1)} all-to-all(f32[64,4,256]{2,1,0:T(4,128)S(1)} %broadcast_in_dim.21), channel_id=1, replica_groups=mesh['gx'=16,'gy'=4,'gz'=4] {'gx','gy'}, dimensions={0} | all-to-all | bytes 524288 | tf_op jit(solution)/shard_map/all_to_all | solution.py:28
  137.6 0.1 reshape_reshape.7
  137.7 0.8 copy.59
  (30 shorter events, 0.3 us)
Async XLA Ops:
  3.3 2.6 %copy-start.2 = (f32[5,16,32,128]{3,2,1,0:T(8,128)S(1)}, f32[5,16,32,128]{3,2,1,0:T(8,128)}, u32[]{:S(2)}) copy-start(f32[5,16,32,128]{3,2,1,0:T(8,128)} %param.9) | copy-start | bytes 3932164
  3.6 15.9 %copy-start.9 = (f32[2,4096]{1,0:T(2,128)S(1)}, f32[2,4096]{1,0:T(2,128)}, u32[]{:S(2)}) copy-start(f32[2,4096]{1,0:T(2,128)} %param.12) | copy-start | bytes 98308
  3.7 16.9 %copy-start.10 = (f32[2,1024]{1,0:T(2,128)S(1)}, f32[2,1024]{1,0:T(2,128)}, u32[]{:S(2)}) copy-start(f32[2,1024]{1,0:T(2,128)} %param.14) | copy-start | bytes 24580
  3.7 17.1 %copy-start.11 = (f32[1024]{0:T(1024)S(1)}, f32[1024]{0:T(1024)}, u32[]{:S(2)}) copy-start(f32[1024]{0:T(1024)} %param.15) | copy-start | bytes 12292
  3.7 17.2 %copy-start.1 = (s32[32,128]{1,0:T(8,128)S(1)}, s32[32,128]{1,0:T(8,128)}, u32[]{:S(2)}) copy-start(s32[32,128]{1,0:T(8,128)} %param.11) | copy-start | bytes 49156
  3.7 20.5 %collective-permute-start = (f32[5,4,8,128]{3,2,1,0:T(8,128)S(1)}, f32[5,4,8,128]{3,2,1,0:T(8,128)S(1)}, u32[]{:S(2)}, u32[]{:S(2)}) collective-permute-start(f32[5,4,8,128]{3,2,1,0:T(8,128)S(1)} %get-tuple-element.23), channel_id=1, source_target_pairs={{0,1},{1,2},{2,3},{3,0},{4,5},{5,6},{6,7},{7,4},{8,9},{9,10},{10,1... | collective-permute-start | bytes 245768 | tf_op jit(solution)/shard_map/ppermute | solution.py:42
  6.0 21.9 %collective-permute-start.2 = (f32[5,48,128]{2,1,0:T(8,128)S(1)}, f32[5,48,128]{2,1,0:T(8,128)S(1)}, u32[]{:S(2)}, u32[]{:S(2)}) collective-permute-start(f32[5,48,128]{2,1,0:T(8,128)S(1)} %reshape.265), channel_id=1, source_target_pairs={{0,4},{4,8},{8,12},{12,0},{1,5},{5,9},{9,13},{13,1},{2,6},{6,10},{... | collective-permute-start | bytes 368648 | tf_op jit(solution)/shard_map/ppermute | solution.py:42
  13.9 14.0 %collective-permute-start.3 = (f32[5,48,128]{2,1,0:T(8,128)S(1)}, f32[5,48,128]{2,1,0:T(8,128)S(1)}, u32[]{:S(2)}, u32[]{:S(2)}) collective-permute-start(f32[5,48,128]{2,1,0:T(8,128)S(1)} %reshape.266), channel_id=1, source_target_pairs={{4,0},{8,4},{12,8},{0,12},{5,1},{9,5},{13,9},{1,13},{6,2},{10,6},{... | collective-permute-start | bytes 368648 | tf_op jit(solution)/shard_map/ppermute | solution.py:42
  14.1 13.9 %collective-permute-start.4 = (f32[5,96,128]{2,1,0:T(8,128)S(1)}, f32[5,96,128]{2,1,0:T(8,128)S(1)}, u32[]{:S(2)}, u32[]{:S(2)}) collective-permute-start(f32[5,96,128]{2,1,0:T(8,128)S(1)} %get-tuple-element.17), channel_id=1, source_target_pairs={{0,16},{16,32},{32,48},{48,64},{64,80},{80,96},{96,112},{112,128},... | collective-permute-start | bytes 737288 | tf_op jit(solution)/shard_map/ppermute | solution.py:42
  14.9 16.7 %collective-permute-start.5 = (f32[5,96,128]{2,1,0:T(8,128)S(1)}, f32[5,96,128]{2,1,0:T(8,128)S(1)}, u32[]{:S(2)}, u32[]{:S(2)}) collective-permute-start(f32[5,96,128]{2,1,0:T(8,128)S(1)} %get-tuple-element.16), channel_id=1, source_target_pairs={{16,0},{32,16},{48,32},{64,48},{80,64},{96,80},{112,96},{128,112},... | collective-permute-start | bytes 737288 | tf_op jit(solution)/shard_map/ppermute | solution.py:42
  24.2 7.4 %copy-start.7 = (f32[5,4,8,128]{3,2,1,0:T(8,128)}, f32[5,4,8,128]{3,2,1,0:T(8,128)S(1)}, u32[]{:S(2)}) copy-start(f32[5,4,8,128]{3,2,1,0:T(8,128)S(1)} %collective-permute-done.z_lo) | copy-start | bytes 245764
  24.2 3.7 %collective-permute-start.1 = (f32[5,4,8,128]{3,2,1,0:T(8,128)S(1)}, f32[5,4,8,128]{3,2,1,0:T(8,128)S(1)}, u32[]{:S(2)}, u32[]{:S(2)}) collective-permute-start(f32[5,4,8,128]{3,2,1,0:T(8,128)S(1)} %get-tuple-element.22), channel_id=1, source_target_pairs={{1,0},{2,1},{3,2},{0,3},{5,4},{6,5},{7,6},{4,7},{9,8},{10,9},{11,1... | collective-permute-start | bytes 245768 | tf_op jit(solution)/shard_map/ppermute | solution.py:42
  27.9 3.7 %copy-start.8 = (f32[5,4,8,128]{3,2,1,0:T(8,128)}, f32[5,4,8,128]{3,2,1,0:T(8,128)S(1)}, u32[]{:S(2)}) copy-start(f32[5,4,8,128]{3,2,1,0:T(8,128)S(1)} %collective-permute-done.1.z_hi) | copy-start | bytes 245764
  27.9 3.7 %copy-start.5 = (f32[5,48,128]{2,1,0:T(8,128)}, f32[5,48,128]{2,1,0:T(8,128)S(1)}, u32[]{:S(2)}) copy-start(f32[5,48,128]{2,1,0:T(8,128)S(1)} %collective-permute-done.2.y_lo) | copy-start | bytes 368644
  27.9 3.7 %copy-start.6 = (f32[5,48,128]{2,1,0:T(8,128)}, f32[5,48,128]{2,1,0:T(8,128)S(1)}, u32[]{:S(2)}) copy-start(f32[5,48,128]{2,1,0:T(8,128)S(1)} %collective-permute-done.3.y_hi) | copy-start | bytes 368644
  27.9 3.7 %copy-start.3 = (f32[5,96,128]{2,1,0:T(8,128)}, f32[5,96,128]{2,1,0:T(8,128)S(1)}, u32[]{:S(2)}) copy-start(f32[5,96,128]{2,1,0:T(8,128)S(1)} %collective-permute-done.4.x_lo) | copy-start | bytes 737284
  31.6 0.7 copy-start.4
  57.1 1.3 copy-start

commit v4 on v3

--- a/solution.py
+++ b/solution.py
@@ -19,20 +19,132 @@
 EPS = 0.75 * 4.0 * SCALE * SCALE * WENO_EPS
 
 
-def summed_on_arrival(blocks, axis):
-    return jnp.sum(lax.all_to_all(blocks, axis, 0, 0, tiled=True), axis=0)
-
-
-def collect(shard, axis):
-    copies = jnp.broadcast_to(shard, (lax.axis_size(axis), *shard.shape))
-    return lax.all_to_all(copies, axis, split_axis=0, concat_axis=0, tiled=True)
-
-
-def sum_by_parts(shard, axes):
-    size = lax.axis_size(axes)
-    lines = shard.reshape(size, -1, shard.shape[-1])
-    own = summed_on_arrival(lines, axes)
-    return collect(own, axes).reshape(shard.shape)
+MESH = pl.DeviceIdType.MESH
+TILES = 32
+
+
+def sum_kernel(part, out, came0, sums, came1, total, came2, mine, full, other, s0, r0, s1, r1, s2, r2, s3, r3, s4, r4):
+    gx, gy, gz = (lax.axis_index(a) for a in ("gx", "gy", "gz"))
+    core, upper = lax.rem(gy, 2), gy // 2
+    m = gx * 2 + upper
+    partner = {"gx": gx, "gy": upper * 2 + (1 - core), "gz": gz}
+
+    def along(k):
+        return {"gx": gx, "gy": gy, "gz": lax.rem(gz + k, 4)}
+
+    def chip(r):
+        t = lax.rem(m + r, TILES)
+        return t, {"gx": t // 2, "gy": lax.rem(t, 2) * 2 + core, "gz": gz}
+
+    barrier = pltpu.get_barrier_semaphore()
+
+    def greet(device):
+        pl.semaphore_signal(barrier, inc=1, device_id=device, device_id_type=MESH)
+
+    greet(partner)
+    for k in (1, 2, 3):
+        greet(along(k))
+
+    def greet_chip(r, carry):
+        greet(chip(r)[1])
+        return carry
+
+    lax.fori_loop(1, TILES, greet_chip, 0)
+    pl.semaphore_wait(barrier, TILES + 3)
+
+    def remote(src, dst, send, recv, device):
+        return pltpu.make_async_remote_copy(
+            src_ref=src, dst_ref=dst, send_sem=send, recv_sem=recv, device_id=device, device_id_type=MESH
+        )
+
+    shares, along_gz = {}, {}
+    for k in (2, 1, 3, 0):
+        shares[k] = remote(
+            part.at[lax.rem(gz + k, 4), 1 - core], came0.at[k], s0.at[k], r0.at[k], partner
+        )
+        shares[k].start()
+    for k in (2, 1, 3, 0):
+        shares[k].wait_recv()
+        sums[k] = part[lax.rem(gz + k, 4), core] + came0[k]
+        if k > 0:
+            along_gz[k] = remote(sums.at[k], came1.at[k - 1], s1.at[k - 1], r1.at[k - 1], along(k))
+            along_gz[k].start()
+    for k in (1, 3, 2):
+        along_gz[k].wait_recv()
+    total[...] = (sums[0] + came1[0]) + (came1[1] + came1[2])
+
+    def scatter(r, carry):
+        t, device = chip(r)
+        remote(total.at[t], came2.at[r - 1], s2, r2, device).start()
+        return carry
+
+    lax.fori_loop(1, TILES, scatter, 0)
+    pltpu.make_async_copy(came2, came2, r2).wait()
+    own = total[m]
+    for r in range(TILES - 1):
+        own = own + came2[r]
+    mine[...] = own
+    full[m] = own
+
+    def gather(r, carry):
+        remote(mine, full.at[m], s3, r3, chip(r)[1]).start()
+        return carry
+
+    lax.fori_loop(1, TILES, gather, 0)
+    pltpu.make_async_copy(came2, came2, r3).wait()
+    swap = remote(full, other, s4, r4, partner)
+    swap.start()
+
+    def lay(which, tiles):
+        for h in range(2):
+            block = jnp.concatenate([tiles[2 * a + h] for a in range(16)], axis=0)
+            out[which, pl.ds(128 * h, 128), :] = jnp.transpose(block)
+
+    lay(core, full)
+    swap.wait_recv()
+    lay(1 - core, other)
+    for k in (0, 1, 2, 3):
+        shares[k].wait_send()
+        if k > 0:
+            along_gz[k].wait_send()
+    pltpu.make_async_copy(came2, came2, s2).wait()
+    pltpu.make_async_copy(came2, came2, s3).wait()
+    swap.wait_send()
+
+
+def summed_spectra(part):
+    vmem = pl.BlockSpec(memory_space=pltpu.VMEM)
+    f32 = jnp.float32
+    tiles = (TILES, 8, 128)
+    dma = pltpu.SemaphoreType.DMA
+    return pl.pallas_call(
+        sum_kernel,
+        out_shape=jax.ShapeDtypeStruct((2, 256, FREQS), f32),
+        in_specs=[vmem],
+        out_specs=vmem,
+        scratch_shapes=[
+            pltpu.VMEM((4, *tiles), f32),
+            pltpu.VMEM((4, *tiles), f32),
+            pltpu.VMEM((3, *tiles), f32),
+            pltpu.VMEM(tiles, f32),
+            pltpu.VMEM((TILES - 1, 8, 128), f32),
+            pltpu.VMEM((8, 128), f32),
+            pltpu.VMEM(tiles, f32),
+            pltpu.VMEM(tiles, f32),
+            dma((4,)),
+            dma((4,)),
+            dma((3,)),
+            dma((3,)),
+            dma,
+            dma,
+            dma,
+            dma,
+            dma,
+            dma,
+        ],
+        compiler_params=pltpu.CompilerParams(collective_id=1, has_side_effects=True),
+        name="sum_spectra",
+    )(part)
 
 
 def edge_swap(low_edge, high_edge, axis):
@@ -411,8 +523,8 @@
             for a in range(FREQS // 8):
                 re = product[8 * a : 8 * a + 8, lanes]
                 im = product[FREQS + 8 * a : FREQS + 8 * a + 8, lanes]
-                out[o, 0, pl.ds(8 * a, 8), lanes] += re * cosine + im * sine
-                out[o, 1, pl.ds(8 * a, 8), lanes] += im * cosine - re * sine
+                out[o, 0, 2 * a + h] += re * cosine + im * sine
+                out[o, 1, 2 * a + h] += im * cosine - re * sine
                 if a + 1 < FREQS // 8:
                     sine, before_s = twice * sine - before_s, sine
                     cosine, before_c = twice * cosine - before_c, cosine
@@ -439,7 +551,7 @@
     bf16 = jnp.bfloat16
     return pl.pallas_call(
         panel_kernel,
-        out_shape=jax.ShapeDtypeStruct((1024 // OBS_CHUNK, 2, FREQS, OBS_CHUNK), jnp.float32),
+        out_shape=jax.ShapeDtypeStruct((1024 // OBS_CHUNK, 2, 32, 8, 128), jnp.float32),
         in_specs=[
             pl.BlockSpec(memory_space=pltpu.SMEM),
             pl.BlockSpec(memory_space=pl.ANY),
@@ -521,9 +633,7 @@
         listeners,
         dft_table(panel_record.shape[1], FREQS),
     )
-    gz_share = summed_on_arrival(partial, "gz")
-    spectra_out = sum_by_parts(gz_share.reshape(2 * FREQS, OBS_CHUNK), ("gx", "gy"))
-    return updated.reshape(state_section.shape), jnp.transpose(spectra_out.reshape(2, FREQS, OBS_CHUNK), (0, 2, 1))
+    return updated.reshape(state_section.shape), summed_spectra(partial)
 
 
 def solution(mesh):

time: 139 us -> 116 us (0.83)
  blocking collectives: 54.9 us -> 0 us
  Pallas kernels: 48.9 us -> 78.5 us
  local copies, waits for them, and re-layouts: 6.39 us -> 7.99 us
    all_to_all x3 -> x0, blocking collectives: 54.9 us -> none  [the longest x2 37.1 us: summed_on_arrival(): return jnp.sum(lax.all_to_all(blocks, axis, 0, 0, tiled=True), axis=0)]
    pallas_call x0 -> x1, Pallas kernels: none -> 48.2 us  [summed_spectra(): pl.pallas_call(sum_kernel, out_shape=jax.ShapeDtypeStruct((2, 256, FREQS)...]
    pallas_call x1, Pallas kernels: 24 us -> 5.44 us  [panel_sums(): pl.pallas_call(panel_kernel, out_shape=jax.ShapeDtypeStruct((1024 // OBS_...]
    unnamed x25 -> x27, local copies, waits for them, and re-layouts: 2.87 us -> 4.67 us
  transfers between devices with their start and end apart: 6 -> 6, of which waited for: 2 -> 2; matrix products, arithmetic and copies ran while one was open for 3% -> 4% of each run, Pallas kernels for 0% -> 0%
where the time goes in v4:
time: 116 us; the launch traced here: 115 us
  Pallas kernels  78.5 us (68%)
  starting transfers between devices  17.6 us (15%)
  local copies, waits for them, and re-layouts  7.99 us (7%)
  waiting for transfers between devices  5.27 us (5%)
  other arithmetic  3.78 us (3%)
  between operations  1.62 us (1%)
    pallas_call x1, Pallas kernels, summed_spectra(): pl.pallas_call(sum_kernel, out_shape=jax.ShapeDtypeStruct((2, 256, FREQS)...  48.2 us
    pallas_call x1, Pallas kernels, flow_update(): pl.pallas_call(functools.partial(flow_kernel, coefs), out_shape=jax.Shape...  24.8 us
    ppermute x3, starting transfers between devices, edge_swap(): lax.ppermute(high_edge, axis, up)  10.8 us
    ppermute x3, starting transfers between devices, edge_swap(): lax.ppermute(low_edge, axis, down)  6.75 us
    pallas_call x1, Pallas kernels, panel_sums(): pl.pallas_call(panel_kernel, out_shape=jax.ShapeDtypeStruct((1024 // OBS_...  5.44 us
    ppermute x3, waiting for transfers between devices, edge_swap(): lax.ppermute(low_edge, axis, down)  5.26 us
    unnamed x27, local copies, waits for them, and re-layouts  4.67 us
  transfers between devices with their start and end apart: 6, of which 2 were waited for; matrix products, arithmetic and copies ran while one was open for 4% of the time, Pallas kernels for 0%

profile of v4, /device:TPU:1, one launch (start us, length us, event | category | flops | bytes accessed | tf_op | source)
XLA Modules:
  0.0 114.7 jit_solution(14979681617283577461)
XLA Ops:
  0.6 2.2 %fusion.40 = (f32[5,16,32,8]{3,2,1,0:T(8,128)S(1)}, f32[5,16,32,8]{3,2,1,0:T(8,128)S(1)}) fusion(f32[5,16,32,128]{3,2,1,0:T(8,128)} %param.9), kind=kLoop, calls=%fused_computation.79 | loop fusion | bytes 327680 | tf_op jit(solution)/shard_map/slice | solution.py:364
  2.9 0.4 pad_maximum_fusion
  3.3 0.0 copy-start.3
  3.3 0.4 copy.27
  3.7 0.0 copy-start.11
  3.7 0.0 copy-start.12
  3.7 0.0 copy-start.2
  3.7 2.2 %collective-permute-start = (f32[5,4,8,128]{3,2,1,0:T(8,128)S(1)}, f32[5,4,8,128]{3,2,1,0:T(8,128)S(1)}, u32[]{:S(2)}, u32[]{:S(2)}) collective-permute-start(f32[5,4,8,128]{3,2,1,0:T(8,128)S(1)} %get-tuple-element.15), channel_id=1, source_target_pairs={{0,1},{1,2},{2,3},{3,0},{4,5},{5,6},{6,7},{7,4},{8,9},{9,10},{10,1... | collective-permute-start | bytes 245768 | tf_op jit(solution)/shard_map/ppermute | solution.py:154
  5.9 0.0 copy-done.3
  5.9 0.1 fusion.39
  6.0 0.1 reshape.265
  6.0 7.8 %collective-permute-start.2 = (f32[5,48,128]{2,1,0:T(8,128)S(1)}, f32[5,48,128]{2,1,0:T(8,128)S(1)}, u32[]{:S(2)}, u32[]{:S(2)}) collective-permute-start(f32[5,48,128]{2,1,0:T(8,128)S(1)} %reshape.265), channel_id=1, source_target_pairs={{0,4},{4,8},{8,12},{12,0},{1,5},{5,9},{9,13},{13,1},{2,6},{6,10},{... | collective-permute-start | bytes 368648 | tf_op jit(solution)/shard_map/ppermute | solution.py:154
  13.9 0.1 reshape.266
  13.9 0.1 collective-permute-start.3
  14.1 0.8 collective-permute-start.4
  14.9 4.6 %collective-permute-start.5 = (f32[5,96,128]{2,1,0:T(8,128)S(1)}, f32[5,96,128]{2,1,0:T(8,128)S(1)}, u32[]{:S(2)}, u32[]{:S(2)}) collective-permute-start(f32[5,96,128]{2,1,0:T(8,128)S(1)} %get-tuple-element.8), channel_id=1, source_target_pairs={{16,0},{32,16},{48,32},{64,48},{80,64},{96,80},{112,96},{128,112},... | collective-permute-start | bytes 737288 | tf_op jit(solution)/shard_map/ppermute | solution.py:154
  19.5 0.0 copy-done.10
  19.5 1.0 cosine_multiply_fusion
  20.5 0.0 copy-done.11
  20.5 0.2 cosine_multiply_fusion.1
  20.8 0.0 copy-done.12
  20.9 0.0 copy-done.2
  20.9 0.1 fusion.36
  21.0 0.1 pad.5.clone
  21.1 0.1 pad.3.clone
  21.2 1.1 fusion.7
  22.3 0.1 fusion.34
  22.4 0.6 sqrt_multiply_fusion.turns
  23.1 0.1 maximum_maximum_fusion.listeners
  23.9 0.3 stack.48.geo
  24.2 0.0 collective-permute-done.z_lo
  24.2 0.0 copy-start.8
  24.2 2.0 %collective-permute-start.1 = (f32[5,4,8,128]{3,2,1,0:T(8,128)S(1)}, f32[5,4,8,128]{3,2,1,0:T(8,128)S(1)}, u32[]{:S(2)}, u32[]{:S(2)}) collective-permute-start(f32[5,4,8,128]{3,2,1,0:T(8,128)S(1)} %get-tuple-element.14), channel_id=1, source_target_pairs={{1,0},{2,1},{3,2},{0,3},{5,4},{6,5},{7,6},{4,7},{9,8},{10,9},{11,1... | collective-permute-start | bytes 245768 | tf_op jit(solution)/shard_map/ppermute | solution.py:154
  26.3 1.6 %collective-permute-done.1.z_hi = f32[5,4,8,128]{3,2,1,0:T(8,128)S(1)} collective-permute-done((f32[5,4,8,128]{3,2,1,0:T(8,128)S(1)}, f32[5,4,8,128]{3,2,1,0:T(8,128)S(1)}, u32[]{:S(2)}, u32[]{:S(2)}) %collective-permute-start.1) | collective-permute-done | bytes 81952 | tf_op jit(solution)/shard_map/ppermute | solution.py:154
  27.9 0.0 collective-permute-done.2.y_lo
  27.9 0.0 collective-permute-done.3.y_hi
  27.9 0.0 copy-start.7
  27.9 0.0 collective-permute-done.4.x_lo
  27.9 0.0 copy-start.4
  27.9 3.6 %collective-permute-done.5.x_hi = f32[5,96,128]{2,1,0:T(8,128)S(1)} collective-permute-done((f32[5,96,128]{2,1,0:T(8,128)S(1)}, f32[5,96,128]{2,1,0:T(8,128)S(1)}, u32[]{:S(2)}, u32[]{:S(2)}) %collective-permute-start.5) | collective-permute-done | bytes 245792 | tf_op jit(solution)/shard_map/ppermute | solution.py:154
  31.6 0.6 copy-done.5
  32.2 24.8 %flow.1.updated = f32[5,512,128]{2,1,0:T(8,128)} custom-call(f32[5,512,128]{2,1,0:T(8,128)} %bitcast.54, f32[5,512,128]{2,1,0:T(8,128)} %bitcast.57, f32[5,4,8,128]{3,2,1,0:T(8,128)} %copy-done.8, f32[5,4,8,128]{3,2,1,0:T(8,128)} %copy-done.9, f32[5,48,128]{2,1,0:T(8,128)} %copy-done.6, f32[5,48,128]{2,1,0:T(8,128)} %copy-done.7, f32[5,96,128]{2,1,0:T(8,128)} %copy-done.4, ...), custom_call_target="tpu_custom_call" | custom-call | flops 100000000 | bytes 6000000 | tf_op jit(solution)/shard_map/flow/pallas_call | solution.py:368
  57.1 1.3 %copy-done = f32[5,512,128]{2,1,0:T(8,128)S(1)} copy-done((f32[5,512,128]{2,1,0:T(8,128)S(1)}, f32[5,512,128]{2,1,0:T(8,128)}, u32[]{:S(2)}) %copy-start) | copy-done | bytes 1310744
  58.4 5.4 %panels.1.part = f32[4,2,32,8,128]{4,3,2,1,0:T(8,128)S(1)} custom-call(s32[1]{0:T(128)S(6)} %copy.39.live, f32[5,512,128]{2,1,0:T(8,128)S(1)} %copy-done, bf16[4096,512]{1,0:T(8,128)(2,1)} %record.1, s32[8,1,512]{2,1,0:T(1,128)S(1)} %bitcast.53, f32[32,16,128]{2,1,0:T(8,128)S(1)} %stack.48.geo, f32[32,1,1024]{2,1,0:T(1,128)S(1)} %sqrt_multiply_fusion.turns, ...), custom_call_target="tpu_custom_call" | custom-call | flops 4000000000 | bytes 8000000 | tf_op jit(solution)/shard_map/panels/pallas_call | solution.py:552
  63.8 0.0 copy-start.1
  63.8 1.0 copy-done.1
  64.8 48.2 %sum_spectra.1 = f32[2,256,128]{2,1,0:T(8,128)} custom-call(f32[4,2,32,8,128]{4,3,2,1,0:T(8,128)} %copy-done.1), custom_call_target="tpu_custom_call" | custom-call | tf_op jit(solution)/shard_map/sum_spectra/pallas_call | solution.py:120
  113.0 1.7 %copy.40 = f32[2,256,128]{2,1,0:T(8,128)} copy(f32[2,256,128]{2,1,0:T(8,128)} %sum_spectra.1) | data formatting | bytes 524288
  (25 shorter events, 0.2 us)
Async XLA Ops:
  3.3 2.6 %copy-start.3 = (f32[5,16,32,128]{3,2,1,0:T(8,128)S(1)}, f32[5,16,32,128]{3,2,1,0:T(8,128)}, u32[]{:S(2)}) copy-start(f32[5,16,32,128]{3,2,1,0:T(8,128)} %param.9) | copy-start | bytes 3932164
  3.6 15.9 %copy-start.10 = (f32[2,4096]{1,0:T(2,128)S(1)}, f32[2,4096]{1,0:T(2,128)}, u32[]{:S(2)}) copy-start(f32[2,4096]{1,0:T(2,128)} %param.12) | copy-start | bytes 98308
  3.7 16.9 %copy-start.11 = (f32[2,1024]{1,0:T(2,128)S(1)}, f32[2,1024]{1,0:T(2,128)}, u32[]{:S(2)}) copy-start(f32[2,1024]{1,0:T(2,128)} %param.14) | copy-start | bytes 24580
  3.7 17.1 %copy-start.12 = (f32[1024]{0:T(1024)S(1)}, f32[1024]{0:T(1024)}, u32[]{:S(2)}) copy-start(f32[1024]{0:T(1024)} %param.15) | copy-start | bytes 12292
  3.7 17.2 %copy-start.2 = (s32[32,128]{1,0:T(8,128)S(1)}, s32[32,128]{1,0:T(8,128)}, u32[]{:S(2)}) copy-start(s32[32,128]{1,0:T(8,128)} %param.11) | copy-start | bytes 49156
  3.7 20.5 %collective-permute-start = (f32[5,4,8,128]{3,2,1,0:T(8,128)S(1)}, f32[5,4,8,128]{3,2,1,0:T(8,128)S(1)}, u32[]{:S(2)}, u32[]{:S(2)}) collective-permute-start(f32[5,4,8,128]{3,2,1,0:T(8,128)S(1)} %get-tuple-element.15), channel_id=1, source_target_pairs={{0,1},{1,2},{2,3},{3,0},{4,5},{5,6},{6,7},{7,4},{8,9},{9,10},{10,1... | collective-permute-start | bytes 245768 | tf_op jit(solution)/shard_map/ppermute | solution.py:154
  6.0 21.9 %collective-permute-start.2 = (f32[5,48,128]{2,1,0:T(8,128)S(1)}, f32[5,48,128]{2,1,0:T(8,128)S(1)}, u32[]{:S(2)}, u32[]{:S(2)}) collective-permute-start(f32[5,48,128]{2,1,0:T(8,128)S(1)} %reshape.265), channel_id=1, source_target_pairs={{0,4},{4,8},{8,12},{12,0},{1,5},{5,9},{9,13},{13,1},{2,6},{6,10},{... | collective-permute-start | bytes 368648 | tf_op jit(solution)/shard_map/ppermute | solution.py:154
  13.9 14.0 %collective-permute-start.3 = (f32[5,48,128]{2,1,0:T(8,128)S(1)}, f32[5,48,128]{2,1,0:T(8,128)S(1)}, u32[]{:S(2)}, u32[]{:S(2)}) collective-permute-start(f32[5,48,128]{2,1,0:T(8,128)S(1)} %reshape.266), channel_id=1, source_target_pairs={{4,0},{8,4},{12,8},{0,12},{5,1},{9,5},{13,9},{1,13},{6,2},{10,6},{... | collective-permute-start | bytes 368648 | tf_op jit(solution)/shard_map/ppermute | solution.py:154
  14.1 13.9 %collective-permute-start.4 = (f32[5,96,128]{2,1,0:T(8,128)S(1)}, f32[5,96,128]{2,1,0:T(8,128)S(1)}, u32[]{:S(2)}, u32[]{:S(2)}) collective-permute-start(f32[5,96,128]{2,1,0:T(8,128)S(1)} %get-tuple-element.9), channel_id=1, source_target_pairs={{0,16},{16,32},{32,48},{48,64},{64,80},{80,96},{96,112},{112,128},... | collective-permute-start | bytes 737288 | tf_op jit(solution)/shard_map/ppermute | solution.py:154
  14.9 16.7 %collective-permute-start.5 = (f32[5,96,128]{2,1,0:T(8,128)S(1)}, f32[5,96,128]{2,1,0:T(8,128)S(1)}, u32[]{:S(2)}, u32[]{:S(2)}) collective-permute-start(f32[5,96,128]{2,1,0:T(8,128)S(1)} %get-tuple-element.8), channel_id=1, source_target_pairs={{16,0},{32,16},{48,32},{64,48},{80,64},{96,80},{112,96},{128,112},... | collective-permute-start | bytes 737288 | tf_op jit(solution)/shard_map/ppermute | solution.py:154
  24.2 7.4 %copy-start.8 = (f32[5,4,8,128]{3,2,1,0:T(8,128)}, f32[5,4,8,128]{3,2,1,0:T(8,128)S(1)}, u32[]{:S(2)}) copy-start(f32[5,4,8,128]{3,2,1,0:T(8,128)S(1)} %collective-permute-done.z_lo) | copy-start | bytes 245764
  24.2 3.7 %collective-permute-start.1 = (f32[5,4,8,128]{3,2,1,0:T(8,128)S(1)}, f32[5,4,8,128]{3,2,1,0:T(8,128)S(1)}, u32[]{:S(2)}, u32[]{:S(2)}) collective-permute-start(f32[5,4,8,128]{3,2,1,0:T(8,128)S(1)} %get-tuple-element.14), channel_id=1, source_target_pairs={{1,0},{2,1},{3,2},{0,3},{5,4},{6,5},{7,6},{4,7},{9,8},{10,9},{11,1... | collective-permute-start | bytes 245768 | tf_op jit(solution)/shard_map/ppermute | solution.py:154
  27.9 3.7 %copy-start.9 = (f32[5,4,8,128]{3,2,1,0:T(8,128)}, f32[5,4,8,128]{3,2,1,0:T(8,128)S(1)}, u32[]{:S(2)}) copy-start(f32[5,4,8,128]{3,2,1,0:T(8,128)S(1)} %collective-permute-done.1.z_hi) | copy-start | bytes 245764
  27.9 3.7 %copy-start.6 = (f32[5,48,128]{2,1,0:T(8,128)}, f32[5,48,128]{2,1,0:T(8,128)S(1)}, u32[]{:S(2)}) copy-start(f32[5,48,128]{2,1,0:T(8,128)S(1)} %collective-permute-done.2.y_lo) | copy-start | bytes 368644
  27.9 3.7 %copy-start.7 = (f32[5,48,128]{2,1,0:T(8,128)}, f32[5,48,128]{2,1,0:T(8,128)S(1)}, u32[]{:S(2)}) copy-start(f32[5,48,128]{2,1,0:T(8,128)S(1)} %collective-permute-done.3.y_hi) | copy-start | bytes 368644
  27.9 3.7 %copy-start.4 = (f32[5,96,128]{2,1,0:T(8,128)}, f32[5,96,128]{2,1,0:T(8,128)S(1)}, u32[]{:S(2)}) copy-start(f32[5,96,128]{2,1,0:T(8,128)S(1)} %collective-permute-done.4.x_lo) | copy-start | bytes 737284
  31.6 0.7 copy-start.5
  57.1 1.3 %copy-start = (f32[5,512,128]{2,1,0:T(8,128)S(1)}, f32[5,512,128]{2,1,0:T(8,128)}, u32[]{:S(2)}) copy-start(f32[5,512,128]{2,1,0:T(8,128)} %flow.1.updated) | copy-start | bytes 3932164
  63.8 1.0 copy-start.1

commit v5 on v4

--- a/solution.py
+++ b/solution.py
@@ -147,13 +147,6 @@
     )(part)
 
 
-def edge_swap(low_edge, high_edge, axis):
-    size = lax.axis_size(axis)
-    up = [(i, (i + 1) % size) for i in range(size)]
-    down = [(b, a) for a, b in up]
-    return lax.ppermute(high_edge, axis, up), lax.ppermute(low_edge, axis, down)
-
-
 def flux_of(state, axis_d):
     density, energy = state[0], state[4]
     momenta = state[1:4]
@@ -240,16 +233,15 @@
     lax.fori_loop(0, cells + 1, face, 0)
 
 
-def z_part(coef, q, lo, hi, out, turned, planes, dq, df, fs, m2, faces, diff):
+def z_turn(q, turned):
     for c in range(5):
         for blk in range(4):
             tile = jnp.transpose(q[c, pl.ds(128 * blk, 128), :]) * SCALE
-            base = 160 * blk
-            turned[c, pl.ds(base, 8), :] = lo[c, blk] * SCALE
-            turned[c, pl.ds(base + 8, 72), :] = tile[:72]
-            turned[c, pl.ds(base + 80, 72), :] = tile[56:]
-            turned[c, pl.ds(base + 152, 8), :] = hi[c, blk] * SCALE
-
+            turned[c, pl.ds(160 * blk + 8, 72), :] = tile[:72]
+            turned[c, pl.ds(160 * blk + 80, 72), :] = tile[56:]
+
+
+def z_part(coef, out, turned, planes, dq, df, fs, m2, faces, diff):
     def gather(j, carry):
         for c in range(5):
             planes[c, j] = turned[c, pl.ds(j + 5, 8, stride=80), :]
@@ -272,23 +264,7 @@
             out[c, pl.ds(128 * blk, 128), :] = jnp.transpose(tile)
 
 
-def y_part(coef, q, lo, hi, out, planes, dq, df, fs, m2, faces, diff):
-    for c in range(5):
-        for h in range(2):
-            rows = pl.ds(8 * h, 8)
-            for k in range(3):
-                planes[c, k, rows, :] = lo[c, pl.ds(24 * h + k, 8, stride=3), :] * SCALE
-                planes[c, 35 + k, rows, :] = hi[c, pl.ds(24 * h + k, 8, stride=3), :] * SCALE
-
-    def gather(j, carry):
-        for c in range(5):
-            for h in range(2):
-                planes[c, j + 3, pl.ds(8 * h, 8), :] = (
-                    q[c, pl.ds(j + 256 * h, 8, stride=32), :] * SCALE
-                )
-        return carry
-
-    lax.fori_loop(0, 32, gather, 0)
+def y_part(coef, out, planes, dq, df, fs, m2, faces, diff):
     sweep(planes, dq, df, fs, m2, faces, 1, 32, 2, [(((0, 0), (1, 0)), 13)])
 
     def difference(i, carry):
@@ -310,18 +286,7 @@
     lax.fori_loop(0, 16, back, 0)
 
 
-def x_part(coef, q, lo, hi, add, old, out, planes, dq, df, fs, m2, faces):
-    for c in range(5):
-        for k in range(3):
-            planes[c, k] = lo[c, pl.ds(32 * k, 32), :] * SCALE
-            planes[c, 19 + k] = hi[c, pl.ds(32 * k, 32), :] * SCALE
-
-    def gather(j, carry):
-        for c in range(5):
-            planes[c, j + 3] = q[c, pl.ds(pl.multiple_of(32 * j, 32), 32), :] * SCALE
-        return carry
-
-    lax.fori_loop(0, 16, gather, 0)
+def x_part(coef, q, add, old, out, planes, dq, df, fs, m2, faces):
     streams = [(((0, 0), (1, 0)), 7), (((2, 0), (3, 0)), 7)]
     sweep(planes, dq, df, fs, m2, faces, 0, 16, 4, streams)
 
@@ -335,10 +300,81 @@
     lax.fori_loop(0, 16, finish, 0)
 
 
-def flow_kernel(coefs, q, old, z_lo, z_hi, y_lo, y_hi, x_lo, x_hi, out, turned, diff, add, *spaces):
-    z_part(coefs[2], q, z_lo, z_hi, add, turned, *spaces[0:6], diff)
-    y_part(coefs[1], q, y_lo, y_hi, add, *spaces[6:12], diff)
-    x_part(coefs[0], q, x_lo, x_hi, add, old, out, *spaces[12:18])
+def flow_kernel(coefs, q, old_in, out, turned, diff, add, old, send, recv, old_sem, *spaces):
+    here = {a: lax.axis_index(a) for a in ("gx", "gy", "gz")}
+
+    def beside(axis, step):
+        return {**here, axis: lax.rem(here[axis] + step, lax.axis_size(axis))}
+
+    sides = {a: (beside(a, 1), beside(a, lax.axis_size(a) - 1)) for a in here}
+    barrier = pltpu.get_barrier_semaphore()
+    for up, down in sides.values():
+        for device in (up, down):
+            pl.semaphore_signal(barrier, inc=1, device_id=device, device_id_type=MESH)
+
+    fetch_old = pltpu.make_async_copy(old_in, old, old_sem)
+    fetch_old.start()
+    planes_x, planes_y = spaces[12], spaces[6]
+
+    def gather_x(j, carry):
+        for c in range(5):
+            planes_x[c, j + 3] = q[c, pl.ds(pl.multiple_of(32 * j, 32), 32), :] * SCALE
+        return carry
+
+    lax.fori_loop(0, 16, gather_x, 0)
+
+    def gather_y(j, carry):
+        for c in range(5):
+            for h in range(2):
+                planes_y[c, j + 3, pl.ds(8 * h, 8), :] = (
+                    q[c, pl.ds(j + 256 * h, 8, stride=32), :] * SCALE
+                )
+        return carry
+
+    lax.fori_loop(0, 32, gather_y, 0)
+    pl.semaphore_wait(barrier, 6)
+    slots = iter(range(12))
+
+    def move(src, dst, device):
+        k = next(slots)
+        copy = pltpu.make_async_remote_copy(
+            src_ref=src,
+            dst_ref=dst,
+            send_sem=send.at[k],
+            recv_sem=recv.at[k],
+            device_id=device,
+            device_id_type=MESH,
+        )
+        copy.start()
+        return copy
+
+    along_y = [
+        move(planes_y.at[:, pl.ds(32, 3)], planes_y.at[:, pl.ds(0, 3)], sides["gy"][0]),
+        move(planes_y.at[:, pl.ds(3, 3)], planes_y.at[:, pl.ds(35, 3)], sides["gy"][1]),
+    ]
+    along_x = [
+        move(planes_x.at[:, pl.ds(16, 3)], planes_x.at[:, pl.ds(0, 3)], sides["gx"][0]),
+        move(planes_x.at[:, pl.ds(3, 3)], planes_x.at[:, pl.ds(19, 3)], sides["gx"][1]),
+    ]
+    z_turn(q, turned)
+    along_z = []
+    for blk in range(4):
+        low, high = turned.at[:, pl.ds(160 * blk, 8)], turned.at[:, pl.ds(160 * blk + 152, 8)]
+        first, last = turned.at[:, pl.ds(160 * blk + 8, 8)], turned.at[:, pl.ds(160 * blk + 144, 8)]
+        along_z.append(move(last, low, sides["gz"][0]))
+        along_z.append(move(first, high, sides["gz"][1]))
+    for copy in along_z:
+        copy.wait_recv()
+    z_part(coefs[2], add, turned, *spaces[0:6], diff)
+    for copy in along_y:
+        copy.wait_recv()
+    y_part(coefs[1], add, *spaces[6:12], diff)
+    for copy in along_x:
+        copy.wait_recv()
+    fetch_old.wait()
+    x_part(coefs[0], q, add, old, out, *spaces[12:18])
+    for copy in along_x + along_y + along_z:
+        copy.wait_send()
 
 
 def sweep_scratch(cells, rows):
@@ -356,27 +392,23 @@
 
 def flow_update(state_old, state_section, counts, step_size):
     f32 = jnp.float32
-    rows = state_section.reshape(5, 512, 128)
-    x_lo, x_hi = edge_swap(rows[:, :96], rows[:, 416:], "gx")
-    y_lo, y_hi = edge_swap(
-        state_section[:, :, :3].reshape(5, 48, 128), state_section[:, :, 29:].reshape(5, 48, 128), "gy"
-    )
-    strips = jnp.concatenate([state_section[..., :8], state_section[..., 120:]], axis=-1)
-    strips = jnp.transpose(strips.reshape(5, 4, 128, 16), (0, 1, 3, 2))
-    z_lo, z_hi = edge_swap(strips[:, :, :8], strips[:, :, 8:], "gz")
     coefs = [0.25 * step_size * n / (2.0 * SCALE) for n in counts]
     return pl.pallas_call(
         functools.partial(flow_kernel, coefs),
         out_shape=jax.ShapeDtypeStruct((5, 512, 128), f32),
+        in_specs=[pl.BlockSpec(memory_space=pltpu.VMEM), pl.BlockSpec(memory_space=pl.ANY)],
         scratch_shapes=[pltpu.VMEM((5, 640, 128), f32)]
-        + [pltpu.VMEM((5, 512, 128), f32)] * 2
+        + [pltpu.VMEM((5, 512, 128), f32)] * 3
+        + [pltpu.SemaphoreType.DMA((12,)), pltpu.SemaphoreType.DMA((12,)), pltpu.SemaphoreType.DMA]
         + sweep_scratch(64, 8)
         + sweep_scratch(32, 16)
         + sweep_scratch(16, 32),
-        compiler_params=pltpu.CompilerParams(vmem_limit_bytes=56 * 2**20),
+        compiler_params=pltpu.CompilerParams(
+            vmem_limit_bytes=56 * 2**20, collective_id=0, has_side_effects=True
+        ),
         cost_estimate=pl.CostEstimate(flops=100_000_000, bytes_accessed=6_000_000, transcendentals=0),
         name="flow",
-    )(rows, state_old.reshape(5, 512, 128), z_lo, z_hi, y_lo, y_hi, x_lo, x_hi)
+    )(state_section.reshape(5, 512, 128), state_old.reshape(5, 512, 128))
 
 
 def directions(angles):

time: 116 us -> 104 us (0.90)
  starting transfers between devices: 17.6 us -> 0 us
  Pallas kernels: 78.5 us -> 90.1 us
  waiting for transfers between devices: 5.27 us -> 0 us
  local copies, waits for them, and re-layouts: 7.99 us -> 4.56 us
  other arithmetic: 3.78 us -> 7.1 us
    ppermute x6 -> x0, starting transfers between devices: 17.6 us -> none  [the longest x3 10.8 us: edge_swap(): lax.ppermute(high_edge, axis, up)]
    pallas_call x1, Pallas kernels: 24.8 us -> 36.6 us  [flow_update(): pl.pallas_call(functools.partial(flow_kernel, coefs), out_shape=jax.Shape...]
    ppermute x6 -> x0, waiting for transfers between devices: 5.27 us -> none  [the longest x3 5.26 us: edge_swap(): lax.ppermute(low_edge, axis, down)]
    pallas_call x1, Pallas kernels: 5.44 us -> 2.55 us  [panel_sums(): pl.pallas_call(panel_kernel, out_shape=jax.ShapeDtypeStruct((1024 // OBS_...]
    pallas_call x1, Pallas kernels: 48.2 us -> 50.9 us  [summed_spectra(): pl.pallas_call(sum_kernel, out_shape=jax.ShapeDtypeStruct((2, 256, FREQS)...]
    slice x4 -> x0, local copies, waits for them, and re-layouts: 2.33 us -> none  [the longest x1 2.22 us: flow_update(): state_section[..., :8]]
    mul x2, other arithmetic: 1.21 us -> 2.8 us  [directions(): jnp.cos(polar_angle) * jnp.cos(azimuth)]
    reduce_sum x2, other arithmetic: 0.27 us -> 1.71 us  [panel_geometry(): centres = [jnp.mean(p, axis=1, keepdims=True) for p in places]]
  transfers between devices with their start and end apart: 6 -> 0, of which waited for: 2 -> 0; matrix products, arithmetic and copies ran while one was open for 4% -> 0% of each run, Pallas kernels for 0% -> 0%
where the time goes in v5:
time: 104 us; the launch traced here: 103 us
  Pallas kernels  90.1 us (87%)
  other arithmetic  7.1 us (7%)
  local copies, waits for them, and re-layouts  4.56 us (4%)
  between operations  1.46 us (1%)
    pallas_call x1, Pallas kernels, summed_spectra(): pl.pallas_call(sum_kernel, out_shape=jax.ShapeDtypeStruct((2, 256, FREQS)...  50.9 us
    pallas_call x1, Pallas kernels, flow_update(): pl.pallas_call(functools.partial(flow_kernel, coefs), out_shape=jax.Shape...  36.6 us
    unnamed x12, local copies, waits for them, and re-layouts  4.05 us
    mul x2, other arithmetic, directions(): jnp.cos(polar_angle) * jnp.cos(azimuth)  2.8 us
    pallas_call x1, Pallas kernels, panel_sums(): pl.pallas_call(panel_kernel, out_shape=jax.ShapeDtypeStruct((1024 // OBS_...  2.55 us

profile of v5, /device:TPU:1, one launch (start us, length us, event | category | flops | bytes accessed | tf_op | source)
XLA Modules:
  0.0 103.2 jit_solution(15141065251355250241)
XLA Ops:
  1.3 0.1 pad.5.clone
  1.4 0.1 pad.3.clone
  1.4 1.0 cosine_multiply_fusion.1
  2.5 0.7 multiply_reduce_fusion
  3.2 0.1 maximum_maximum_fusion.listeners
  3.3 0.8 fusion.36
  4.1 1.8 %cosine_multiply_fusion = (f32[1,4096]{1,0:T(1,128)S(1)}, f32[1,4096]{1,0:T(1,128)S(1)}, f32[1,4096]{1,0:T(1,128)S(1)}) fusion(f32[2,4096]{1,0:T(2,128)} %param.12), kind=kLoop, calls=%fused_computation.55 | loop fusion | flops 12288 | bytes 81920 | tf_op jit(solution)/shard_map/mul | solution.py:419
  6.0 0.9 fusion.34
  6.9 0.3 stack.48.geo
  7.2 0.6 sqrt_multiply_fusion.turns
  7.8 1.1 %fusion.7 = (f32[128,512]{1,0:T(8,128)S(1)}, f32[128,512]{1,0:T(8,128)S(1)}) fusion(s32[128]{0:T(128)S(1)} %iota_add_fusion), kind=kLoop, calls=%fused_computation.12 | loop fusion | flops 983040 | bytes 524800 | tf_op jit(solution)/shard_map/cos | solution.py:442
  9.0 0.0 copy-start.3
  9.0 36.6 %flow.1.updated = f32[5,512,128]{2,1,0:T(8,128)} custom-call(f32[5,512,128]{2,1,0:T(8,128)} %bitcast.52, f32[5,512,128]{2,1,0:T(8,128)} %bitcast.53), custom_call_target="tpu_custom_call" | custom-call | flops 100000000 | bytes 6000000 | tf_op jit(solution)/shard_map/flow/pallas_call | solution.py:396
  45.7 0.0 copy-done.3
  45.7 0.0 copy-start
  45.7 1.3 %copy-done = f32[5,512,128]{2,1,0:T(8,128)S(1)} copy-done((f32[5,512,128]{2,1,0:T(8,128)S(1)}, f32[5,512,128]{2,1,0:T(8,128)}, u32[]{:S(2)}) %copy-start) | copy-done | bytes 1310744
  47.0 2.5 %panels.1.part = f32[4,2,32,8,128]{4,3,2,1,0:T(8,128)S(1)} custom-call(s32[1]{0:T(128)S(6)} %copy.27.live, f32[5,512,128]{2,1,0:T(8,128)S(1)} %copy-done, bf16[4096,512]{1,0:T(8,128)(2,1)} %record.1, s32[8,1,512]{2,1,0:T(1,128)S(1)} %bitcast.51, f32[32,16,128]{2,1,0:T(8,128)S(1)} %stack.48.geo, f32[32,1,1024]{2,1,0:T(1,128)S(1)} %sqrt_multiply_fusion.turns, ...), custom_call_target="tpu_custom_call" | custom-call | flops 4000000000 | bytes 8000000 | tf_op jit(solution)/shard_map/panels/pallas_call | solution.py:584
  49.5 0.0 copy-start.2
  49.6 1.0 copy-done.2
  50.5 0.0 copy-start.1
  50.5 50.9 %sum_spectra.1 = f32[2,256,128]{2,1,0:T(8,128)} custom-call(f32[4,2,32,8,128]{4,3,2,1,0:T(8,128)} %copy-done.2), custom_call_target="tpu_custom_call" | custom-call | tf_op jit(solution)/shard_map/sum_spectra/pallas_call | solution.py:120
  101.4 0.0 copy-done.1
  101.4 0.0 copy-start.4
  101.4 1.1 %copy.28 = f32[5,16,32,128]{3,2,1,0:T(8,128)} copy(f32[5,16,32,128]{3,2,1,0:T(8,128)S(1)} %bitcast.50) | data formatting | bytes 2621440
  102.5 0.0 copy-done.4
  102.5 0.7 copy.29
  (12 shorter events, 0.1 us)
Async XLA Ops:
  9.0 36.7 %copy-start.3 = (s32[32,128]{1,0:T(8,128)S(1)}, s32[32,128]{1,0:T(8,128)}, u32[]{:S(2)}) copy-start(s32[32,128]{1,0:T(8,128)} %param.11) | copy-start | bytes 49156
  45.7 1.3 %copy-start = (f32[5,512,128]{2,1,0:T(8,128)S(1)}, f32[5,512,128]{2,1,0:T(8,128)}, u32[]{:S(2)}) copy-start(f32[5,512,128]{2,1,0:T(8,128)} %flow.1.updated) | copy-start | bytes 3932164
  49.5 1.0 copy-start.2
  50.5 50.9 %copy-start.1 = (f32[5,512,128]{2,1,0:T(8,128)S(1)}, f32[5,512,128]{2,1,0:T(8,128)}, u32[]{:S(2)}) copy-start(f32[5,512,128]{2,1,0:T(8,128)} %flow.1.updated) | copy-start | bytes 3932164
  101.4 1.1 %copy-start.4 = (f32[2,256,128]{2,1,0:T(8,128)S(1)}, f32[2,256,128]{2,1,0:T(8,128)}, u32[]{:S(2)}) copy-start(f32[2,256,128]{2,1,0:T(8,128)} %sum_spectra.1) | copy-start | bytes 786436

commit v6 on v5

--- a/solution.py
+++ b/solution.py
@@ -3,6 +3,7 @@
 
 import jax
 import jax.numpy as jnp
+import numpy as np
 from jax import lax
 from jax.experimental import pallas as pl
 from jax.experimental.pallas import tpu as pltpu
@@ -142,7 +143,9 @@
             dma,
             dma,
         ],
-        compiler_params=pltpu.CompilerParams(collective_id=1, has_side_effects=True),
+        compiler_params=pltpu.CompilerParams(
+            vmem_limit_bytes=63 * 2**20, collective_id=1, has_side_effects=True
+        ),
         name="sum_spectra",
     )(part)
 
@@ -286,21 +289,20 @@
     lax.fori_loop(0, 16, back, 0)
 
 
-def x_part(coef, q, add, old, out, planes, dq, df, fs, m2, faces):
+def x_part(coef, add, out, planes, dq, df, fs, m2, faces):
     streams = [(((0, 0), (1, 0)), 7), (((2, 0), (3, 0)), 7)]
     sweep(planes, dq, df, fs, m2, faces, 0, 16, 4, streams)
 
     def finish(i, carry):
         rows = pl.ds(pl.multiple_of(32 * i, 32), 32)
         for c in range(5):
-            change = add[c, rows, :] + coef * (faces[c, i + 1] - faces[c, i])
-            out[c, rows, :] = (0.75 * old[c, rows, :] + 0.25 * q[c, rows, :]) - change
+            out[c, rows, :] = add[c, rows, :] + coef * (faces[c, i + 1] - faces[c, i])
         return carry
 
     lax.fori_loop(0, 16, finish, 0)
 
 
-def flow_kernel(coefs, q, old_in, out, turned, diff, add, old, send, recv, old_sem, *spaces):
+def flow_kernel(coefs, q, out, turned, diff, add, send, recv, *spaces):
     here = {a: lax.axis_index(a) for a in ("gx", "gy", "gz")}
 
     def beside(axis, step):
@@ -312,8 +314,6 @@
         for device in (up, down):
             pl.semaphore_signal(barrier, inc=1, device_id=device, device_id_type=MESH)
 
-    fetch_old = pltpu.make_async_copy(old_in, old, old_sem)
-    fetch_old.start()
     planes_x, planes_y = spaces[12], spaces[6]
 
     def gather_x(j, carry):
@@ -371,8 +371,7 @@
     y_part(coefs[1], add, *spaces[6:12], diff)
     for copy in along_x:
         copy.wait_recv()
-    fetch_old.wait()
-    x_part(coefs[0], q, add, old, out, *spaces[12:18])
+    x_part(coefs[0], add, out, *spaces[12:18])
     for copy in along_x + along_y + along_z:
         copy.wait_send()
 
@@ -390,58 +389,34 @@
     ]
 
 
-def flow_update(state_old, state_section, counts, step_size):
+def flow_change(section, counts, step_size):
     f32 = jnp.float32
     coefs = [0.25 * step_size * n / (2.0 * SCALE) for n in counts]
     return pl.pallas_call(
         functools.partial(flow_kernel, coefs),
         out_shape=jax.ShapeDtypeStruct((5, 512, 128), f32),
-        in_specs=[pl.BlockSpec(memory_space=pltpu.VMEM), pl.BlockSpec(memory_space=pl.ANY)],
+        in_specs=[pl.BlockSpec(memory_space=pltpu.VMEM)],
         scratch_shapes=[pltpu.VMEM((5, 640, 128), f32)]
-        + [pltpu.VMEM((5, 512, 128), f32)] * 3
-        + [pltpu.SemaphoreType.DMA((12,)), pltpu.SemaphoreType.DMA((12,)), pltpu.SemaphoreType.DMA]
+        + [pltpu.VMEM((5, 512, 128), f32)] * 2
+        + [pltpu.SemaphoreType.DMA((12,)), pltpu.SemaphoreType.DMA((12,))]
         + sweep_scratch(64, 8)
         + sweep_scratch(32, 16)
         + sweep_scratch(16, 32),
         compiler_params=pltpu.CompilerParams(
-            vmem_limit_bytes=56 * 2**20, collective_id=0, has_side_effects=True
+            vmem_limit_bytes=63 * 2**20, collective_id=0, has_side_effects=True
         ),
         cost_estimate=pl.CostEstimate(flops=100_000_000, bytes_accessed=6_000_000, transcendentals=0),
         name="flow",
-    )(state_section.reshape(5, 512, 128), state_old.reshape(5, 512, 128))
-
-
-def directions(angles):
-    polar_angle = 0.5 * angles[0]
-    azimuth = angles[1]
-    return jnp.stack(
-        [
-            jnp.cos(polar_angle) * jnp.cos(azimuth),
-            jnp.cos(polar_angle) * jnp.sin(azimuth),
-            jnp.sin(polar_angle),
-        ]
-    )
-
-
-def panel_places(cell_rows, blocks, cells, counts):
-    along = (
-        cell_rows // (cells[1] * cells[2]),
-        cell_rows // cells[2] % cells[1],
-        cell_rows % cells[2],
-    )
-    return [
-        ((blocks[d] * cells[d] + along[d]).astype(jnp.float32) + 0.5) / counts[d] for d in range(3)
-    ]
+    )(section)
 
 
 def dft_table(sample_count, freq_count):
-    times = jnp.arange(sample_count, dtype=jnp.int32)[None, :]
-    orders = jnp.arange(1, freq_count + 1, dtype=jnp.int32)[:, None]
-    phases = 2.0 * math.pi / sample_count * (times * orders % sample_count).astype(jnp.float32)
+    times = np.arange(sample_count)[None, :]
+    orders = np.arange(1, freq_count + 1)[:, None]
+    phases = 2.0 * math.pi / sample_count * (times * orders % sample_count)
     scaling = 1.0 / math.sqrt(sample_count)
-    return (jnp.concatenate([jnp.cos(phases), -jnp.sin(phases)], axis=0) * scaling).astype(
-        jnp.bfloat16
-    )
+    table = np.concatenate([np.cos(phases), -np.sin(phases)], axis=0).astype(np.float32) * scaling
+    return jnp.asarray(table.astype(np.float32).astype(jnp.bfloat16))
 
 
 def sin_cos(turns):
@@ -481,29 +456,75 @@
 
 
 def panel_kernel(
-    live, updated, record, cells, geo, turns, listeners, table, out, density, records, pieces, heard, spectra, sems
+    counts, live, change, old, section, record, cells, angles, ears, ranges, table,
+    out, updated, state, olds, sections, records, pieces, heard, shown, spectra, sems,
 ):
     groups = (live[0] + GROUP - 1) // GROUP
+    origin = [lax.axis_index(a) * n for a, n in zip(("gx", "gy", "gz"), (16, 32, 128))]
 
     def fetch(g):
         return pltpu.make_async_copy(
             record.at[pl.ds(128 * GROUP * g, 128 * GROUP)], records.at[g], sems.at[g]
         )
 
-    first = pltpu.make_async_copy(updated.at[0], density, sems.at[GROUPS])
-    first.start()
+    def bring(first, count, sem):
+        rows = pl.ds(first, count)
+        return [
+            pltpu.make_async_copy(change.at[rows], state.at[rows], sems.at[sem]),
+            pltpu.make_async_copy(old.at[rows], olds.at[rows], sems.at[sem + 1]),
+            pltpu.make_async_copy(section.at[rows], sections.at[rows], sems.at[sem + 2]),
+        ]
+
+    def finish(c):
+        state[c] = (0.75 * olds[c] + 0.25 * sections[c]) - state[c]
+
+    density_in, rest_in = bring(0, 1, GROUPS), bring(1, 4, GROUPS + 3)
+    density_out = pltpu.make_async_copy(state.at[0], updated.at[0], sems.at[GROUPS + 6])
+    rest_out = pltpu.make_async_copy(
+        state.at[pl.ds(1, 4)], updated.at[pl.ds(1, 4)], sems.at[GROUPS + 7]
+    )
+    for copy in density_in:
+        copy.start()
     for g in range(GROUPS):
         pl.when(g < groups)(fetch(g).start)
+    for copy in rest_in:
+        copy.start()
 
     out[...] = jnp.zeros_like(out)
-    split = in_pieces(listeners[...])
-    heard[...] = jnp.concatenate([split[t] for _, t in PAIRS], axis=0).astype(jnp.bfloat16)
-    first.wait()
+    place = lax.broadcasted_iota(jnp.int32, (8, 128), 0)
+    half_turn = 0.5 / math.pi
+
+    def tile(*rows):
+        made = jnp.where(place == 0, rows[0], 0.0)
+        for k, row in enumerate(rows[1:], 1):
+            made = jnp.where(place == k, row, made)
+        return made
+
+    def direction(sine, cosine):
+        return cosine[0:1] * cosine[1:2], cosine[0:1] * sine[1:2], sine[0:1]
+
+    def turned_angles(pair):
+        row = lax.broadcasted_iota(jnp.int32, pair.shape, 0)
+        return pair * jnp.where(row == 0, 0.5 * half_turn, half_turn)
+
+    for k in range(8):
+        lanes = pl.ds(128 * k, 128)
+        reach = ranges[:, lanes]
+        spot = [reach * d for d in direction(*sin_cos(turned_angles(ears[:, lanes])))]
+        far = (spot[0] * spot[0] + spot[1] * spot[1]) + spot[2] * spot[2]
+        split = in_pieces(tile(*spot, jnp.ones_like(far), far))
+        heard[:, lanes] = jnp.concatenate([split[t] for _, t in PAIRS], axis=0).astype(jnp.bfloat16)
+        shown[:, lanes] = tile(*spot)
+
+    for copy in density_in:
+        copy.wait()
+    finish(0)
     turned = jnp.concatenate(
-        [jnp.transpose(density[pl.ds(128 * k, 128), :]) for k in range(4)], axis=1
+        [jnp.transpose(state[0, pl.ds(128 * k, 128), :]) for k in range(4)], axis=1
     )
     for k, piece in enumerate(in_pieces(turned)):
         pieces[pl.ds(128 * k, 128), :] = piece.astype(jnp.bfloat16)
+    density_out.start()
 
     def front(g, carry):
         cell = cells[g]
@@ -525,13 +546,37 @@
 
     lax.fori_loop(0, groups, front, 0)
 
-    order = (lax.broadcasted_iota(jnp.int32, (8, 128), 0) + 1).astype(jnp.float32)
+    for copy in rest_in:
+        copy.wait()
+    for c in range(1, 5):
+        finish(c)
+    rest_out.start()
+    order = (place + 1).astype(jnp.float32)
 
     def features(b, alive):
-        facing, apart = in_pieces(geo[b, 0:8] * alive), in_pieces(geo[b, 8:16])
-        return jnp.concatenate(
+        cell = cells[b // GROUP, :, pl.ds(pl.multiple_of(128 * lax.rem(b, GROUP), 128), 128)]
+        along = (cell >> 12, (cell >> 7) & 31, cell & 127)
+        spot = [
+            ((origin[d] + along[d]).astype(jnp.float32) + 0.5) * (1.0 / counts[d]) - 0.5
+            for d in range(3)
+        ]
+        lanes = pl.ds(pl.multiple_of(128 * b, 128), 128)
+        normal = direction(*sin_cos(turned_angles(angles[:, lanes])))
+        normal = [n * (alive * (0.25 / math.pi)) for n in normal]
+        across = -((normal[0] * spot[0] + normal[1] * spot[1]) + normal[2] * spot[2])
+        square = (spot[0] * spot[0] + spot[1] * spot[1]) + spot[2] * spot[2]
+        twice = [-2.0 * p for p in spot]
+        facing = in_pieces(tile(*normal, across))
+        apart = in_pieces(tile(*twice, square, jnp.ones_like(square)))
+        seen = jnp.concatenate(
             [jnp.concatenate([facing[s], apart[s]], axis=1) for s, _ in PAIRS], axis=0
         ).astype(jnp.bfloat16)
+        return seen, jnp.sum(tile(*twice), axis=1, keepdims=True)
+
+    def turns_of(centre, first):
+        apart = shown[:, pl.ds(first, 128)] + centre * (1.0 / 256.0)
+        square = jnp.sum(apart * apart, axis=0, keepdims=True)
+        return square * lax.rsqrt(square) * (WAVE_STEP * half_turn)
 
     def weights_of(seen, o):
         both = lax.dot_general(
@@ -542,10 +587,10 @@
         )
         return (both[:128] / both[128:]).astype(jnp.bfloat16)
 
-    def add_turned(b, o, product):
+    def add_turned(centre, o, product):
         for h in range(OBS_CHUNK // 128):
             lanes = slice(128 * h, 128 * h + 128)
-            base = turns[b, :, pl.ds(OBS_CHUNK * o + 128 * h, 128)]
+            base = turns_of(centre, OBS_CHUNK * o + 128 * h)
             sine, cosine = sin_cos(base * order)
             step_s = jnp.broadcast_to(sine[7:8], (8, 128))
             step_c = jnp.broadcast_to(cosine[7:8], (8, 128))
@@ -566,69 +611,46 @@
         for k in range(PAIR):
             b = PAIR * pair + k
             alive = jnp.where(b < live[0], 1.0, 0.0)
-            blocks.append((b, features(b, alive), spectra[b]))
+            blocks.append((*features(b, alive), spectra[b]))
         for o in range(1024 // OBS_CHUNK):
-            for b, seen, spectrum in blocks:
+            for seen, centre, spectrum in blocks:
                 product = jnp.dot(
                     spectrum, weights_of(seen, o), preferred_element_type=jnp.float32
                 )
-                add_turned(b, o, product)
+                add_turned(centre, o, product)
         return carry
 
     lax.fori_loop(0, (live[0] + PAIR - 1) // PAIR, back, 0)
-
-
-def panel_sums(live_count, updated, record, cells, geo, turns, listeners, table):
-    vmem = pl.BlockSpec(memory_space=pltpu.VMEM)
-    bf16 = jnp.bfloat16
+    density_out.wait()
+    rest_out.wait()
+
+
+def panel_sums(counts, live_count, change, old, section, record, cells, angles, ears, ranges, table):
+    vmem, anywhere = pl.BlockSpec(memory_space=pltpu.VMEM), pl.BlockSpec(memory_space=pl.ANY)
+    bf16, f32 = jnp.bfloat16, jnp.float32
     return pl.pallas_call(
-        panel_kernel,
-        out_shape=jax.ShapeDtypeStruct((1024 // OBS_CHUNK, 2, 32, 8, 128), jnp.float32),
-        in_specs=[
-            pl.BlockSpec(memory_space=pltpu.SMEM),
-            pl.BlockSpec(memory_space=pl.ANY),
-            pl.BlockSpec(memory_space=pl.ANY),
-        ]
-        + [vmem] * 5,
-        out_specs=vmem,
-        scratch_shapes=[
-            pltpu.VMEM((512, 128), jnp.float32),
+        functools.partial(panel_kernel, counts),
+        out_shape=(
+            jax.ShapeDtypeStruct((1024 // OBS_CHUNK, 2, TILES, 8, 128), f32),
+            jax.ShapeDtypeStruct((5, 512, 128), f32),
+        ),
+        in_specs=[pl.BlockSpec(memory_space=pltpu.SMEM)] + [anywhere] * 4 + [vmem] * 5,
+        out_specs=(vmem, anywhere),
+        scratch_shapes=[pltpu.VMEM((5, 512, 128), f32)] * 3
+        + [
             pltpu.VMEM((GROUPS, 128 * GROUP, 512), bf16),
             pltpu.VMEM((384, 512), bf16),
             pltpu.VMEM((8 * len(PAIRS), 1024), bf16),
+            pltpu.VMEM((8, 1024), f32),
             pltpu.VMEM((32, 256, 128), bf16),
-            pltpu.SemaphoreType.DMA((GROUPS + 1,)),
+            pltpu.SemaphoreType.DMA((GROUPS + 8,)),
         ],
-        compiler_params=pltpu.CompilerParams(vmem_limit_bytes=48 * 2**20),
+        compiler_params=pltpu.CompilerParams(vmem_limit_bytes=63 * 2**20),
         cost_estimate=pl.CostEstimate(
             flops=4_000_000_000, bytes_accessed=8_000_000, transcendentals=0
         ),
         name="panels",
-    )(live_count, updated, record, cells, geo, turns, listeners, table)
-
-
-def panel_geometry(panel_cell, panel_angles, listener_angles, listener_range, blocks, cells, counts):
-    slot_count, block_rows = panel_cell.shape
-    places = [p - 0.5 for p in panel_places(panel_cell, blocks, cells, counts)]
-    normals = directions(panel_angles.reshape(2, slot_count, block_rows)) * (0.25 / math.pi)
-    across = -sum(normals[d] * places[d] for d in range(3))
-    square = sum(p * p for p in places)
-    blank = jnp.zeros_like(square)
-    geo = jnp.stack(
-        [normals[0], normals[1], normals[2], across, blank, blank, blank, blank]
-        + [-2.0 * p for p in places]
-        + [square, blank + 1.0, blank, blank, blank],
-        axis=1,
-    )
-    heard = listener_range[None, :] * directions(listener_angles)
-    centres = [jnp.mean(p, axis=1, keepdims=True) for p in places]
-    apart = sum((heard[d][None, :] - centres[d]) ** 2 for d in range(3))
-    turns = jnp.sqrt(apart) * (WAVE_STEP / (2.0 * math.pi))
-    listeners = jnp.concatenate(
-        [heard, jnp.ones_like(heard[:1]), jnp.sum(heard * heard, axis=0, keepdims=True), jnp.zeros_like(heard)],
-        axis=0,
-    )
-    return geo, turns.reshape(slot_count, 1, -1), listeners
+    )(live_count, change, old, section, record, cells, angles, ears, ranges, table)
 
 
 def local(
@@ -642,30 +664,23 @@
     listener_range,
 ):
     cells = state_section.shape[1:]
-    axes = ("gx", "gy", "gz")
-    counts = tuple(n * lax.axis_size(a) for n, a in zip(cells, axes))
-    step_size = COURANT / max(counts)
-    geo, turns, listeners = panel_geometry(
-        panel_cell,
+    counts = tuple(n * lax.axis_size(a) for n, a in zip(cells, ("gx", "gy", "gz")))
+    section = state_section.reshape(5, 512, 128)
+    change = flow_change(section, counts, COURANT / max(counts))
+    part, updated = panel_sums(
+        counts,
+        owned_blocks,
+        change,
+        state_old.reshape(5, 512, 128),
+        section,
+        panel_record,
+        panel_cell.reshape(GROUPS, 1, 128 * GROUP),
         panel_angles,
         listener_angles,
-        listener_range,
-        [lax.axis_index(a) for a in axes],
-        cells,
-        counts,
-    )
-    updated = flow_update(state_old, state_section, counts, step_size)
-    partial = panel_sums(
-        owned_blocks,
-        updated,
-        panel_record,
-        panel_cell.reshape(GROUPS, 1, 128 * GROUP),
-        geo,
-        turns,
-        listeners,
+        listener_range.reshape(1, -1),
         dft_table(panel_record.shape[1], FREQS),
     )
-    return updated.reshape(state_section.shape), summed_spectra(partial)
+    return updated.reshape(state_section.shape), summed_spectra(part)
 
 
 def solution(mesh):

time: 104 us -> 96.3 us (0.926)
  other arithmetic: 7.1 us -> 0 us
  Pallas kernels: 90.1 us -> 93.2 us
  local copies, waits for them, and re-layouts: 4.56 us -> 1.67 us
    mul x4 -> x0, other arithmetic: 3.42 us -> none  [the longest x2 2.8 us: directions(): jnp.cos(polar_angle) * jnp.cos(azimuth)]
    pallas_call x2, Pallas kernels: 39.2 us -> 42.2 us  [the longest x1 36.5 us: flow_change(): pl.pallas_call(functools.partial(flow_kernel, coefs), out_shape=jax.Shape...]
    reduce_sum x3 -> x0, other arithmetic: 2.43 us -> none  [the longest x2 1.71 us: panel_geometry(): centres = [jnp.mean(p, axis=1, keepdims=True) for p in places]]
    unnamed x12 -> x1, local copies, waits for them, and re-layouts: 4.05 us -> 1.67 us
    cos x1 -> x0, other arithmetic: 1.1 us -> none  [dft_table(): jnp.cos(phases)]
where the time goes in v6:
time: 96.3 us; the launch traced here: 96.2 us
  Pallas kernels  93.2 us (97%)
  local copies, waits for them, and re-layouts  1.67 us (2%)
  between operations  1.3 us (1%)
    pallas_call x1, Pallas kernels, summed_spectra(): pl.pallas_call(sum_kernel, out_shape=jax.ShapeDtypeStruct((2, 256, FREQS)...  51 us
    pallas_call x1, Pallas kernels, flow_change(): pl.pallas_call(functools.partial(flow_kernel, coefs), out_shape=jax.Shape...  36.5 us
    pallas_call x1, Pallas kernels, panel_sums(): pl.pallas_call(functools.partial(panel_kernel, counts), out_shape=(jax.Sh...  5.68 us

profile of v6, /device:TPU:1, one launch (start us, length us, event | category | flops | bytes accessed | tf_op | source)
XLA Modules:
  0.0 96.2 jit_solution(11018950875371952932)
XLA Ops:
  1.3 36.5 %flow.1.change = f32[5,512,128]{2,1,0:T(8,128)} custom-call(f32[5,512,128]{2,1,0:T(8,128)} %bitcast.5), custom_call_target="tpu_custom_call" | custom-call | flops 100000000 | bytes 6000000 | tf_op jit(solution)/shard_map/flow/pallas_call | solution.py:395
  37.8 5.7 %panels.1 = (f32[4,2,32,8,128]{4,3,2,1,0:T(8,128)}, f32[5,512,128]{2,1,0:T(8,128)}) custom-call(s32[1]{0:T(128)S(6)} %copy.12.live, f32[5,512,128]{2,1,0:T(8,128)} %flow.1.change, f32[5,512,128]{2,1,0:T(8,128)} %bitcast.7, f32[5,512,128]{2,1,0:T(8,128)} %bitcast.6, bf16[4096,512]{1,0:T(8,128)(2,1)} %record.1, s32[8,1,512]{2,1,0:T(1,128)} %bitcast.8, ...), custom_call_target="tpu_custom_call" | custom-call | flops 4000000000 | bytes 8000000 | tf_op jit(solution)/shard_map/panels/pallas_call | solution.py:631
  43.5 51.0 %sum_spectra.1 = f32[2,256,128]{2,1,0:T(8,128)} custom-call(f32[4,2,32,8,128]{4,3,2,1,0:T(8,128)} %get-tuple-element.5.part), custom_call_target="tpu_custom_call" | custom-call | tf_op jit(solution)/shard_map/sum_spectra/pallas_call | solution.py:121
  94.5 1.7 %copy.13 = f32[2,256,128]{2,1,0:T(8,128)} copy(f32[2,256,128]{2,1,0:T(8,128)} %sum_spectra.1) | data formatting | bytes 524288

commit v7 on v6

--- a/solution.py
+++ b/solution.py
@@ -192,35 +192,36 @@
     return fsum + ((0.5 * (up[1] - dn[3]) - aq[2]) + ratio) * (1.0 / 3.0)
 
 
-def sweep(planes, dq, df, fs, m2, faces, axis_d, cells, chunks, streams):
+def differences(planes, dq, df, fs, m2, axis_d, group, length, unroll):
     def load(r, j):
         return [planes[c, j, pl.ds(8 * r, 8), :] for c in range(5)]
 
-    for group, length in streams:
-
-        def step(k, carry):
-            for u in range(3):
-                after = []
-                for (r, start), (state, flux, speed) in zip(group, carry):
-                    j, rows = start + 3 * k + u, pl.ds(8 * r, 8)
-                    next_state = load(r, j + 1)
-                    next_flux, next_speed = flux_of(next_state, axis_d)
-                    for c in range(5):
-                        dq[c, j, rows, :] = next_state[c] - state[c]
-                        df[c, j, rows, :] = next_flux[c] - flux[c]
-                        fs[c, j, rows, :] = next_flux[c] + flux[c]
-                    m2[j, rows, :] = jnp.maximum(next_speed, speed)
-                    after.append((next_state, next_flux, next_speed))
-                carry = after
-            return carry
-
-        begin = []
-        for r, start in group:
-            state = load(r, start)
-            begin.append((state, *flux_of(state, axis_d)))
-        lax.fori_loop(0, length, step, begin)
-
-    def face(i, carry):
+    def step(k, carry):
+        for u in range(unroll):
+            after = []
+            for (r, start), (state, flux, speed) in zip(group, carry):
+                j, rows = start + unroll * k + u, pl.ds(8 * r, 8)
+                next_state = load(r, j + 1)
+                next_flux, next_speed = flux_of(next_state, axis_d)
+                for c in range(5):
+                    dq[c, j, rows, :] = next_state[c] - state[c]
+                    df[c, j, rows, :] = next_flux[c] - flux[c]
+                    fs[c, j, rows, :] = next_flux[c] + flux[c]
+                m2[j, rows, :] = jnp.maximum(next_speed, speed)
+                after.append((next_state, next_flux, next_speed))
+            carry = after
+        return carry
+
+    begin = []
+    for r, start in group:
+        state = load(r, start)
+        begin.append((state, *flux_of(state, axis_d)))
+    lax.fori_loop(0, length, step, begin)
+
+
+def face_fluxes(dq, df, fs, m2, faces, chunks, count, which):
+    def face(k, carry):
+        i = which(k)
         for r in range(chunks):
             rows = pl.ds(8 * r, 8)
             alpha = jnp.maximum(jnp.maximum(m2[i, rows, :], m2[i + 2, rows, :]), m2[i + 4, rows, :])
@@ -233,7 +234,7 @@
                 )
         return carry
 
-    lax.fori_loop(0, cells + 1, face, 0)
+    lax.fori_loop(0, count, face, 0)
 
 
 def z_turn(q, turned):
@@ -251,7 +252,8 @@
         return carry
 
     lax.fori_loop(0, 70, gather, 0, unroll=2)
-    sweep(planes, dq, df, fs, m2, faces, 2, 64, 1, [(((0, 0), (0, 33)), 12)])
+    differences(planes, dq, df, fs, m2, 2, ((0, 0), (0, 33)), 12, 3)
+    face_fluxes(dq, df, fs, m2, faces, 1, 65, lambda k: k)
 
     def difference(i, carry):
         for c in range(5):
@@ -267,8 +269,17 @@
             out[c, pl.ds(128 * blk, 128), :] = jnp.transpose(tile)
 
 
+def y_inner(planes, dq, df, fs, m2, faces):
+    both = ((0, 3), (1, 3))
+    differences(planes, dq, df, fs, m2, 1, both, 10, 3)
+    differences(planes, dq, df, fs, m2, 1, ((0, 33), (1, 33)), 1, 1)
+    face_fluxes(dq, df, fs, m2, faces, 2, 27, lambda k: k + 3)
+
+
 def y_part(coef, out, planes, dq, df, fs, m2, faces, diff):
-    sweep(planes, dq, df, fs, m2, faces, 1, 32, 2, [(((0, 0), (1, 0)), 13)])
+    differences(planes, dq, df, fs, m2, 1, ((0, 0), (1, 0)), 1, 3)
+    differences(planes, dq, df, fs, m2, 1, ((0, 34), (1, 34)), 1, 3)
+    face_fluxes(dq, df, fs, m2, faces, 2, 6, lambda k: k + 27 * (k // 3))
 
     def difference(i, carry):
         for c in range(5):
@@ -289,9 +300,17 @@
     lax.fori_loop(0, 16, back, 0)
 
 
+def x_inner(planes, dq, df, fs, m2, faces):
+    differences(planes, dq, df, fs, m2, 0, ((0, 3), (1, 3)), 5, 3)
+    differences(planes, dq, df, fs, m2, 0, ((2, 3), (3, 3)), 5, 3)
+    face_fluxes(dq, df, fs, m2, faces, 4, 11, lambda k: k + 3)
+
+
 def x_part(coef, add, out, planes, dq, df, fs, m2, faces):
-    streams = [(((0, 0), (1, 0)), 7), (((2, 0), (3, 0)), 7)]
-    sweep(planes, dq, df, fs, m2, faces, 0, 16, 4, streams)
+    for start in (0, 18):
+        differences(planes, dq, df, fs, m2, 0, ((0, start), (1, start)), 1, 3)
+        differences(planes, dq, df, fs, m2, 0, ((2, start), (3, start)), 1, 3)
+    face_fluxes(dq, df, fs, m2, faces, 4, 6, lambda k: k + 11 * (k // 3))
 
     def finish(i, carry):
         rows = pl.ds(pl.multiple_of(32 * i, 32), 32)
@@ -363,9 +382,11 @@
         first, last = turned.at[:, pl.ds(160 * blk + 8, 8)], turned.at[:, pl.ds(160 * blk + 144, 8)]
         along_z.append(move(last, low, sides["gz"][0]))
         along_z.append(move(first, high, sides["gz"][1]))
+    y_inner(*spaces[6:12])
     for copy in along_z:
         copy.wait_recv()
     z_part(coefs[2], add, turned, *spaces[0:6], diff)
+    x_inner(*spaces[12:18])
     for copy in along_y:
         copy.wait_recv()
     y_part(coefs[1], add, *spaces[6:12], diff)
@@ -378,13 +399,12 @@
 
 def sweep_scratch(cells, rows):
     f32 = jnp.float32
-    steps = -(-(cells + 5) // 3) * 3
     return [
-        pltpu.VMEM((5, steps + 1, rows, 128), f32),
-        pltpu.VMEM((5, steps, rows, 128), f32),
-        pltpu.VMEM((5, steps, rows, 128), f32),
-        pltpu.VMEM((5, steps, rows, 128), f32),
-        pltpu.VMEM((steps, rows, 128), f32),
+        pltpu.VMEM((5, cells + 6, rows, 128), f32),
+        pltpu.VMEM((5, cells + 5, rows, 128), f32),
+        pltpu.VMEM((5, cells + 5, rows, 128), f32),
+        pltpu.VMEM((5, cells + 5, rows, 128), f32),
+        pltpu.VMEM((cells + 5, rows, 128), f32),
         pltpu.VMEM((5, cells + 1, rows, 128), f32),
     ]
 

time: 96.3 us -> 92.8 us (0.964)
  Pallas kernels: 93.2 us -> 89.7 us
    pallas_call x1, Pallas kernels: 36.5 us -> 32 us  [flow_change(): pl.pallas_call(functools.partial(flow_kernel, coefs), out_shape=jax.Shape...]
    pallas_call x1, Pallas kernels: 51 us -> 52.1 us  [summed_spectra(): pl.pallas_call(sum_kernel, out_shape=jax.ShapeDtypeStruct((2, 256, FREQS)...]
where the time goes in v7:
time: 92.8 us; the launch traced here: 92.7 us
  Pallas kernels  89.7 us (97%)
  local copies, waits for them, and re-layouts  1.67 us (2%)
  between operations  1.3 us (1%)
    pallas_call x1, Pallas kernels, summed_spectra(): pl.pallas_call(sum_kernel, out_shape=jax.ShapeDtypeStruct((2, 256, FREQS)...  52.1 us
    pallas_call x1, Pallas kernels, flow_change(): pl.pallas_call(functools.partial(flow_kernel, coefs), out_shape=jax.Shape...  32 us
    pallas_call x1, Pallas kernels, panel_sums(): pl.pallas_call(functools.partial(panel_kernel, counts), out_shape=(jax.Sh...  5.68 us

profile of v7, /device:TPU:1, one launch (start us, length us, event | category | flops | bytes accessed | tf_op | source)
XLA Modules:
  0.0 92.7 jit_solution(16112108295246287299)
XLA Ops:
  1.3 32.0 %flow.1.change = f32[5,512,128]{2,1,0:T(8,128)} custom-call(f32[5,512,128]{2,1,0:T(8,128)} %bitcast.5), custom_call_target="tpu_custom_call" | custom-call | flops 100000000 | bytes 6000000 | tf_op jit(solution)/shard_map/flow/pallas_call | solution.py:415
  33.3 5.7 %panels.1 = (f32[4,2,32,8,128]{4,3,2,1,0:T(8,128)}, f32[5,512,128]{2,1,0:T(8,128)}) custom-call(s32[1]{0:T(128)S(6)} %copy.12.live, f32[5,512,128]{2,1,0:T(8,128)} %flow.1.change, f32[5,512,128]{2,1,0:T(8,128)} %bitcast.7, f32[5,512,128]{2,1,0:T(8,128)} %bitcast.6, bf16[4096,512]{1,0:T(8,128)(2,1)} %record.1, s32[8,1,512]{2,1,0:T(1,128)} %bitcast.8, ...), custom_call_target="tpu_custom_call" | custom-call | flops 4000000000 | bytes 8000000 | tf_op jit(solution)/shard_map/panels/pallas_call | solution.py:651
  39.0 52.1 %sum_spectra.1 = f32[2,256,128]{2,1,0:T(8,128)} custom-call(f32[4,2,32,8,128]{4,3,2,1,0:T(8,128)} %get-tuple-element.5.part), custom_call_target="tpu_custom_call" | custom-call | tf_op jit(solution)/shard_map/sum_spectra/pallas_call | solution.py:121
  91.0 1.7 %copy.13 = f32[2,256,128]{2,1,0:T(8,128)} copy(f32[2,256,128]{2,1,0:T(8,128)} %sum_spectra.1) | data formatting | bytes 524288

commit v8 on v7

--- a/solution.py
+++ b/solution.py
@@ -24,7 +24,7 @@
 TILES = 32
 
 
-def sum_kernel(part, out, came0, sums, came1, total, came2, mine, full, other, s0, r0, s1, r1, s2, r2, s3, r3, s4, r4):
+def sum_kernel(part, out, kept, came0, sums, came1, total, came2, mine, full, other, s0, r0, s1, r1, s2, r2, s3, r3, s4, r4, keep):
     gx, gy, gz = (lax.axis_index(a) for a in ("gx", "gy", "gz"))
     core, upper = lax.rem(gy, 2), gy // 2
     m = gx * 2 + upper
@@ -37,6 +37,12 @@
         t = lax.rem(m + r, TILES)
         return t, {"gx": t // 2, "gy": lax.rem(t, 2) * 2 + core, "gz": gz}
 
+    keeps = [
+        pltpu.make_async_copy(part.at[lax.rem(gz + k, 4), core], kept.at[k], keep.at[k])
+        for k in range(4)
+    ]
+    for copy in keeps:
+        copy.start()
     barrier = pltpu.get_barrier_semaphore()
 
     def greet(device):
@@ -65,8 +71,9 @@
         )
         shares[k].start()
     for k in (2, 1, 3, 0):
+        keeps[k].wait()
         shares[k].wait_recv()
-        sums[k] = part[lax.rem(gz + k, 4), core] + came0[k]
+        sums[k] = kept[k] + came0[k]
         if k > 0:
             along_gz[k] = remote(sums.at[k], came1.at[k - 1], s1.at[k - 1], r1.at[k - 1], along(k))
             along_gz[k].start()
@@ -98,8 +105,8 @@
 
     def lay(which, tiles):
         for h in range(2):
-            block = jnp.concatenate([tiles[2 * a + h] for a in range(16)], axis=0)
-            out[which, pl.ds(128 * h, 128), :] = jnp.transpose(block)
+            for a in range(16):
+                out[which, pl.ds(8 * a, 8), pl.ds(128 * h, 128)] = tiles[2 * a + h]
 
     lay(core, full)
     swap.wait_recv()
@@ -120,10 +127,11 @@
     dma = pltpu.SemaphoreType.DMA
     return pl.pallas_call(
         sum_kernel,
-        out_shape=jax.ShapeDtypeStruct((2, 256, FREQS), f32),
-        in_specs=[vmem],
+        out_shape=jax.ShapeDtypeStruct((2, FREQS, 256), f32),
+        in_specs=[pl.BlockSpec(memory_space=pl.ANY)],
         out_specs=vmem,
         scratch_shapes=[
+            pltpu.VMEM((4, *tiles), f32),
             pltpu.VMEM((4, *tiles), f32),
             pltpu.VMEM((4, *tiles), f32),
             pltpu.VMEM((3, *tiles), f32),
@@ -142,6 +150,7 @@
             dma,
             dma,
             dma,
+            dma((4,)),
         ],
         compiler_params=pltpu.CompilerParams(
             vmem_limit_bytes=63 * 2**20, collective_id=1, has_side_effects=True
@@ -321,19 +330,22 @@
     lax.fori_loop(0, 16, finish, 0)
 
 
-def flow_kernel(coefs, q, out, turned, diff, add, send, recv, *spaces):
+def flow_kernel(coefs, q_in, out, q, turned, diff, add, send, recv, q_sem, *spaces):
     here = {a: lax.axis_index(a) for a in ("gx", "gy", "gz")}
 
     def beside(axis, step):
         return {**here, axis: lax.rem(here[axis] + step, lax.axis_size(axis))}
 
     sides = {a: (beside(a, 1), beside(a, lax.axis_size(a) - 1)) for a in here}
+    fetch_q = pltpu.make_async_copy(q_in, q, q_sem)
+    fetch_q.start()
     barrier = pltpu.get_barrier_semaphore()
     for up, down in sides.values():
         for device in (up, down):
             pl.semaphore_signal(barrier, inc=1, device_id=device, device_id_type=MESH)
 
     planes_x, planes_y = spaces[12], spaces[6]
+    fetch_q.wait()
 
     def gather_x(j, carry):
         for c in range(5):
@@ -415,10 +427,10 @@
     return pl.pallas_call(
         functools.partial(flow_kernel, coefs),
         out_shape=jax.ShapeDtypeStruct((5, 512, 128), f32),
-        in_specs=[pl.BlockSpec(memory_space=pltpu.VMEM)],
-        scratch_shapes=[pltpu.VMEM((5, 640, 128), f32)]
+        in_specs=[pl.BlockSpec(memory_space=pl.ANY)],
+        scratch_shapes=[pltpu.VMEM((5, 512, 128), f32), pltpu.VMEM((5, 640, 128), f32)]
         + [pltpu.VMEM((5, 512, 128), f32)] * 2
-        + [pltpu.SemaphoreType.DMA((12,)), pltpu.SemaphoreType.DMA((12,))]
+        + [pltpu.SemaphoreType.DMA((12,)), pltpu.SemaphoreType.DMA((12,)), pltpu.SemaphoreType.DMA]
         + sweep_scratch(64, 8)
         + sweep_scratch(32, 16)
         + sweep_scratch(16, 32),
@@ -566,11 +578,6 @@
 
     lax.fori_loop(0, groups, front, 0)
 
-    for copy in rest_in:
-        copy.wait()
-    for c in range(1, 5):
-        finish(c)
-    rest_out.start()
     order = (place + 1).astype(jnp.float32)
 
     def features(b, alive):
@@ -641,6 +648,11 @@
         return carry
 
     lax.fori_loop(0, (live[0] + PAIR - 1) // PAIR, back, 0)
+    for copy in rest_in:
+        copy.wait()
+    for c in range(1, 5):
+        finish(c)
+    rest_out.start()
     density_out.wait()
     rest_out.wait()
 
@@ -700,7 +712,7 @@
         listener_range.reshape(1, -1),
         dft_table(panel_record.shape[1], FREQS),
     )
-    return updated.reshape(state_section.shape), summed_spectra(part)
+    return updated.reshape(state_section.shape), jnp.transpose(summed_spectra(part), (0, 2, 1))
 
 
 def solution(mesh):

time: 92.8 us -> 91.8 us (0.989)
  Pallas kernels: 89.7 us -> 88.6 us
    pallas_call x1, Pallas kernels: 32 us -> 30.7 us  [flow_change(): pl.pallas_call(functools.partial(flow_kernel, coefs), out_shape=jax.Shape...]
where the time goes in v8:
time: 91.8 us; the launch traced here: 91.7 us
  Pallas kernels  88.6 us (97%)
  local copies, waits for them, and re-layouts  1.79 us (2%)
  between operations  1.3 us (1%)
    pallas_call x1, Pallas kernels, summed_spectra(): pl.pallas_call(sum_kernel, out_shape=jax.ShapeDtypeStruct((2, FREQS, 256)...  51.3 us
    pallas_call x1, Pallas kernels, flow_change(): pl.pallas_call(functools.partial(flow_kernel, coefs), out_shape=jax.Shape...  30.7 us
    pallas_call x1, Pallas kernels, panel_sums(): pl.pallas_call(functools.partial(panel_kernel, counts), out_shape=(jax.Sh...  6.49 us

profile of v8, /device:TPU:1, one launch (start us, length us, event | category | flops | bytes accessed | tf_op | source)
XLA Modules:
  0.0 91.7 jit_solution(51663605663276732)
XLA Ops:
  1.3 30.7 %flow.1.change = f32[5,512,128]{2,1,0:T(8,128)} custom-call(f32[5,512,128]{2,1,0:T(8,128)} %bitcast.6), custom_call_target="tpu_custom_call" | custom-call | flops 100000000 | bytes 6000000 | tf_op jit(solution)/shard_map/flow/pallas_call | solution.py:427
  32.0 6.5 %panels.1 = (f32[4,2,32,8,128]{4,3,2,1,0:T(8,128)}, f32[5,512,128]{2,1,0:T(8,128)}) custom-call(s32[1]{0:T(128)S(6)} %copy.12.live, f32[5,512,128]{2,1,0:T(8,128)} %flow.1.change, f32[5,512,128]{2,1,0:T(8,128)} %bitcast.9, f32[5,512,128]{2,1,0:T(8,128)} %bitcast.7, bf16[4096,512]{1,0:T(8,128)(2,1)} %record.1, s32[8,1,512]{2,1,0:T(1,128)} %bitcast.10, ...), custom_call_target="tpu_custom_call" | custom-call | flops 4000000000 | bytes 8000000 | tf_op jit(solution)/shard_map/panels/pallas_call | solution.py:663
  38.5 51.3 %sum_spectra.1 = f32[2,128,256]{2,1,0:T(8,128)} custom-call(f32[4,2,32,8,128]{4,3,2,1,0:T(8,128)} %get-tuple-element.5.part), custom_call_target="tpu_custom_call" | custom-call | tf_op jit(solution)/shard_map/sum_spectra/pallas_call | solution.py:128
  89.9 1.8 %copy.11 = f32[2,256,128]{2,1,0:T(8,128)} copy(f32[2,256,128]{1,2,0:T(8,128)} %bitcast.8) | data formatting | bytes 524288
